TPU v7x, 128 devices: a whole 4x4x4 slice. The times are simulated.
128 devices in a mesh: rows: 16 (over z, x_lo, core), aux: 8 (over x_hi, y).
Axes of the slice: x: 4 (x_hi: 2, x_lo: 2; x = x_hi * 2 + x_lo), y: 4, z: 4, core: 2. Of those that a mesh axis runs over, the one named last changes fastest.
Arguments:
- pair_coeffs: float32 [36000, 16384], P('aux', 'rows'), may hold values from -0.046875 to 0.046875
- pair_gaps: float32 [16384], P('rows'), may hold values from 0.2 to 20
- trial_vectors: float32 [36000, 128], P('aux'), may hold values from -0.03125 to 0.03125
Outputs:
- vectors_out: float32 [36000, 128], P('aux')
- rayleigh: float32 [128, 128], replicated
All inputs are finite; a program needn't handle non-finite values.
Results may differ from a plain program's by a relative error of at most 0.00011.
Values sent between devices are 32-bit elements; how exact they have to be, the bound alone decides.
No kernel may reach another device: no remote copies, remote signals or barrier semaphores. Data moves between devices by JAX's collectives and lax.ppermute only.
A program may use at most 128 MiB of HBM per device.

v0:
```python
import jax
import jax.numpy as jnp
from jax import lax
from jax.experimental import pallas as pl
from jax.experimental.pallas import tpu as pltpu
from jax.sharding import Mesh, PartitionSpec as P


F32 = jnp.float32
BF16 = jnp.bfloat16
HIGHEST = lax.Precision.HIGHEST

NAUX_L = 4500
PAIRS_L = 1024
K = 128
CHUNK = 768
CHUNKS = 6
ROWS = CHUNK * CHUNKS
HALF = ROWS // 2
TAIL = NAUX_L - CHUNK * (CHUNKS - 1)
CHIPS = 8
PIECE = HALF // CHIPS
PAIRS_J = PAIRS_L // CHIPS
GRAM_J = K // CHIPS


def split(x):
    hi = x.astype(BF16)
    return hi, (x - hi.astype(F32)).astype(BF16)


def dot(a, b, ca, cb, precision=None):
    return lax.dot_general(
        a, b, (((ca,), (cb,)), ((), ())), precision=precision, preferred_element_type=F32
    )


VMEM_SPEC = pl.BlockSpec(memory_space=pltpu.VMEM)


def cost(us):
    return pl.CostEstimate(flops=int(us * 1.5e8), bytes_accessed=0, transcendentals=0)


def core_of(dev):
    return (dev[0] >> 3) & 1


def near_of(dev):
    return ((dev[0] >> 4) & 1) * 4 + (dev[0] >> 5)


def aux_of(dev):
    return dev[0] & 7


def kernel_call(body, outs, smem, hbm, vmem, scratch=(), limit=12 << 20, us=0.3):
    return pl.pallas_call(
        body,
        out_shape=[pltpu.VMEM(s, d) for s, d in outs],
        in_specs=[pl.BlockSpec(memory_space=pltpu.SMEM)] * len(smem)
        + [pl.BlockSpec(memory_space=pl.ANY)] * len(hbm)
        + [VMEM_SPEC] * len(vmem),
        out_specs=[VMEM_SPEC] * len(outs),
        scratch_shapes=list(scratch),
        compiler_params=pltpu.CompilerParams(vmem_limit_bytes=limit),
        cost_estimate=cost(us),
    )(*smem, *hbm, *[pltpu.with_memory_space_constraint(v, pltpu.VMEM) for v in vmem])


def transposed_halves(v):
    hi, lo = split(v.T)
    return jnp.concatenate([hi, lo], axis=0)


def fold(x):
    return x[0:K, :] + x[K : 2 * K, :]


def first_projection(coeffs, vectors):
    def body(b_hbm, v_hbm, bhi, blo, out, bbuf, vbuf, btail, vtail, sems):
        def copies(i):
            last = i == CHUNKS - 1
            rows = pl.ds(i * CHUNK, TAIL if last else CHUNK)
            return (
                pltpu.make_async_copy(b_hbm.at[rows], btail if last else bbuf.at[i], sems.at[0, i]),
                pltpu.make_async_copy(v_hbm.at[rows], vtail if last else vbuf.at[i], sems.at[1, i]),
            )

        for i in range(CHUNKS):
            for c in copies(i):
                c.start()
        for i in range(CHUNKS):
            for c in copies(i):
                c.wait()
            slot = i
            if i == CHUNKS - 1:
                slot = 0
                bbuf[0, TAIL // 8 * 8 :, :] = jnp.zeros((CHUNK - TAIL // 8 * 8, PAIRS_L), F32)
                vbuf[0, TAIL // 8 * 8 :, :] = jnp.zeros((CHUNK - TAIL // 8 * 8, K), F32)
                bbuf[0, 0:TAIL, :] = btail[...]
                vbuf[0, 0:TAIL, :] = vtail[...]
            vt = transposed_halves(vbuf[slot])
            for n in range(4):
                hi, lo = split(bbuf[slot, :, 256 * n : 256 * n + 256])
                bhi[n, CHUNK * i : CHUNK * (i + 1), :] = hi
                blo[n, CHUNK * i : CHUNK * (i + 1), :] = lo
                part = fold(dot(vt, hi, 1, 0) + dot(vt, lo, 1, 0))
                for t in range(2):
                    value = part[:, 128 * t : 128 * t + 128]
                    out[2 * n + t] = value if i == 0 else out[2 * n + t] + value

    halves = ((4, ROWS, 256), BF16)
    coeffs = pltpu.with_memory_space_constraint(coeffs, pltpu.HBM)
    vectors = pltpu.with_memory_space_constraint(vectors, pltpu.HBM)
    return kernel_call(
        body,
        [halves, halves, ((CHIPS, K, PAIRS_J), F32)],
        [],
        [coeffs, vectors],
        [],
        scratch=[
            pltpu.VMEM((CHUNKS - 1, CHUNK, PAIRS_L), F32),
            pltpu.VMEM((CHUNKS - 1, CHUNK, K), F32),
            pltpu.VMEM((TAIL, PAIRS_L), F32),
            pltpu.VMEM((TAIL, K), F32),
            pltpu.SemaphoreType.DMA((2, CHUNKS)),
        ],
        limit=26 << 20,
        us=8.0,
    )


def project_half(dev, bhi, blo, v, so_far, gram_rows=GRAM_J):
    def body(dev, bhi, blo, v, *rest):
        if so_far is None:
            acc, gacc = rest
            half = core_of(dev)
        else:
            acc0, gacc0, out, acc, gacc = rest
            half = 1 - core_of(dev)
        for i in range(3):
            row0 = pl.multiple_of(half * HALF + i * CHUNK, CHUNK)
            vt = transposed_halves(v[CHUNK * i : CHUNK * (i + 1), :])
            for n in range(4):
                part = fold(
                    dot(vt, bhi[n, pl.ds(row0, CHUNK), :], 1, 0)
                    + dot(vt, blo[n, pl.ds(row0, CHUNK), :], 1, 0)
                )
                for t in range(2):
                    value = part[:, 128 * t : 128 * t + 128]
                    j = 2 * n + t
                    if i > 0:
                        value = acc[j] + value
                    if so_far is not None and i == 2:
                        out[j, 0:K, :] = acc0[j] + value
                    else:
                        acc[j] = value
            g = dot(vt, vt, 1, 1)
            gacc[...] = g if i == 0 else gacc[...] + g
        if so_far is not None:
            g = gacc[...] + gacc0[...]
            gram = (g[0:K, 0:K] + g[K:, K:]) + (g[0:K, K:] + g[K:, 0:K])
            for j in range(CHIPS):
                first = GRAM_J * j if gram_rows < K else 0
                out[j, K:, :] = gram[first : first + gram_rows, :]

    acc = ((CHIPS, K, PAIRS_J), F32)
    gacc = ((2 * K, 2 * K), F32)
    if so_far is None:
        return kernel_call(body, [acc, gacc], [dev], [], [bhi, blo, v], us=3.0)
    return kernel_call(
        body,
        [((CHIPS, K + gram_rows, PAIRS_J), F32)],
        [dev],
        [],
        [bhi, blo, v, *so_far],
        scratch=[pltpu.VMEM(*acc), pltpu.VMEM(*gacc)],
        us=3.0,
    )


def sum_aux(dev, parts, gaps, copies):
    rows = parts.shape[1]

    def body(dev, p, gaps, *outs):
        gap = gaps[pl.ds(aux_of(dev), 1), :]
        s = ((p[0] + p[1]) + (p[2] + p[3])) + ((p[4] + p[5]) + (p[6] + p[7]))
        piece = s[0:K] * (4.0 * gap / (gap * gap + 1.0))
        if copies:
            for j in range(CHIPS):
                outs[0][j, 0:K, :] = piece
                if rows > K:
                    outs[0][j, K:, :] = s[K:]
        else:
            outs[0][...] = dot(piece, s[0:K], 1, 1, HIGHEST)
            outs[1][...] = s[K:]

    if copies:
        outs = [((CHIPS, rows, PAIRS_J), F32)]
    else:
        outs = [((K, K), F32), ((K, K), F32)]
    return kernel_call(body, outs, [dev], [], [parts, gaps])


NEAR_MASK = {("z", 1): 1, ("z", 3): 3, ("xl", 1): 4}
CROSS = ((("z", 1), ("z", 3), ("xl", 1)), (("xl", 1), ("z", 1), ("z", 3)))


def piece_at(core, near, p):
    masks = [0, 0]
    for c in range(2):
        for t in range(3):
            if (p >> (2 - t)) & 1:
                masks[c] ^= NEAR_MASK[CROSS[c][t]]
    return near ^ jnp.where(core == 0, masks[0], masks[1])


def apply_pieces(dev, bhi, blo, scaled, other, make_rhs, first):
    def body(dev, bhi, blo, s, out, *rest):
        if make_rhs:
            st = rest[0]
            for j in range(CHIPS):
                hi, lo = split(s[j, 0:K, :])
                lanes = slice(128 * (j % 2), 128 * (j % 2) + 128)
                st[j // 2, 0:K, lanes] = hi
                st[j // 2, K : 2 * K, lanes] = lo
        else:
            st = s
        core = core_of(dev)
        if other:
            core = 1 - core

        for i in range(4):
            start = core * HALF + piece_at(core, near_of(dev), first + i) * PIECE
            start = pl.multiple_of(start, PIECE)
            res = None
            for ref in (bhi, blo):
                for n in range(4):
                    d = dot(ref[n, pl.ds(start, PIECE), :], st[n], 1, 1)
                    res = d if res is None else res + d
            out[i] = res[:, 0:K] + res[:, K : 2 * K]

    outs = [((4, PIECE, K), F32)]
    if make_rhs:
        outs.append(((4, 2 * K, 256), BF16))
    return kernel_call(body, outs, [dev], [], [bhi, blo, scaled], us=1.4)


def add_slots(first, count, *parts):
    def body(*refs):
        total = refs[0][first : first + count]
        for r in refs[1:-1]:
            total = total + r[first : first + count]
        refs[-1][...] = total

    return kernel_call(body, [((count, PIECE, K), F32)], [], [], list(parts))[0]


def sum_rows(parts, inverse):
    def body(*refs):
        out = refs[-1]
        own, got, r1, r2, r3 = refs[:5]
        s = (own[0] + got[0]) + r1[0] + (r2[0] + r3[0])
        if inverse is not None:
            s = dot(s, refs[len(parts)][...], 1, 1, HIGHEST)
        for j in range(CHIPS):
            out[j] = s

    extra = [] if inverse is None else [inverse]
    return kernel_call(body, [((CHIPS, PIECE, K), F32)], [], [], [*parts, *extra])[0]


def pivots(gs, ws, begin, end):
    lane = lax.broadcasted_iota(jnp.int32, (K, K), 1)
    sub = lax.broadcasted_iota(jnp.int32, (K, K), 0)

    def step(h, low):
        k = 4 * h
        lanes, rows = lane[low:], sub[low:, 0:1]
        g, w_all = gs[low:, :], ws[low:, :]

        def pick(x, at):
            return jnp.sum(jnp.where(lanes[0 : x.shape[0]] == at, x, 0.0), axis=1, keepdims=True)

        r = [gs[pl.ds(k + i, 1), :] for i in range(4)]
        w = [ws[pl.ds(k + i, 1), :] for i in range(4)]
        c = [pick(g, k + i) for i in range(4)]
        d = [[pick(r[i], k + t) for t in range(4)] for i in range(4)]
        for i in range(4):
            inv = 1.0 / d[i][i]
            f = jnp.where(rows > k + i, c[i] * inv, 0.0)
            for t in range(i + 1, 4):
                c[t] = c[t] - f * d[i][t]
                m = d[t][i] * inv
                r[t] = r[t] - m * r[i]
                w[t] = w[t] - m * w[i]
                for u in range(i + 1, 4):
                    d[t][u] = d[t][u] - m * d[i][u]
            g = g - f * r[i]
            w_all = w_all - f * w[i]
        gs[low:, :] = g
        ws[low:, :] = w_all

    for low, top in ((0, 64), (64, K)):
        one, last = max(begin, low), min(end, top)
        if one < last:
            lax.fori_loop(one // 4, last // 4, lambda h, c, low=low: (step(h, low), c)[1], 0)


def scaled_rows(gs, ws):
    lane = lax.broadcasted_iota(jnp.int32, (K, K), 1)
    sub = lax.broadcasted_iota(jnp.int32, (K, K), 0)
    d = jnp.sum(jnp.where(lane == sub, gs[...], 0.0), axis=1, keepdims=True)
    return ws[...] / jnp.sqrt(d)


def eliminate(state, begin, end):
    start, stop = begin == 0, end == K

    def body(*refs):
        gs, ws = refs[-2:]
        if start:
            g_ref = refs[0]
            if len(g_ref.shape) == 2:
                gs[...] = g_ref[...]
            else:
                row0 = g_ref.shape[1] - GRAM_J
                for j in range(CHIPS):
                    gs[GRAM_J * j : GRAM_J * (j + 1), :] = g_ref[j, row0:, :]
            lane = lax.broadcasted_iota(jnp.int32, (K, K), 1)
            sub = lax.broadcasted_iota(jnp.int32, (K, K), 0)
            ws[...] = jnp.where(lane == sub, 1.0, 0.0).astype(F32)
        else:
            gs[...] = refs[0][...]
            ws[...] = refs[1][...]
        pivots(gs, ws, begin, end)
        if stop:
            refs[-3][...] = scaled_rows(gs, ws)

    square = ((K, K), F32)
    if stop:
        outs, scratch = [square], [pltpu.VMEM(*square), pltpu.VMEM(*square)]
    else:
        outs, scratch = [square, square], []
    return kernel_call(body, outs, [], [], list(state), scratch=scratch, us=(end - begin) / 20)


def in_between(value, state, cuts):
    state = eliminate(state, cuts[0], cuts[1])
    value, *state = lax.optimization_barrier((value, *state))
    return value, state


def finish(dev, mine, theirs, state, begin):
    def body(dev, mine, theirs, g, w, out, inv, gs, ws, both, buf, tail, sem):
        gs[...] = g[...]
        ws[...] = w[...]
        pivots(gs, ws, begin, K)
        inv[...] = scaled_rows(gs, ws)
        both[core_of(dev)] = mine[...]
        both[1 - core_of(dev)] = theirs[...]
        ihi, ilo = split(inv[...])
        rhs = jnp.concatenate([ihi, ilo], axis=0)

        def copy(i):
            last = i == CHUNKS - 1
            rows = pl.ds(i * CHUNK, TAIL if last else CHUNK)
            return pltpu.make_async_copy(tail if last else buf.at[i], out.at[rows], sem.at[i])

        for i in range(CHUNKS):
            start = CHUNK * (i % 3)
            vhi, vlo = split(both[i // 3, start : start + CHUNK, :])
            r = dot(vhi, rhs, 1, 1) + dot(vlo, rhs, 1, 1)
            r = r[:, 0:K] + r[:, K : 2 * K]
            if i == CHUNKS - 1:
                tail[...] = r[0:TAIL]
            else:
                buf[i] = r
            copy(i).start()
        for i in range(CHUNKS):
            copy(i).wait()

    square = pltpu.VMEM((K, K), F32)
    return pl.pallas_call(
        body,
        out_shape=[jax.ShapeDtypeStruct((NAUX_L, K), F32), square],
        in_specs=[pl.BlockSpec(memory_space=pltpu.SMEM)] + [VMEM_SPEC] * 4,
        out_specs=[pl.BlockSpec(memory_space=pl.ANY), VMEM_SPEC],
        scratch_shapes=[
            square,
            square,
            pltpu.VMEM((2, HALF, K), F32),
            pltpu.VMEM((CHUNKS - 1, CHUNK, K), F32),
            pltpu.VMEM((TAIL, K), F32),
            pltpu.SemaphoreType.DMA((CHUNKS,)),
        ],
        compiler_params=pltpu.CompilerParams(vmem_limit_bytes=16 << 20),
        cost_estimate=cost(4.2),
        name="finish",
    )(dev, *[pltpu.with_memory_space_constraint(v, pltpu.VMEM) for v in (mine, theirs, *state)])


def rayleigh_matrix(inverse, parts):
    def body(inv, a, b, c, d, out):
        total = (a[...] + b[...]) + (c[...] + d[...])
        out[...] = dot(dot(inv[...], total, 1, 0, HIGHEST), inv[...], 1, 1, HIGHEST)

    return kernel_call(body, [((K, K), F32)], [], [], [inverse, *parts])[0]


def exchange(value, axis, mask):
    n = lax.axis_size(axis)
    return lax.ppermute(value, axis, [(i, i ^ mask) for i in range(n)])


def to_each(value, axes):
    return lax.all_to_all(value, axes, split_axis=0, concat_axis=0, tiled=True)


NEAR = ("xl", "z")
AUX = ("xh", "y")


def cross(value, step):
    nz, nx = lax.axis_size("z"), lax.axis_size("xl")
    pairs = []
    for z in range(nz):
        for x in range(nx):
            for c in range(2):
                axis, mask = CROSS[c][step]
                to = (z ^ mask, x) if axis == "z" else (z, x ^ mask)
                pairs.append(((z * nx + x) * 2 + c, (to[0] * nx + to[1]) * 2 + c))
    return lax.ppermute(value, ("z", "xl", "c"), pairs)


def reduce_rows(dev, bhi, blo, scaled, eliminating):
    send, rhs = apply_pieces(dev, bhi, blo, scaled, True, True, 4)
    got = exchange(send, "c", 1)
    (own,) = apply_pieces(dev, bhi, blo, rhs, False, False, 4)
    first = add_slots(0, 4, own, got)
    r1 = cross(first, 0)
    first, rhs = lax.optimization_barrier((first, rhs))
    (send,) = apply_pieces(dev, bhi, blo, rhs, True, False, 0)
    got = exchange(send, "c", 1)
    (own,) = apply_pieces(dev, bhi, blo, rhs, False, False, 0)
    r1, own, got = lax.optimization_barrier((r1, own, got))
    inverse = None
    if eliminating:
        r1, state = in_between(r1, [scaled], (0, 40))
    r2 = cross(add_slots(2, 2, own, got, r1), 1)
    if eliminating:
        r2, state = in_between(r2, state, (40, 80))
    r3 = cross(add_slots(1, 1, own, got, r1, r2), 2)
    if eliminating:
        r3, (inverse,) = in_between(r3, state, (80, 128))
    return sum_rows([own, got, r1, r2, r3], inverse)


def shards(pair_coeffs, pair_gaps, trial_vectors):
    dev = lax.axis_index(("z", "xl", "c") + AUX).astype(jnp.int32)[None]
    gaps = pair_gaps.reshape(CHIPS, PAIRS_J)
    dev, gaps, trial_vectors = lax.optimization_barrier((dev, gaps, trial_vectors))
    bhi, blo, parts = first_projection(pair_coeffs, trial_vectors)
    for step in range(2):
        (copies,) = sum_aux(dev, to_each(parts, AUX), gaps, True)
        scaled = to_each(copies, AUX)
        near = reduce_rows(dev, bhi, blo, scaled, step == 1)
        mine = to_each(near, NEAR).reshape(HALF, K)
        theirs = exchange(mine, "c", 1)
        so_far = project_half(dev, bhi, blo, mine, None)
        (parts,) = project_half(dev, bhi, blo, theirs, so_far, K if step == 1 else GRAM_J)
    total, gram = sum_aux(dev, to_each(parts, AUX), gaps, False)
    total = total + exchange(total, "c", 1)
    state = [gram]
    for axis, cut in (("z", (0, 40)), ("y", (40, 84)), (("xl", "xh"), None)):
        got = []
        for mask in (1, 2, 3):
            got.append(exchange(total, axis, mask))
        if cut:
            got, state = in_between(got, state, cut)
            total = (total + got[0]) + (got[1] + got[2])
    vectors_out, inverse = finish(dev, mine, theirs, state, 84)
    rayleigh = rayleigh_matrix(inverse, [total, *got])
    return vectors_out, rayleigh


def solution(mesh):
    cube = Mesh(mesh.devices.reshape(4, 2, 2, 2, 4), ("z", "xl", "c", "xh", "y"))

    return jax.shard_map(
        shards,
        mesh=cube,
        in_specs=(P(AUX, ("z", "xl", "c")), P(("z", "xl", "c")), P(AUX, None)),
        out_specs=(P(AUX, None), P()),
        check_vma=False,
    )
```

profile of v0, /device:TPU:1, one launch (start us, length us, event | category | flops | bytes accessed | tf_op | source)
XLA Modules:
  0.0 223.2 jit_solution(14114267681254662181)
XLA Ops:
  0.7 8.4 %shard_map.50 = (bf16[4,4608,256]{2,1,0:T(8,128)(2,1)S(1)}, bf16[4,4608,256]{2,1,0:T(8,128)(2,1)S(1)}, f32[8,128,128]{2,1,0:T(8,128)S(1)}) custom-call(f32[4500,1024]{1,0:T(8,128)} %b_hbm.1, f32[4500,128]{1,0:T(8,128)} %v_hbm), custom_call_target="tpu_custom_call" | custom-call | flops 1200000000 | tf_op jit(solution)/shard_map/pallas_call | solution.py:58
  9.0 17.3 %all_to_all.35.p = f32[8,128,128]{2,1,0:T(8,128)S(1)} all-to-all(f32[8,128,128]{2,1,0:T(8,128)S(1)} %get-tuple-element.58), channel_id=1, replica_groups=mesh['z'=4,'xl'=2,'c'=2,'xh'=2,'y'=4] {'xh','y'}, dimensions={0} | all-to-all | bytes 1048576 | tf_op jit(solution)/shard_map/all_to_all | solution.py:418
  26.4 12.1 %all_to_all.36.s = f32[8,128,128]{2,1,0:T(8,128)S(1)} all-to-all(f32[8,128,128]{2,1,0:T(8,128)S(1)} %shard_map.51), channel_id=1, replica_groups=mesh['z'=4,'xl'=2,'c'=2,'xh'=2,'y'=4] {'xh','y'}, dimensions={0} | all-to-all | bytes 1048576 | tf_op jit(solution)/shard_map/all_to_all | solution.py:418
  38.4 1.4 shard_map.52
  39.9 3.5 %collective-permute-start = (f32[4,288,128]{2,1,0:T(8,128)S(1)}, f32[4,288,128]{2,1,0:T(8,128)S(1)}, u32[]{:S(2)}, u32[]{:S(2)}) collective-permute-start(f32[4,288,128]{2,1,0:T(8,128)S(1)} %get-tuple-element.61), channel_id=1, source_target_pairs={{0,8},{8,0},{1,9},{9,1},{2,10},{10,2},{3,11},{11,3},{4,12},{12,4},... | collective-permute-start | bytes 1769480 | tf_op jit(solution)/shard_map/ppermute | solution.py:414
  43.4 1.4 shard_map.53.refs_0_
  45.1 1.4 shard_map.56
  47.3 1.4 shard_map.55.refs_0_
  48.7 7.3 %collective-permute-done.1.refs_2_ = f32[4,288,128]{2,1,0:T(8,128)S(1)} collective-permute-done((f32[4,288,128]{2,1,0:T(8,128)S(1)}, f32[4,288,128]{2,1,0:T(8,128)S(1)}, u32[]{:S(2)}, u32[]{:S(2)}) %collective-permute-start.1) | collective-permute-done | bytes 589856 | tf_op jit(solution)/shard_map/ppermute | solution.py:434
  56.0 1.7 collective-permute-start.3
  57.7 4.1 %collective-permute-done.3.refs_3_ = f32[2,288,128]{2,1,0:T(8,128)S(1)} collective-permute-done((f32[2,288,128]{2,1,0:T(8,128)S(1)}, f32[2,288,128]{2,1,0:T(8,128)S(1)}, u32[]{:S(2)}, u32[]{:S(2)}) %collective-permute-start.3) | collective-permute-done | bytes 294944 | tf_op jit(solution)/shard_map/ppermute | solution.py:434
  61.9 4.0 %collective-permute-start.4 = (f32[1,288,128]{2,1,0:T(8,128)S(1)}, f32[1,288,128]{2,1,0:T(8,128)S(1)}, u32[]{:S(2)}, u32[]{:S(2)}) collective-permute-start(f32[1,288,128]{2,1,0:T(8,128)S(1)} %shard_map.58), channel_id=1, source_target_pairs={{0,16},{8,104},{16,0},{24,120},{32,48},{40,72},{48,32},{56,88},{64... | collective-permute-start | bytes 442376 | tf_op jit(solution)/shard_map/ppermute | solution.py:434
  65.9 2.5 %collective-permute-done.4.refs_4_ = f32[1,288,128]{2,1,0:T(8,128)S(1)} collective-permute-done((f32[1,288,128]{2,1,0:T(8,128)S(1)}, f32[1,288,128]{2,1,0:T(8,128)S(1)}, u32[]{:S(2)}, u32[]{:S(2)}) %collective-permute-start.4) | collective-permute-done | bytes 147488 | tf_op jit(solution)/shard_map/ppermute | solution.py:434
  68.5 17.4 %all_to_all.37 = f32[8,288,128]{2,1,0:T(8,128)S(1)} all-to-all(f32[8,288,128]{2,1,0:T(8,128)S(1)} %shard_map.59), channel_id=1, replica_groups=mesh['z'=4,'xl'=2,'c'=2,'xh'=2,'y'=4] {'xl','z'}, dimensions={0} | all-to-all | bytes 2359296 | tf_op jit(solution)/shard_map/all_to_all | solution.py:418
  85.8 4.5 %collective-permute-start.5 = (f32[2304,128]{1,0:T(8,128)S(1)}, f32[2304,128]{1,0:T(8,128)S(1)}, u32[]{:S(2)}, u32[]{:S(2)}) collective-permute-start(f32[2304,128]{1,0:T(8,128)S(1)} %bitcast.7), channel_id=1, source_target_pairs={{0,8},{8,0},{1,9},{9,1},{2,10},{10,2},{3,11},{11,3},{4,12},{12,4},... | collective-permute-start | bytes 3538952 | tf_op jit(solution)/shard_map/ppermute | solution.py:414
  90.3 3.0 %shard_map.60 = (f32[8,128,128]{2,1,0:T(8,128)S(1)}, f32[256,256]{1,0:T(8,128)S(1)}) custom-call(s32[1]{0:T(128)} %bitcast.dev, bf16[4,4608,256]{2,1,0:T(8,128)(2,1)S(1)} %get-tuple-element.56.bhi, bf16[4,4608,256]{2,1,0:T(8,128)(2,1)S(1)} %get-tuple-element.57.blo, f32[2304,128]{1,0:T(8,128)S(1)} %bitcast.8), custom_call_target="tpu_custom_call" | custom-call | flops 450000000 | tf_op jit(solution)/shard_map/pallas_call | solution.py:58
  93.4 3.0 %shard_map.61 = f32[8,144,128]{2,1,0:T(8,128)S(1)} custom-call(s32[1]{0:T(128)} %bitcast.dev, bf16[4,4608,256]{2,1,0:T(8,128)(2,1)S(1)} %get-tuple-element.56.bhi, bf16[4,4608,256]{2,1,0:T(8,128)(2,1)S(1)} %get-tuple-element.57.blo, f32[2304,128]{1,0:T(8,128)S(1)} %collective-permute-done.5.v, f32[8,128,128]{2,1,0:T(8,128)S(1)} %get-tuple-element.66.rest_0_, ...), custom_call_target="tpu_custom_call" | custom-call | flops 450000000 | tf_op jit(solution)/shard_map/pallas_call | solution.py:58
  96.4 14.8 %all_to_all.38.p = f32[8,144,128]{2,1,0:T(8,128)S(1)} all-to-all(f32[8,144,128]{2,1,0:T(8,128)S(1)} %shard_map.61), channel_id=1, replica_groups=mesh['z'=4,'xl'=2,'c'=2,'xh'=2,'y'=4] {'xh','y'}, dimensions={0} | all-to-all | bytes 1179648 | tf_op jit(solution)/shard_map/all_to_all | solution.py:418
  111.3 14.7 %all_to_all.39.s.refs_0_ = f32[8,144,128]{2,1,0:T(8,128)S(1)} all-to-all(f32[8,144,128]{2,1,0:T(8,128)S(1)} %shard_map.62), channel_id=1, replica_groups=mesh['z'=4,'xl'=2,'c'=2,'xh'=2,'y'=4] {'xh','y'}, dimensions={0} | all-to-all | bytes 1179648 | tf_op jit(solution)/shard_map/all_to_all | solution.py:418
  125.9 1.4 shard_map.63
  127.4 1.9 collective-permute-start.6
  129.2 1.4 shard_map.64.refs_0_
  131.0 1.4 shard_map.67
  132.8 2.0 shard_map.68
  134.8 1.4 shard_map.66.refs_0_
  136.3 5.6 %collective-permute-done.7.refs_2_ = f32[4,288,128]{2,1,0:T(8,128)S(1)} collective-permute-done((f32[4,288,128]{2,1,0:T(8,128)S(1)}, f32[4,288,128]{2,1,0:T(8,128)S(1)}, u32[]{:S(2)}, u32[]{:S(2)}) %collective-permute-start.7) | collective-permute-done | bytes 589856 | tf_op jit(solution)/shard_map/ppermute | solution.py:434
  142.2 1.8 shard_map.70
  144.0 3.9 %collective-permute-done.9.refs_3_ = f32[2,288,128]{2,1,0:T(8,128)S(1)} collective-permute-done((f32[2,288,128]{2,1,0:T(8,128)S(1)}, f32[2,288,128]{2,1,0:T(8,128)S(1)}, u32[]{:S(2)}, u32[]{:S(2)}) %collective-permute-start.9) | collective-permute-done | bytes 294944 | tf_op jit(solution)/shard_map/ppermute | solution.py:434
  147.9 0.9 collective-permute-start.10
  148.8 1.9 shard_map.72.refs_5_
  150.7 2.5 %collective-permute-done.10.refs_4_ = f32[1,288,128]{2,1,0:T(8,128)S(1)} collective-permute-done((f32[1,288,128]{2,1,0:T(8,128)S(1)}, f32[1,288,128]{2,1,0:T(8,128)S(1)}, u32[]{:S(2)}, u32[]{:S(2)}) %collective-permute-start.10) | collective-permute-done | bytes 147488 | tf_op jit(solution)/shard_map/ppermute | solution.py:434
  153.5 16.0 %all_to_all.40 = f32[8,288,128]{2,1,0:T(8,128)S(1)} all-to-all(f32[8,288,128]{2,1,0:T(8,128)S(1)} %shard_map.73), channel_id=1, replica_groups=mesh['z'=4,'xl'=2,'c'=2,'xh'=2,'y'=4] {'xl','z'}, dimensions={0} | all-to-all | bytes 2359296 | tf_op jit(solution)/shard_map/all_to_all | solution.py:418
  169.5 4.5 %collective-permute-start.11 = (f32[2304,128]{1,0:T(8,128)S(1)}, f32[2304,128]{1,0:T(8,128)S(1)}, u32[]{:S(2)}, u32[]{:S(2)}) collective-permute-start(f32[2304,128]{1,0:T(8,128)S(1)} %bitcast.4), channel_id=1, source_target_pairs={{0,8},{8,0},{1,9},{9,1},{2,10},{10,2},{3,11},{11,3},{4,12},{12,4},... | collective-permute-start | bytes 3538952 | tf_op jit(solution)/shard_map/ppermute | solution.py:414
  174.0 3.0 %shard_map.74 = (f32[8,128,128]{2,1,0:T(8,128)S(1)}, f32[256,256]{1,0:T(8,128)S(1)}) custom-call(s32[1]{0:T(128)} %bitcast.dev, bf16[4,4608,256]{2,1,0:T(8,128)(2,1)S(1)} %get-tuple-element.56.bhi, bf16[4,4608,256]{2,1,0:T(8,128)(2,1)S(1)} %get-tuple-element.57.blo, f32[2304,128]{1,0:T(8,128)S(1)} %bitcast.5), custom_call_target="tpu_custom_call" | custom-call | flops 450000000 | tf_op jit(solution)/shard_map/pallas_call | solution.py:58
  177.0 3.0 %shard_map.75 = f32[8,256,128]{2,1,0:T(8,128)S(1)} custom-call(s32[1]{0:T(128)} %bitcast.dev, bf16[4,4608,256]{2,1,0:T(8,128)(2,1)S(1)} %get-tuple-element.56.bhi, bf16[4,4608,256]{2,1,0:T(8,128)(2,1)S(1)} %get-tuple-element.57.blo, f32[2304,128]{1,0:T(8,128)S(1)} %collective-permute-done.11.v.theirs, f32[8,128,128]{2,1,0:T(8,128)S(1)} %get-tuple-element.86.rest_0_, ...), custom_call_target="tpu_custom_call" | custom-call | flops 450000000 | tf_op jit(solution)/shard_map/pallas_call | solution.py:58
  180.0 19.0 %all_to_all.41.p = f32[8,256,128]{2,1,0:T(8,128)S(1)} all-to-all(f32[8,256,128]{2,1,0:T(8,128)S(1)} %shard_map.75), channel_id=1, replica_groups=mesh['z'=4,'xl'=2,'c'=2,'xh'=2,'y'=4] {'xh','y'}, dimensions={0} | all-to-all | bytes 2097152 | tf_op jit(solution)/shard_map/all_to_all | solution.py:418
  199.3 1.3 collective-permute-start.12
  200.6 0.9 collective-permute-done.12
  201.6 0.9 collective-permute-start.15
  202.5 1.2 collective-permute-start.14
  203.6 1.2 collective-permute-start.13
  204.9 2.0 shard_map.77
  207.9 0.7 collective-permute-start.18
  208.6 1.1 collective-permute-start.17
  209.7 1.5 collective-permute-start.16
  211.2 1.9 shard_map.78
  214.2 3.6 %collective-permute-start.19 = (f32[128,128]{1,0:T(8,128)S(1)}, f32[128,128]{1,0:T(8,128)S(1)}, u32[]{:S(2)}, u32[]{:S(2)}) collective-permute-start(f32[128,128]{1,0:T(8,128)S(1)} %add_add_fusion.a), channel_id=1, source_target_pairs={{0,4},{4,0},{16,20},{20,16},{1,5},{5,1},{17,21},{21,17},{2,6},{6,2... | collective-permute-start | bytes 196616 | tf_op jit(solution)/shard_map/ppermute | solution.py:414
  217.8 4.2 %finish.1 = (f32[4500,128]{1,0:T(8,128)}, f32[128,128]{1,0:T(8,128)S(1)}) custom-call(s32[1]{0:T(128)} %bitcast.dev, f32[2304,128]{1,0:T(8,128)S(1)} %bitcast.6, f32[2304,128]{1,0:T(8,128)S(1)} %collective-permute-done.11.v.theirs, f32[128,128]{1,0:T(8,128)S(1)} %get-tuple-element.99.g, f32[128,128]{1,0:T(8,128)S(1)} %get-tuple-element.100.w), custom_call_target="tpu_custom_call" | custom-call | flops 630000000 | tf_op jit(solution)/shard_map/finish/pallas_call | solution.py:385
  (40 shorter events, 6.3 us)
Async XLA Ops:
  0.6 25.7 %copy-start = (f32[1024]{0:T(1024)S(1)}, f32[1024]{0:T(1024)}, u32[]{:S(2)}) copy-start(f32[1024]{0:T(1024)} %param.4) | copy-start | bytes 12292
  39.9 5.1 %collective-permute-start = (f32[4,288,128]{2,1,0:T(8,128)S(1)}, f32[4,288,128]{2,1,0:T(8,128)S(1)}, u32[]{:S(2)}, u32[]{:S(2)}) collective-permute-start(f32[4,288,128]{2,1,0:T(8,128)S(1)} %get-tuple-element.61), channel_id=1, source_target_pairs={{0,8},{8,0},{1,9},{9,1},{2,10},{10,2},{3,11},{11,3},{4,12},{12,4},... | collective-permute-start | bytes 1769480 | tf_op jit(solution)/shard_map/ppermute | solution.py:414
  46.5 2.2 collective-permute-start.2
  47.0 9.0 %collective-permute-start.1 = (f32[4,288,128]{2,1,0:T(8,128)S(1)}, f32[4,288,128]{2,1,0:T(8,128)S(1)}, u32[]{:S(2)}, u32[]{:S(2)}) collective-permute-start(f32[4,288,128]{2,1,0:T(8,128)S(1)} %shard_map.54), channel_id=1, source_target_pairs={{0,32},{8,24},{16,48},{24,8},{32,0},{40,56},{48,16},{56,40},{64,96... | collective-permute-start | bytes 1769480 | tf_op jit(solution)/shard_map/ppermute | solution.py:434
  56.0 5.8 %collective-permute-start.3 = (f32[2,288,128]{2,1,0:T(8,128)S(1)}, f32[2,288,128]{2,1,0:T(8,128)S(1)}, u32[]{:S(2)}, u32[]{:S(2)}) collective-permute-start(f32[2,288,128]{2,1,0:T(8,128)S(1)} %shard_map.57), channel_id=1, source_target_pairs={{0,96},{8,40},{16,112},{24,56},{32,64},{40,8},{48,80},{56,24},{64,... | collective-permute-start | bytes 884744 | tf_op jit(solution)/shard_map/ppermute | solution.py:434
  61.9 6.5 %collective-permute-start.4 = (f32[1,288,128]{2,1,0:T(8,128)S(1)}, f32[1,288,128]{2,1,0:T(8,128)S(1)}, u32[]{:S(2)}, u32[]{:S(2)}) collective-permute-start(f32[1,288,128]{2,1,0:T(8,128)S(1)} %shard_map.58), channel_id=1, source_target_pairs={{0,16},{8,104},{16,0},{24,120},{32,48},{40,72},{48,32},{56,88},{64... | collective-permute-start | bytes 442376 | tf_op jit(solution)/shard_map/ppermute | solution.py:434
  85.8 7.5 %collective-permute-start.5 = (f32[2304,128]{1,0:T(8,128)S(1)}, f32[2304,128]{1,0:T(8,128)S(1)}, u32[]{:S(2)}, u32[]{:S(2)}) collective-permute-start(f32[2304,128]{1,0:T(8,128)S(1)} %bitcast.7), channel_id=1, source_target_pairs={{0,8},{8,0},{1,9},{9,1},{2,10},{10,2},{3,11},{11,3},{4,12},{12,4},... | collective-permute-start | bytes 3538952 | tf_op jit(solution)/shard_map/ppermute | solution.py:414
  127.4 3.5 %collective-permute-start.6 = (f32[4,288,128]{2,1,0:T(8,128)S(1)}, f32[4,288,128]{2,1,0:T(8,128)S(1)}, u32[]{:S(2)}, u32[]{:S(2)}) collective-permute-start(f32[4,288,128]{2,1,0:T(8,128)S(1)} %get-tuple-element.69), channel_id=1, source_target_pairs={{0,8},{8,0},{1,9},{9,1},{2,10},{10,2},{3,11},{11,3},{4,12},{12,4},... | collective-permute-start | bytes 1769480 | tf_op jit(solution)/shard_map/ppermute | solution.py:414
  132.4 3.9 %collective-permute-start.8 = (f32[4,288,128]{2,1,0:T(8,128)S(1)}, f32[4,288,128]{2,1,0:T(8,128)S(1)}, u32[]{:S(2)}, u32[]{:S(2)}) collective-permute-start(f32[4,288,128]{2,1,0:T(8,128)S(1)} %shard_map.67), channel_id=1, source_target_pairs={{0,8},{8,0},{1,9},{9,1},{2,10},{10,2},{3,11},{11,3},{4,12},{12,4},... | collective-permute-start | bytes 1769480 | tf_op jit(solution)/shard_map/ppermute | solution.py:414
  132.8 9.0 %collective-permute-start.7 = (f32[4,288,128]{2,1,0:T(8,128)S(1)}, f32[4,288,128]{2,1,0:T(8,128)S(1)}, u32[]{:S(2)}, u32[]{:S(2)}) collective-permute-start(f32[4,288,128]{2,1,0:T(8,128)S(1)} %shard_map.65), channel_id=1, source_target_pairs={{0,32},{8,24},{16,48},{24,8},{32,0},{40,56},{48,16},{56,40},{64,96... | collective-permute-start | bytes 1769480 | tf_op jit(solution)/shard_map/ppermute | solution.py:434
  141.9 5.9 %collective-permute-start.9 = (f32[2,288,128]{2,1,0:T(8,128)S(1)}, f32[2,288,128]{2,1,0:T(8,128)S(1)}, u32[]{:S(2)}, u32[]{:S(2)}) collective-permute-start(f32[2,288,128]{2,1,0:T(8,128)S(1)} %shard_map.69), channel_id=1, source_target_pairs={{0,96},{8,40},{16,112},{24,56},{32,64},{40,8},{48,80},{56,24},{64,... | collective-permute-start | bytes 884744 | tf_op jit(solution)/shard_map/ppermute | solution.py:434
  147.9 5.3 %collective-permute-start.10 = (f32[1,288,128]{2,1,0:T(8,128)S(1)}, f32[1,288,128]{2,1,0:T(8,128)S(1)}, u32[]{:S(2)}, u32[]{:S(2)}) collective-permute-start(f32[1,288,128]{2,1,0:T(8,128)S(1)} %shard_map.71), channel_id=1, source_target_pairs={{0,16},{8,104},{16,0},{24,120},{32,48},{40,72},{48,32},{56,88},{64... | collective-permute-start | bytes 442376 | tf_op jit(solution)/shard_map/ppermute | solution.py:434
  169.5 7.5 %collective-permute-start.11 = (f32[2304,128]{1,0:T(8,128)S(1)}, f32[2304,128]{1,0:T(8,128)S(1)}, u32[]{:S(2)}, u32[]{:S(2)}) collective-permute-start(f32[2304,128]{1,0:T(8,128)S(1)} %bitcast.4), channel_id=1, source_target_pairs={{0,8},{8,0},{1,9},{9,1},{2,10},{10,2},{3,11},{11,3},{4,12},{12,4},... | collective-permute-start | bytes 3538952 | tf_op jit(solution)/shard_map/ppermute | solution.py:414
  199.3 2.2 collective-permute-start.12
  201.6 5.3 %collective-permute-start.15 = (f32[128,128]{1,0:T(8,128)S(1)}, f32[128,128]{1,0:T(8,128)S(1)}, u32[]{:S(2)}, u32[]{:S(2)}) collective-permute-start(f32[128,128]{1,0:T(8,128)S(1)} %add.37), channel_id=1, source_target_pairs={{0,96},{32,64},{64,32},{96,0},{1,97},{33,65},{65,33},{97,1},{2,98}... | collective-permute-start | bytes 196616 | tf_op jit(solution)/shard_map/ppermute | solution.py:414
  202.5 4.7 %collective-permute-start.14 = (f32[128,128]{1,0:T(8,128)S(1)}, f32[128,128]{1,0:T(8,128)S(1)}, u32[]{:S(2)}, u32[]{:S(2)}) collective-permute-start(f32[128,128]{1,0:T(8,128)S(1)} %add.37), channel_id=1, source_target_pairs={{0,64},{32,96},{64,0},{96,32},{1,65},{33,97},{65,1},{97,33},{2,66}... | collective-permute-start | bytes 196616 | tf_op jit(solution)/shard_map/ppermute | solution.py:414
  203.6 4.2 %collective-permute-start.13 = (f32[128,128]{1,0:T(8,128)S(1)}, f32[128,128]{1,0:T(8,128)S(1)}, u32[]{:S(2)}, u32[]{:S(2)}) collective-permute-start(f32[128,128]{1,0:T(8,128)S(1)} %add.37), channel_id=1, source_target_pairs={{0,32},{32,0},{64,96},{96,64},{1,33},{33,1},{65,97},{97,65},{2,34}... | collective-permute-start | bytes 196616 | tf_op jit(solution)/shard_map/ppermute | solution.py:414
  207.9 5.3 %collective-permute-start.18 = (f32[128,128]{1,0:T(8,128)S(1)}, f32[128,128]{1,0:T(8,128)S(1)}, u32[]{:S(2)}, u32[]{:S(2)}) collective-permute-start(f32[128,128]{1,0:T(8,128)S(1)} %add_add_fusion.1), channel_id=1, source_target_pairs={{0,3},{1,2},{2,1},{3,0},{4,7},{5,6},{6,5},{7,4},{8,11},{9,10},{10,... | collective-permute-start | bytes 196616 | tf_op jit(solution)/shard_map/ppermute | solution.py:414
  208.6 4.6 %collective-permute-start.17 = (f32[128,128]{1,0:T(8,128)S(1)}, f32[128,128]{1,0:T(8,128)S(1)}, u32[]{:S(2)}, u32[]{:S(2)}) collective-permute-start(f32[128,128]{1,0:T(8,128)S(1)} %add_add_fusion.1), channel_id=1, source_target_pairs={{0,2},{1,3},{2,0},{3,1},{4,6},{5,7},{6,4},{7,5},{8,10},{9,11},{10,... | collective-permute-start | bytes 196616 | tf_op jit(solution)/shard_map/ppermute | solution.py:414
  209.7 4.1 %collective-permute-start.16 = (f32[128,128]{1,0:T(8,128)S(1)}, f32[128,128]{1,0:T(8,128)S(1)}, u32[]{:S(2)}, u32[]{:S(2)}) collective-permute-start(f32[128,128]{1,0:T(8,128)S(1)} %add_add_fusion.1), channel_id=1, source_target_pairs={{0,1},{1,0},{2,3},{3,2},{4,5},{5,4},{6,7},{7,6},{8,9},{9,8},{10,11... | collective-permute-start | bytes 196616 | tf_op jit(solution)/shard_map/ppermute | solution.py:414
  213.9 8.2 %collective-permute-start.21 = (f32[128,128]{1,0:T(8,128)S(1)}, f32[128,128]{1,0:T(8,128)S(1)}, u32[]{:S(2)}, u32[]{:S(2)}) collective-permute-start(f32[128,128]{1,0:T(8,128)S(1)} %add_add_fusion.a), channel_id=1, source_target_pairs={{0,20},{4,16},{16,4},{20,0},{1,21},{5,17},{17,5},{21,1},{2,22},{6,... | collective-permute-start | bytes 196616 | tf_op jit(solution)/shard_map/ppermute | solution.py:414
  214.2 7.8 %collective-permute-start.20 = (f32[128,128]{1,0:T(8,128)S(1)}, f32[128,128]{1,0:T(8,128)S(1)}, u32[]{:S(2)}, u32[]{:S(2)}) collective-permute-start(f32[128,128]{1,0:T(8,128)S(1)} %add_add_fusion.a), channel_id=1, source_target_pairs={{0,16},{4,20},{16,0},{20,4},{1,17},{5,21},{17,1},{21,5},{2,18},{6,... | collective-permute-start | bytes 196616 | tf_op jit(solution)/shard_map/ppermute | solution.py:414
  214.2 7.8 %collective-permute-start.19 = (f32[128,128]{1,0:T(8,128)S(1)}, f32[128,128]{1,0:T(8,128)S(1)}, u32[]{:S(2)}, u32[]{:S(2)}) collective-permute-start(f32[128,128]{1,0:T(8,128)S(1)} %add_add_fusion.a), channel_id=1, source_target_pairs={{0,4},{4,0},{16,20},{20,16},{1,5},{5,1},{17,21},{21,17},{2,6},{6,2... | collective-permute-start | bytes 196616 | tf_op jit(solution)/shard_map/ppermute | solution.py:414
where the time goes:
time: 226 us; the launch traced here: 223 us
  blocking collectives  111 us (49%)
  Pallas kernels  47.2 us (21%)
  starting transfers between devices  34.3 us (15%)
  waiting for transfers between devices  28.9 us (13%)
    all_to_all x7, blocking collectives, to_each(): return lax.all_to_all(value, axes, split_axis=0, concat_axis=0, tiled=True)  111 us
    pallas_call x30, Pallas kernels, kernel_call(): pl.pallas_call(body, out_shape=[pltpu.VMEM(s, d) for s, d in outs], in_sp...  43 us
    ppermute x16, starting transfers between devices, exchange(): return lax.ppermute(value, axis, [(i, i ^ mask) for i in range(n)])  27.1 us
    ppermute x6, waiting for transfers between devices, cross(): return lax.ppermute(value, ('z', 'xl', 'c'), pairs)  25.9 us
    ppermute x6, starting transfers between devices, cross(): return lax.ppermute(value, ('z', 'xl', 'c'), pairs)  7.15 us
  transfers between devices with their start and end apart: 22, of which 12 were waited for; matrix products, arithmetic and copies ran while one was open for 0% of the time, Pallas kernels for 11%

commit v1 on v0

--- a/solution.py
+++ b/solution.py
@@ -1,3 +1,5 @@
+import itertools
+
 import jax
 import jax.numpy as jnp
 from jax import lax
@@ -68,6 +70,20 @@
     )(*smem, *hbm, *[pltpu.with_memory_space_constraint(v, pltpu.VMEM) for v in vmem])
 
 
+MASK = {("z", 1): 1, ("z", 3): 3, ("xl", 1): 4, ("y", 1): 1, ("y", 3): 3, ("xh", 1): 4}
+NEAR_LINKS = ((("z", 1), ("z", 3), ("xl", 1)), (("xl", 1), ("z", 1), ("z", 3)))
+AUX_LINKS = ((("y", 1), ("y", 3), ("xh", 1)), (("y", 3), ("y", 1), ("xh", 1)))
+
+
+def piece_at(links, core, me, p):
+    masks = [0, 0]
+    for c in range(2):
+        for t in range(3):
+            if (p >> (2 - t)) & 1:
+                masks[c] ^= MASK[links[c][t]]
+    return me ^ jnp.where(core == 0, masks[0], masks[1])
+
+
 def transposed_halves(v):
     hi, lo = split(v.T)
     return jnp.concatenate([hi, lo], axis=0)
@@ -90,25 +106,38 @@
         for i in range(CHUNKS):
             for c in copies(i):
                 c.start()
-        for i in range(CHUNKS):
-            for c in copies(i):
-                c.wait()
-            slot = i
-            if i == CHUNKS - 1:
-                slot = 0
-                bbuf[0, TAIL // 8 * 8 :, :] = jnp.zeros((CHUNK - TAIL // 8 * 8, PAIRS_L), F32)
-                vbuf[0, TAIL // 8 * 8 :, :] = jnp.zeros((CHUNK - TAIL // 8 * 8, K), F32)
-                bbuf[0, 0:TAIL, :] = btail[...]
-                vbuf[0, 0:TAIL, :] = vtail[...]
+
+        def chunk(slot, row0, first):
             vt = transposed_halves(vbuf[slot])
             for n in range(4):
                 hi, lo = split(bbuf[slot, :, 256 * n : 256 * n + 256])
-                bhi[n, CHUNK * i : CHUNK * (i + 1), :] = hi
-                blo[n, CHUNK * i : CHUNK * (i + 1), :] = lo
-                part = fold(dot(vt, hi, 1, 0) + dot(vt, lo, 1, 0))
+                bhi[n, pl.ds(row0, CHUNK), :] = hi
+                blo[n, pl.ds(row0, CHUNK), :] = lo
+                part = fold(dot(vt, hi, 1, 0)) + dot(vt[0:K], lo, 1, 0)
                 for t in range(2):
                     value = part[:, 128 * t : 128 * t + 128]
-                    out[2 * n + t] = value if i == 0 else out[2 * n + t] + value
+                    out[2 * n + t] = value if first else out[2 * n + t] + value
+
+        for c in copies(0):
+            c.wait()
+        chunk(0, 0, True)
+
+        def middle(i, carry):
+            rows = pl.ds(pl.multiple_of(i * CHUNK, CHUNK), CHUNK)
+            pltpu.make_async_copy(b_hbm.at[rows], bbuf.at[i], sems.at[0, i]).wait()
+            pltpu.make_async_copy(v_hbm.at[rows], vbuf.at[i], sems.at[1, i]).wait()
+            chunk(i, pl.multiple_of(i * CHUNK, CHUNK), False)
+            return carry
+
+        lax.fori_loop(1, CHUNKS - 1, middle, 0)
+        for c in copies(CHUNKS - 1):
+            c.wait()
+        whole = TAIL // 8 * 8
+        bbuf[0, whole:, :] = jnp.zeros((CHUNK - whole, PAIRS_L), F32)
+        vbuf[0, whole:, :] = jnp.zeros((CHUNK - whole, K), F32)
+        bbuf[0, 0:TAIL, :] = btail[...]
+        vbuf[0, 0:TAIL, :] = vtail[...]
+        chunk(0, CHUNK * (CHUNKS - 1), False)
 
     halves = ((4, ROWS, 256), BF16)
     coeffs = pltpu.with_memory_space_constraint(coeffs, pltpu.HBM)
@@ -131,39 +160,43 @@
     )
 
 
-def project_half(dev, bhi, blo, v, so_far, gram_rows=GRAM_J):
+def project_half(dev, bhi, blo, v, so_far, by_position=False):
     def body(dev, bhi, blo, v, *rest):
         if so_far is None:
             acc, gacc = rest
             half = core_of(dev)
         else:
-            acc0, gacc0, out, acc, gacc = rest
+            acc0, gacc0, *outs, acc, gacc = rest
             half = 1 - core_of(dev)
         for i in range(3):
             row0 = pl.multiple_of(half * HALF + i * CHUNK, CHUNK)
             vt = transposed_halves(v[CHUNK * i : CHUNK * (i + 1), :])
             for n in range(4):
-                part = fold(
-                    dot(vt, bhi[n, pl.ds(row0, CHUNK), :], 1, 0)
-                    + dot(vt, blo[n, pl.ds(row0, CHUNK), :], 1, 0)
-                )
+                part = fold(dot(vt, bhi[n, pl.ds(row0, CHUNK), :], 1, 0))
+                part = part + dot(vt[0:K], blo[n, pl.ds(row0, CHUNK), :], 1, 0)
                 for t in range(2):
                     value = part[:, 128 * t : 128 * t + 128]
                     j = 2 * n + t
                     if i > 0:
                         value = acc[j] + value
                     if so_far is not None and i == 2:
-                        out[j, 0:K, :] = acc0[j] + value
-                    else:
-                        acc[j] = value
+                        value = acc0[j] + value
+                    acc[j] = value
             g = dot(vt, vt, 1, 1)
             gacc[...] = g if i == 0 else gacc[...] + g
         if so_far is not None:
             g = gacc[...] + gacc0[...]
             gram = (g[0:K, 0:K] + g[K:, K:]) + (g[0:K, K:] + g[K:, 0:K])
-            for j in range(CHIPS):
-                first = GRAM_J * j if gram_rows < K else 0
-                out[j, K:, :] = gram[first : first + gram_rows, :]
+            if by_position:
+                for t, out in enumerate(outs):
+                    for p in range(4):
+                        at = piece_at(AUX_LINKS, core_of(dev), aux_of(dev), 4 - 4 * t + p)
+                        out[p] = acc[at]
+                    out[4] = gram
+            else:
+                for j in range(CHIPS):
+                    outs[0][j, 0:K, :] = acc[j]
+                    outs[0][j, K:, :] = gram[GRAM_J * j : GRAM_J * (j + 1), :]
 
     acc = ((CHIPS, K, PAIRS_J), F32)
     gacc = ((2 * K, 2 * K), F32)
@@ -171,7 +204,7 @@
         return kernel_call(body, [acc, gacc], [dev], [], [bhi, blo, v], us=3.0)
     return kernel_call(
         body,
-        [((CHIPS, K + gram_rows, PAIRS_J), F32)],
+        [((5, K, K), F32)] * 2 if by_position else [((CHIPS, K + GRAM_J, PAIRS_J), F32)],
         [dev],
         [],
         [bhi, blo, v, *so_far],
@@ -180,40 +213,48 @@
     )
 
 
-def sum_aux(dev, parts, gaps, copies):
-    rows = parts.shape[1]
-
-    def body(dev, p, gaps, *outs):
-        gap = gaps[pl.ds(aux_of(dev), 1), :]
+def weights_of(dev, gaps):
+    gap = gaps[pl.ds(aux_of(dev), 1), :]
+    return 4.0 * gap / (gap * gap + 1.0)
+
+
+def sum_aux(dev, parts, gaps):
+    def body(dev, p, gaps, out):
         s = ((p[0] + p[1]) + (p[2] + p[3])) + ((p[4] + p[5]) + (p[6] + p[7]))
-        piece = s[0:K] * (4.0 * gap / (gap * gap + 1.0))
-        if copies:
-            for j in range(CHIPS):
-                outs[0][j, 0:K, :] = piece
-                if rows > K:
-                    outs[0][j, K:, :] = s[K:]
-        else:
-            outs[0][...] = dot(piece, s[0:K], 1, 1, HIGHEST)
-            outs[1][...] = s[K:]
-
-    if copies:
-        outs = [((CHIPS, rows, PAIRS_J), F32)]
-    else:
-        outs = [((K, K), F32), ((K, K), F32)]
-    return kernel_call(body, outs, [dev], [], [parts, gaps])
-
-
-NEAR_MASK = {("z", 1): 1, ("z", 3): 3, ("xl", 1): 4}
-CROSS = ((("z", 1), ("z", 3), ("xl", 1)), (("xl", 1), ("z", 1), ("z", 3)))
-
-
-def piece_at(core, near, p):
-    masks = [0, 0]
-    for c in range(2):
-        for t in range(3):
-            if (p >> (2 - t)) & 1:
-                masks[c] ^= NEAR_MASK[CROSS[c][t]]
-    return near ^ jnp.where(core == 0, masks[0], masks[1])
+        piece = s[0:K] * weights_of(dev, gaps)
+        for j in range(CHIPS):
+            out[j, 0:K, :] = piece
+            if p.shape[1] > K:
+                out[j, K:, :] = s[K:]
+
+    return kernel_call(body, [(parts.shape, F32)], [dev], [], [parts, gaps])[0]
+
+
+def reduce_aux(dev, send, keep, gaps):
+    def last_step(k, r1, r2, out):
+        out[0] = (k[1] + r1[1]) + r2[1]
+        out[1] = (k[4] + r1[4]) + r2[2]
+
+    def finish_sum(dev, k, r1, r2, r3, gaps, out):
+        own = ((k[0] + r1[0]) + r2[0]) + r3[0]
+        out[0] = dot(own * weights_of(dev, gaps), own, 1, 1, HIGHEST)
+        out[1] = ((k[4] + r1[4]) + r2[2]) + r3[1]
+
+    two = ((2, K, K), F32)
+    r1 = cross(send, 0, AUX_LINKS)
+    r2 = cross(add_slots(2, 3, keep, r1), 1, AUX_LINKS)
+    (send,) = kernel_call(last_step, [two], [], [], [keep, r1, r2])
+    r3 = cross(send, 2, AUX_LINKS)
+    return kernel_call(finish_sum, [two], [dev], [], [keep, r1, r2, r3, gaps])[0]
+
+
+def add_over_cores(dev, both):
+    def body(dev, own, got, total, gram):
+        total[...] = own[0] + got[0]
+        gram[...] = jnp.where(core_of(dev) == 1, own[1], got[1])
+
+    got = exchange(both, "c", 1)
+    return kernel_call(body, [((K, K), F32)] * 2, [dev], [], [both, got])
 
 
 def apply_pieces(dev, bhi, blo, scaled, other, make_rhs, first):
@@ -231,8 +272,8 @@
         if other:
             core = 1 - core
 
-        for i in range(4):
-            start = core * HALF + piece_at(core, near_of(dev), first + i) * PIECE
+        for i in range(2):
+            start = core * HALF + piece_at(NEAR_LINKS, core, near_of(dev), first + i) * PIECE
             start = pl.multiple_of(start, PIECE)
             res = None
             for ref in (bhi, blo):
@@ -241,10 +282,10 @@
                     res = d if res is None else res + d
             out[i] = res[:, 0:K] + res[:, K : 2 * K]
 
-    outs = [((4, PIECE, K), F32)]
+    outs = [((2, PIECE, K), F32)]
     if make_rhs:
         outs.append(((4, 2 * K, 256), BF16))
-    return kernel_call(body, outs, [dev], [], [bhi, blo, scaled], us=1.4)
+    return kernel_call(body, outs, [dev], [], [bhi, blo, scaled], us=0.75)
 
 
 def add_slots(first, count, *parts):
@@ -254,21 +295,21 @@
             total = total + r[first : first + count]
         refs[-1][...] = total
 
-    return kernel_call(body, [((count, PIECE, K), F32)], [], [], list(parts))[0]
+    shape = (count, *parts[0].shape[1:])
+    return kernel_call(body, [(shape, F32)], [], [], list(parts))[0]
 
 
 def sum_rows(parts, inverse):
     def body(*refs):
         out = refs[-1]
         own, got, r1, r2, r3 = refs[:5]
-        s = (own[0] + got[0]) + r1[0] + (r2[0] + r3[0])
+        s = ((own[0] + got[0]) + r1[0]) + (r2[0] + r3[0])
         if inverse is not None:
             s = dot(s, refs[len(parts)][...], 1, 1, HIGHEST)
-        for j in range(CHIPS):
-            out[j] = s
+        out[0] = s
 
     extra = [] if inverse is None else [inverse]
-    return kernel_call(body, [((CHIPS, PIECE, K), F32)], [], [], [*parts, *extra])[0]
+    return kernel_call(body, [((1, PIECE, K), F32)], [], [], [*parts, *extra])[0]
 
 
 def pivots(gs, ws, begin, end):
@@ -418,43 +459,67 @@
     return lax.all_to_all(value, axes, split_axis=0, concat_axis=0, tiled=True)
 
 
-NEAR = ("xl", "z")
 AUX = ("xh", "y")
 
 
-def cross(value, step):
-    nz, nx = lax.axis_size("z"), lax.axis_size("xl")
+def cross(value, step, links=NEAR_LINKS):
+    axes = ("z", "xl", "c") if links is NEAR_LINKS else ("c", "xh", "y")
+    sizes = [lax.axis_size(a) for a in axes]
     pairs = []
-    for z in range(nz):
-        for x in range(nx):
-            for c in range(2):
-                axis, mask = CROSS[c][step]
-                to = (z ^ mask, x) if axis == "z" else (z, x ^ mask)
-                pairs.append(((z * nx + x) * 2 + c, (to[0] * nx + to[1]) * 2 + c))
-    return lax.ppermute(value, ("z", "xl", "c"), pairs)
+    for at in itertools.product(*map(range, sizes)):
+        to = dict(zip(axes, at))
+        axis, mask = links[to["c"]][step]
+        to[axis] ^= mask
+        ids = [(a * sizes[1] + b) * sizes[2] + c for a, b, c in (at, tuple(to.values()))]
+        pairs.append(tuple(ids))
+    return lax.ppermute(value, axes, pairs)
 
 
 def reduce_rows(dev, bhi, blo, scaled, eliminating):
-    send, rhs = apply_pieces(dev, bhi, blo, scaled, True, True, 4)
-    got = exchange(send, "c", 1)
-    (own,) = apply_pieces(dev, bhi, blo, rhs, False, False, 4)
-    first = add_slots(0, 4, own, got)
-    r1 = cross(first, 0)
-    first, rhs = lax.optimization_barrier((first, rhs))
-    (send,) = apply_pieces(dev, bhi, blo, rhs, True, False, 0)
-    got = exchange(send, "c", 1)
-    (own,) = apply_pieces(dev, bhi, blo, rhs, False, False, 0)
-    r1, own, got = lax.optimization_barrier((r1, own, got))
+    rhs = None
+
+    def apply_pair(first):
+        nonlocal rhs
+        send, *made = apply_pieces(
+            dev, bhi, blo, scaled if rhs is None else rhs, True, rhs is None, first
+        )
+        rhs = made[0] if made else rhs
+        got = exchange(send, "c", 1)
+        (own,) = apply_pieces(dev, bhi, blo, rhs, False, False, first)
+        return own, got
+
+    steps = []
+    for first in (6, 4, 2, 0):
+        own, got = apply_pair(first)
+        if first == 0:
+            break
+        value = add_slots(0, 2, own, got, *(steps[:1] if first == 2 else ()))
+        steps.append(cross(value, 1 if first == 2 else 0))
+        value, rhs = lax.optimization_barrier((value, rhs))
+    _, r1, r2 = steps
     inverse = None
     if eliminating:
-        r1, state = in_between(r1, [scaled], (0, 40))
-    r2 = cross(add_slots(2, 2, own, got, r1), 1)
-    if eliminating:
-        r2, state = in_between(r2, state, (40, 80))
+        r2, own, got = lax.optimization_barrier((r2, own, got))
+        r2, state = in_between(r2, [scaled], (0, 64))
     r3 = cross(add_slots(1, 1, own, got, r1, r2), 2)
     if eliminating:
-        r3, (inverse,) = in_between(r3, state, (80, 128))
+        r3, (inverse,) = in_between(r3, state, (64, 128))
     return sum_rows([own, got, r1, r2, r3], inverse)
+
+
+def gather_rows(dev, own):
+    p = [own] + [None] * 7
+    for a, step in ((0, 2), (0, 1), (0, 0), (1, 1), (1, 0), (2, 0), (3, 0)):
+        at = a | (4 >> step)
+        p[at] = cross(p[a], step)
+
+    def body(dev, *refs):
+        for at in range(CHIPS):
+            to = piece_at(NEAR_LINKS, core_of(dev), near_of(dev), at)
+            refs[-1][to] = refs[at][0]
+
+    pieces = ((CHIPS, PIECE, K), F32)
+    return kernel_call(body, [pieces], [dev], [], p)[0].reshape(HALF, K)
 
 
 def shards(pair_coeffs, pair_gaps, trial_vectors):
@@ -463,15 +528,12 @@
     dev, gaps, trial_vectors = lax.optimization_barrier((dev, gaps, trial_vectors))
     bhi, blo, parts = first_projection(pair_coeffs, trial_vectors)
     for step in range(2):
-        (copies,) = sum_aux(dev, to_each(parts, AUX), gaps, True)
-        scaled = to_each(copies, AUX)
-        near = reduce_rows(dev, bhi, blo, scaled, step == 1)
-        mine = to_each(near, NEAR).reshape(HALF, K)
+        scaled = to_each(sum_aux(dev, to_each(parts, AUX), gaps), AUX)
+        mine = gather_rows(dev, reduce_rows(dev, bhi, blo, scaled, step == 1))
         theirs = exchange(mine, "c", 1)
         so_far = project_half(dev, bhi, blo, mine, None)
-        (parts,) = project_half(dev, bhi, blo, theirs, so_far, K if step == 1 else GRAM_J)
-    total, gram = sum_aux(dev, to_each(parts, AUX), gaps, False)
-    total = total + exchange(total, "c", 1)
+        parts, *kept = project_half(dev, bhi, blo, theirs, so_far, step == 1)
+    total, gram = add_over_cores(dev, reduce_aux(dev, parts, *kept, gaps))
     state = [gram]
     for axis, cut in (("z", (0, 40)), ("y", (40, 84)), (("xl", "xh"), None)):
         got = []

time: 226 us -> 216 us (0.956)
  blocking collectives: 111 us -> 57.1 us
  waiting for transfers between devices: 28.9 us -> 52.8 us
  starting transfers between devices: 34.3 us -> 54.5 us
    all_to_all x7 -> x4, blocking collectives: 111 us -> 57.1 us  [to_each(): return lax.all_to_all(value, axes, split_axis=0, concat_axis=0, tiled=True)]
    ppermute x6 -> x25, waiting for transfers between devices: 25.9 us -> 49.7 us  [cross(): return lax.ppermute(value, axes, pairs)]
    ppermute x6 -> x25, starting transfers between devices: 7.15 us -> 17.9 us  [cross(): return lax.ppermute(value, axes, pairs)]
    ppermute x16 -> x20, starting transfers between devices: 27.1 us -> 36.6 us  [exchange(): return lax.ppermute(value, axis, [(i, i ^ mask) for i in range(n)])]
    pallas_call x30 -> x44, Pallas kernels: 43 us -> 42.4 us  [kernel_call(): pl.pallas_call(body, out_shape=[pltpu.VMEM(s, d) for s, d in outs], in_sp...]
  transfers between devices with their start and end apart: 22 -> 45, of which waited for: 12 -> 26; matrix products, arithmetic and copies ran while one was open for 0% -> 0% of each run, Pallas kernels for 11% -> 13%
where the time goes in v1:
time: 216 us; the launch traced here: 213 us
  blocking collectives  57.1 us (26%)
  starting transfers between devices  54.5 us (25%)
  waiting for transfers between devices  52.8 us (24%)
  Pallas kernels  46.7 us (22%)
    all_to_all x4, blocking collectives, to_each(): return lax.all_to_all(value, axes, split_axis=0, concat_axis=0, tiled=True)  57.1 us
    ppermute x25, waiting for transfers between devices, cross(): return lax.ppermute(value, axes, pairs)  49.7 us
    pallas_call x44, Pallas kernels, kernel_call(): pl.pallas_call(body, out_shape=[pltpu.VMEM(s, d) for s, d in outs], in_sp...  42.4 us
    ppermute x20, starting transfers between devices, exchange(): return lax.ppermute(value, axis, [(i, i ^ mask) for i in range(n)])  36.6 us
    ppermute x25, starting transfers between devices, cross(): return lax.ppermute(value, axes, pairs)  17.9 us
  transfers between devices with their start and end apart: 45, of which 26 were waited for; matrix products, arithmetic and copies ran while one was open for 0% of the time, Pallas kernels for 13%

profile of v1, /device:TPU:1, one launch (start us, length us, event | category | flops | bytes accessed | tf_op | source)
XLA Modules:
  0.0 212.8 jit_solution(8178784870271473289)
XLA Ops:
  0.7 8.3 %shard_map.50 = (bf16[4,4608,256]{2,1,0:T(8,128)(2,1)S(1)}, bf16[4,4608,256]{2,1,0:T(8,128)(2,1)S(1)}, f32[8,128,128]{2,1,0:T(8,128)S(1)}) custom-call(f32[4500,1024]{1,0:T(8,128)} %b_hbm.1, f32[4500,128]{1,0:T(8,128)} %v_hbm), custom_call_target="tpu_custom_call" | custom-call | flops 1200000000 | tf_op jit(solution)/shard_map/pallas_call | solution.py:60
  8.9 17.3 %all_to_all.20.p = f32[8,128,128]{2,1,0:T(8,128)S(1)} all-to-all(f32[8,128,128]{2,1,0:T(8,128)S(1)} %get-tuple-element.56), channel_id=1, replica_groups=mesh['z'=4,'xl'=2,'c'=2,'xh'=2,'y'=4] {'xh','y'}, dimensions={0} | all-to-all | bytes 1048576 | tf_op jit(solution)/shard_map/all_to_all | solution.py:459
  26.3 12.1 %all_to_all.21.s = f32[8,128,128]{2,1,0:T(8,128)S(1)} all-to-all(f32[8,128,128]{2,1,0:T(8,128)S(1)} %shard_map.51), channel_id=1, replica_groups=mesh['z'=4,'xl'=2,'c'=2,'xh'=2,'y'=4] {'xh','y'}, dimensions={0} | all-to-all | bytes 1048576 | tf_op jit(solution)/shard_map/all_to_all | solution.py:459
  39.2 3.5 %collective-permute-start = (f32[2,288,128]{2,1,0:T(8,128)S(1)}, f32[2,288,128]{2,1,0:T(8,128)S(1)}, u32[]{:S(2)}, u32[]{:S(2)}) collective-permute-start(f32[2,288,128]{2,1,0:T(8,128)S(1)} %get-tuple-element.59), channel_id=1, source_target_pairs={{0,8},{8,0},{1,9},{9,1},{2,10},{10,2},{3,11},{11,3},{4,12},{12,4},... | collective-permute-start | bytes 884744 | tf_op jit(solution)/shard_map/ppermute | solution.py:455
  47.2 1.7 collective-permute-start.2
  53.0 1.6 collective-permute-start.6
  55.4 3.6 %collective-permute-done.6.refs_3_ = f32[2,288,128]{2,1,0:T(8,128)S(1)} collective-permute-done((f32[2,288,128]{2,1,0:T(8,128)S(1)}, f32[2,288,128]{2,1,0:T(8,128)S(1)}, u32[]{:S(2)}, u32[]{:S(2)}) %collective-permute-start.6) | collective-permute-done | bytes 294944 | tf_op jit(solution)/shard_map/ppermute | solution.py:475
  59.0 3.7 %collective-permute-start.7 = (f32[1,288,128]{2,1,0:T(8,128)S(1)}, f32[1,288,128]{2,1,0:T(8,128)S(1)}, u32[]{:S(2)}, u32[]{:S(2)}) collective-permute-start(f32[1,288,128]{2,1,0:T(8,128)S(1)} %shard_map.63), channel_id=1, source_target_pairs={{0,16},{8,104},{16,0},{24,120},{32,48},{40,72},{48,32},{56,88},{64... | collective-permute-start | bytes 442376 | tf_op jit(solution)/shard_map/ppermute | solution.py:475
  62.7 2.5 %collective-permute-done.7.refs_4_ = f32[1,288,128]{2,1,0:T(8,128)S(1)} collective-permute-done((f32[1,288,128]{2,1,0:T(8,128)S(1)}, f32[1,288,128]{2,1,0:T(8,128)S(1)}, u32[]{:S(2)}, u32[]{:S(2)}) %collective-permute-start.7) | collective-permute-done | bytes 147488 | tf_op jit(solution)/shard_map/ppermute | solution.py:475
  65.3 2.8 %collective-permute-start.8 = (f32[1,288,128]{2,1,0:T(8,128)S(1)}, f32[1,288,128]{2,1,0:T(8,128)S(1)}, u32[]{:S(2)}, u32[]{:S(2)}) collective-permute-start(f32[1,288,128]{2,1,0:T(8,128)S(1)} %shard_map.64.refs_0_), channel_id=1, source_target_pairs={{0,16},{8,104},{16,0},{24,120},{32,48},{40,72},{48,32},{56,88},{64... | collective-permute-start | bytes 442376 | tf_op jit(solution)/shard_map/ppermute | solution.py:475
  68.0 2.5 %collective-permute-done.8.refs_1_ = f32[1,288,128]{2,1,0:T(8,128)S(1)} collective-permute-done((f32[1,288,128]{2,1,0:T(8,128)S(1)}, f32[1,288,128]{2,1,0:T(8,128)S(1)}, u32[]{:S(2)}, u32[]{:S(2)}) %collective-permute-start.8) | collective-permute-done | bytes 147488 | tf_op jit(solution)/shard_map/ppermute | solution.py:475
  70.9 1.1 collective-permute-start.12
  72.4 2.2 %collective-permute-done.10.refs_3_ = f32[1,288,128]{2,1,0:T(8,128)S(1)} collective-permute-done((f32[1,288,128]{2,1,0:T(8,128)S(1)}, f32[1,288,128]{2,1,0:T(8,128)S(1)}, u32[]{:S(2)}, u32[]{:S(2)}) %collective-permute-start.10) | collective-permute-done | bytes 147488 | tf_op jit(solution)/shard_map/ppermute | solution.py:475
  74.9 3.1 %collective-permute-done.13.refs_6_ = f32[1,288,128]{2,1,0:T(8,128)S(1)} collective-permute-done((f32[1,288,128]{2,1,0:T(8,128)S(1)}, f32[1,288,128]{2,1,0:T(8,128)S(1)}, u32[]{:S(2)}, u32[]{:S(2)}) %collective-permute-start.13) | collective-permute-done | bytes 147488 | tf_op jit(solution)/shard_map/ppermute | solution.py:475
  78.0 1.6 collective-permute-done.14.refs_7_
  79.7 6.1 %collective-permute-start.15 = (f32[2304,128]{1,0:T(8,128)S(1)}, f32[2304,128]{1,0:T(8,128)S(1)}, u32[]{:S(2)}, u32[]{:S(2)}) collective-permute-start(f32[2304,128]{1,0:T(8,128)S(1)} %bitcast.7), channel_id=1, source_target_pairs={{0,8},{8,0},{1,9},{9,1},{2,10},{10,2},{3,11},{11,3},{4,12},{12,4},... | collective-permute-start | bytes 3538952 | tf_op jit(solution)/shard_map/ppermute | solution.py:455
  85.8 2.5 %shard_map.66 = (f32[8,128,128]{2,1,0:T(8,128)S(1)}, f32[256,256]{1,0:T(8,128)S(1)}) custom-call(s32[1]{0:T(128)} %bitcast.dev, bf16[4,4608,256]{2,1,0:T(8,128)(2,1)S(1)} %get-tuple-element.54.bhi, bf16[4,4608,256]{2,1,0:T(8,128)(2,1)S(1)} %get-tuple-element.55.blo, f32[2304,128]{1,0:T(8,128)S(1)} %bitcast.8), custom_call_target="tpu_custom_call" | custom-call | flops 450000000 | tf_op jit(solution)/shard_map/pallas_call | solution.py:60
  88.3 2.5 %shard_map.67 = f32[8,144,128]{2,1,0:T(8,128)S(1)} custom-call(s32[1]{0:T(128)} %bitcast.dev, bf16[4,4608,256]{2,1,0:T(8,128)(2,1)S(1)} %get-tuple-element.54.bhi, bf16[4,4608,256]{2,1,0:T(8,128)(2,1)S(1)} %get-tuple-element.55.blo, f32[2304,128]{1,0:T(8,128)S(1)} %collective-permute-done.15.v, f32[8,128,128]{2,1,0:T(8,128)S(1)} %get-tuple-element.63.rest_0_, ...), custom_call_target="tpu_custom_call" | custom-call | flops 450000000 | tf_op jit(solution)/shard_map/pallas_call | solution.py:60
  90.7 14.1 %all_to_all.22.p = f32[8,144,128]{2,1,0:T(8,128)S(1)} all-to-all(f32[8,144,128]{2,1,0:T(8,128)S(1)} %shard_map.67), channel_id=1, replica_groups=mesh['z'=4,'xl'=2,'c'=2,'xh'=2,'y'=4] {'xh','y'}, dimensions={0} | all-to-all | bytes 1179648 | tf_op jit(solution)/shard_map/all_to_all | solution.py:459
  104.9 13.7 %all_to_all.23.s.refs_0_ = f32[8,144,128]{2,1,0:T(8,128)S(1)} all-to-all(f32[8,144,128]{2,1,0:T(8,128)S(1)} %shard_map.68), channel_id=1, replica_groups=mesh['z'=4,'xl'=2,'c'=2,'xh'=2,'y'=4] {'xh','y'}, dimensions={0} | all-to-all | bytes 1179648 | tf_op jit(solution)/shard_map/all_to_all | solution.py:459
  119.4 2.6 %collective-permute-start.16 = (f32[2,288,128]{2,1,0:T(8,128)S(1)}, f32[2,288,128]{2,1,0:T(8,128)S(1)}, u32[]{:S(2)}, u32[]{:S(2)}) collective-permute-start(f32[2,288,128]{2,1,0:T(8,128)S(1)} %get-tuple-element.66), channel_id=1, source_target_pairs={{0,8},{8,0},{1,9},{9,1},{2,10},{10,2},{3,11},{11,3},{4,12},{12,4},... | collective-permute-start | bytes 884744 | tf_op jit(solution)/shard_map/ppermute | solution.py:455
  127.9 2.5 %collective-permute-done.19.refs_2_ = f32[2,288,128]{2,1,0:T(8,128)S(1)} collective-permute-done((f32[2,288,128]{2,1,0:T(8,128)S(1)}, f32[2,288,128]{2,1,0:T(8,128)S(1)}, u32[]{:S(2)}, u32[]{:S(2)}) %collective-permute-start.19) | collective-permute-done | bytes 294944 | tf_op jit(solution)/shard_map/ppermute | solution.py:475
  131.3 1.1 collective-permute-start.21
  132.8 3.2 %shard_map.80 = (f32[128,128]{1,0:T(8,128)S(1)}, f32[128,128]{1,0:T(8,128)S(1)}) custom-call(f32[8,144,128]{2,1,0:T(8,128)S(1)} %all_to_all.23.s.refs_0_), custom_call_target="tpu_custom_call" | custom-call | flops 480000000 | tf_op jit(solution)/shard_map/pallas_call | solution.py:60
  136.9 2.4 %collective-permute-done.20.refs_3_ = f32[2,288,128]{2,1,0:T(8,128)S(1)} collective-permute-done((f32[2,288,128]{2,1,0:T(8,128)S(1)}, f32[2,288,128]{2,1,0:T(8,128)S(1)}, u32[]{:S(2)}, u32[]{:S(2)}) %collective-permute-start.20) | collective-permute-done | bytes 294944 | tf_op jit(solution)/shard_map/ppermute | solution.py:475
  139.3 1.4 collective-permute-start.23
  140.6 2.5 %shard_map.82.refs_5_ = f32[128,128]{1,0:T(8,128)S(1)} custom-call(f32[128,128]{1,0:T(8,128)S(1)} %get-tuple-element.76.refs_0_, f32[128,128]{1,0:T(8,128)S(1)} %get-tuple-element.77.refs_1_), custom_call_target="tpu_custom_call" | custom-call | flops 480000000 | tf_op jit(solution)/shard_map/pallas_call | solution.py:60
  143.1 1.4 collective-permute-done.23.refs_4_
  144.8 1.4 collective-permute-start.24
  146.2 3.9 %collective-permute-done.24.refs_1_ = f32[1,288,128]{2,1,0:T(8,128)S(1)} collective-permute-done((f32[1,288,128]{2,1,0:T(8,128)S(1)}, f32[1,288,128]{2,1,0:T(8,128)S(1)}, u32[]{:S(2)}, u32[]{:S(2)}) %collective-permute-start.24) | collective-permute-done | bytes 147488 | tf_op jit(solution)/shard_map/ppermute | solution.py:475
  150.5 1.1 collective-permute-start.28
  151.9 2.2 %collective-permute-done.26.refs_3_ = f32[1,288,128]{2,1,0:T(8,128)S(1)} collective-permute-done((f32[1,288,128]{2,1,0:T(8,128)S(1)}, f32[1,288,128]{2,1,0:T(8,128)S(1)}, u32[]{:S(2)}, u32[]{:S(2)}) %collective-permute-start.26) | collective-permute-done | bytes 147488 | tf_op jit(solution)/shard_map/ppermute | solution.py:475
  154.8 2.8 %collective-permute-done.29.refs_6_ = f32[1,288,128]{2,1,0:T(8,128)S(1)} collective-permute-done((f32[1,288,128]{2,1,0:T(8,128)S(1)}, f32[1,288,128]{2,1,0:T(8,128)S(1)}, u32[]{:S(2)}, u32[]{:S(2)}) %collective-permute-start.29) | collective-permute-done | bytes 147488 | tf_op jit(solution)/shard_map/ppermute | solution.py:475
  157.6 1.6 collective-permute-done.30.refs_7_
  159.2 5.0 %collective-permute-start.31 = (f32[2304,128]{1,0:T(8,128)S(1)}, f32[2304,128]{1,0:T(8,128)S(1)}, u32[]{:S(2)}, u32[]{:S(2)}) collective-permute-start(f32[2304,128]{1,0:T(8,128)S(1)} %bitcast.4), channel_id=1, source_target_pairs={{0,8},{8,0},{1,9},{9,1},{2,10},{10,2},{3,11},{11,3},{4,12},{12,4},... | collective-permute-start | bytes 3538952 | tf_op jit(solution)/shard_map/ppermute | solution.py:455
  164.2 2.5 %shard_map.85 = (f32[8,128,128]{2,1,0:T(8,128)S(1)}, f32[256,256]{1,0:T(8,128)S(1)}) custom-call(s32[1]{0:T(128)} %bitcast.dev, bf16[4,4608,256]{2,1,0:T(8,128)(2,1)S(1)} %get-tuple-element.54.bhi, bf16[4,4608,256]{2,1,0:T(8,128)(2,1)S(1)} %get-tuple-element.55.blo, f32[2304,128]{1,0:T(8,128)S(1)} %bitcast.5), custom_call_target="tpu_custom_call" | custom-call | flops 450000000 | tf_op jit(solution)/shard_map/pallas_call | solution.py:60
  166.7 2.5 %shard_map.86 = (f32[5,128,128]{2,1,0:T(8,128)S(1)}, f32[5,128,128]{2,1,0:T(8,128)S(1)}) custom-call(s32[1]{0:T(128)} %bitcast.dev, bf16[4,4608,256]{2,1,0:T(8,128)(2,1)S(1)} %get-tuple-element.54.bhi, bf16[4,4608,256]{2,1,0:T(8,128)(2,1)S(1)} %get-tuple-element.55.blo, f32[2304,128]{1,0:T(8,128)S(1)} %collective-permute-done.31.v.theirs, ...), custom_call_target="tpu_custom_call" | custom-call | flops 450000000 | tf_op jit(solution)/shard_map/pallas_call | solution.py:60
  170.2 6.3 %collective-permute-done.32.refs_1_.r1 = f32[5,128,128]{2,1,0:T(8,128)S(1)} collective-permute-done((f32[5,128,128]{2,1,0:T(8,128)S(1)}, f32[5,128,128]{2,1,0:T(8,128)S(1)}, u32[]{:S(2)}, u32[]{:S(2)}) %collective-permute-start.32) | collective-permute-done | bytes 327712 | tf_op jit(solution)/shard_map/ppermute | solution.py:475
  176.5 4.8 %collective-permute-done.33.r2 = f32[3,128,128]{2,1,0:T(8,128)S(1)} collective-permute-done((f32[3,128,128]{2,1,0:T(8,128)S(1)}, f32[3,128,128]{2,1,0:T(8,128)S(1)}, u32[]{:S(2)}, u32[]{:S(2)}) %collective-permute-start.33) | collective-permute-done | bytes 196640 | tf_op jit(solution)/shard_map/ppermute | solution.py:475
  181.7 5.0 %collective-permute-done.34.r3 = f32[2,128,128]{2,1,0:T(8,128)S(1)} collective-permute-done((f32[2,128,128]{2,1,0:T(8,128)S(1)}, f32[2,128,128]{2,1,0:T(8,128)S(1)}, u32[]{:S(2)}, u32[]{:S(2)}) %collective-permute-start.34) | collective-permute-done | bytes 131104 | tf_op jit(solution)/shard_map/ppermute | solution.py:475
  187.0 3.6 %collective-permute-start.35 = (f32[2,128,128]{2,1,0:T(8,128)S(1)}, f32[2,128,128]{2,1,0:T(8,128)S(1)}, u32[]{:S(2)}, u32[]{:S(2)}) collective-permute-start(f32[2,128,128]{2,1,0:T(8,128)S(1)} %shard_map.89.own), channel_id=1, source_target_pairs={{0,8},{8,0},{1,9},{9,1},{2,10},{10,2},{3,11},{11,3},{4,12},{12,4},... | collective-permute-start | bytes 393224 | tf_op jit(solution)/shard_map/ppermute | solution.py:455
  191.6 1.4 collective-permute-start.38
  193.7 1.3 collective-permute-start.36
  195.0 2.0 shard_map.91
  198.7 2.4 %collective-permute-start.39 = (f32[128,128]{1,0:T(8,128)S(1)}, f32[128,128]{1,0:T(8,128)S(1)}, u32[]{:S(2)}, u32[]{:S(2)}) collective-permute-start(f32[128,128]{1,0:T(8,128)S(1)} %add_add_fusion.1), channel_id=1, source_target_pairs={{0,1},{1,0},{2,3},{3,2},{4,5},{5,4},{6,7},{7,6},{8,9},{9,8},{10,11... | collective-permute-start | bytes 196616 | tf_op jit(solution)/shard_map/ppermute | solution.py:455
  201.0 1.9 shard_map.92
  203.9 3.4 %collective-permute-start.42 = (f32[128,128]{1,0:T(8,128)S(1)}, f32[128,128]{1,0:T(8,128)S(1)}, u32[]{:S(2)}, u32[]{:S(2)}) collective-permute-start(f32[128,128]{1,0:T(8,128)S(1)} %add_add_fusion.a), channel_id=1, source_target_pairs={{0,4},{4,0},{16,20},{20,16},{1,5},{5,1},{17,21},{21,17},{2,6},{6,2... | collective-permute-start | bytes 196616 | tf_op jit(solution)/shard_map/ppermute | solution.py:455
  207.4 4.2 %finish.1 = (f32[4500,128]{1,0:T(8,128)}, f32[128,128]{1,0:T(8,128)S(1)}) custom-call(s32[1]{0:T(128)} %bitcast.dev, f32[2304,128]{1,0:T(8,128)S(1)} %bitcast.6, f32[2304,128]{1,0:T(8,128)S(1)} %collective-permute-done.31.v.theirs, f32[128,128]{1,0:T(8,128)S(1)} %get-tuple-element.95.g, f32[128,128]{1,0:T(8,128)S(1)} %get-tuple-element.96.w), custom_call_target="tpu_custom_call" | custom-call | flops 630000000 | tf_op jit(solution)/shard_map/finish/pallas_call | solution.py:426
  (96 shorter events, 29.1 us)
Async XLA Ops:
  0.6 25.6 %copy-start = (f32[1024]{0:T(1024)S(1)}, f32[1024]{0:T(1024)}, u32[]{:S(2)}) copy-start(f32[1024]{0:T(1024)} %param.4) | copy-start | bytes 12292
  39.2 4.7 %collective-permute-start = (f32[2,288,128]{2,1,0:T(8,128)S(1)}, f32[2,288,128]{2,1,0:T(8,128)S(1)}, u32[]{:S(2)}, u32[]{:S(2)}) collective-permute-start(f32[2,288,128]{2,1,0:T(8,128)S(1)} %get-tuple-element.59), channel_id=1, source_target_pairs={{0,8},{8,0},{1,9},{9,1},{2,10},{10,2},{3,11},{11,3},{4,12},{12,4},... | collective-permute-start | bytes 884744 | tf_op jit(solution)/shard_map/ppermute | solution.py:455
  44.7 1.7 collective-permute-start.1
  45.2 5.9 %collective-permute-start.3 = (f32[2,288,128]{2,1,0:T(8,128)S(1)}, f32[2,288,128]{2,1,0:T(8,128)S(1)}, u32[]{:S(2)}, u32[]{:S(2)}) collective-permute-start(f32[2,288,128]{2,1,0:T(8,128)S(1)} %shard_map.54), channel_id=1, source_target_pairs={{0,32},{8,24},{16,48},{24,8},{32,0},{40,56},{48,16},{56,40},{64,96... | collective-permute-start | bytes 884744 | tf_op jit(solution)/shard_map/ppermute | solution.py:475
  47.2 3.8 %collective-permute-start.2 = (f32[2,288,128]{2,1,0:T(8,128)S(1)}, f32[2,288,128]{2,1,0:T(8,128)S(1)}, u32[]{:S(2)}, u32[]{:S(2)}) collective-permute-start(f32[2,288,128]{2,1,0:T(8,128)S(1)} %shard_map.59), channel_id=1, source_target_pairs={{0,8},{8,0},{1,9},{9,1},{2,10},{10,2},{3,11},{11,3},{4,12},{12,4},... | collective-permute-start | bytes 884744 | tf_op jit(solution)/shard_map/ppermute | solution.py:455
  49.0 6.4 %collective-permute-start.5 = (f32[2,288,128]{2,1,0:T(8,128)S(1)}, f32[2,288,128]{2,1,0:T(8,128)S(1)}, u32[]{:S(2)}, u32[]{:S(2)}) collective-permute-start(f32[2,288,128]{2,1,0:T(8,128)S(1)} %shard_map.57), channel_id=1, source_target_pairs={{0,32},{8,24},{16,48},{24,8},{32,0},{40,56},{48,16},{56,40},{64,96... | collective-permute-start | bytes 884744 | tf_op jit(solution)/shard_map/ppermute | solution.py:475
  51.9 3.5 %collective-permute-start.4 = (f32[2,288,128]{2,1,0:T(8,128)S(1)}, f32[2,288,128]{2,1,0:T(8,128)S(1)}, u32[]{:S(2)}, u32[]{:S(2)}) collective-permute-start(f32[2,288,128]{2,1,0:T(8,128)S(1)} %shard_map.62), channel_id=1, source_target_pairs={{0,8},{8,0},{1,9},{9,1},{2,10},{10,2},{3,11},{11,3},{4,12},{12,4},... | collective-permute-start | bytes 884744 | tf_op jit(solution)/shard_map/ppermute | solution.py:455
  53.0 6.0 %collective-permute-start.6 = (f32[2,288,128]{2,1,0:T(8,128)S(1)}, f32[2,288,128]{2,1,0:T(8,128)S(1)}, u32[]{:S(2)}, u32[]{:S(2)}) collective-permute-start(f32[2,288,128]{2,1,0:T(8,128)S(1)} %shard_map.60), channel_id=1, source_target_pairs={{0,96},{8,40},{16,112},{24,56},{32,64},{40,8},{48,80},{56,24},{64,... | collective-permute-start | bytes 884744 | tf_op jit(solution)/shard_map/ppermute | solution.py:475
  59.0 6.2 %collective-permute-start.7 = (f32[1,288,128]{2,1,0:T(8,128)S(1)}, f32[1,288,128]{2,1,0:T(8,128)S(1)}, u32[]{:S(2)}, u32[]{:S(2)}) collective-permute-start(f32[1,288,128]{2,1,0:T(8,128)S(1)} %shard_map.63), channel_id=1, source_target_pairs={{0,16},{8,104},{16,0},{24,120},{32,48},{40,72},{48,32},{56,88},{64... | collective-permute-start | bytes 442376 | tf_op jit(solution)/shard_map/ppermute | solution.py:475
  65.3 5.3 %collective-permute-start.8 = (f32[1,288,128]{2,1,0:T(8,128)S(1)}, f32[1,288,128]{2,1,0:T(8,128)S(1)}, u32[]{:S(2)}, u32[]{:S(2)}) collective-permute-start(f32[1,288,128]{2,1,0:T(8,128)S(1)} %shard_map.64.refs_0_), channel_id=1, source_target_pairs={{0,16},{8,104},{16,0},{24,120},{32,48},{40,72},{48,32},{56,88},{64... | collective-permute-start | bytes 442376 | tf_op jit(solution)/shard_map/ppermute | solution.py:475
  68.0 4.3 %collective-permute-start.9 = (f32[1,288,128]{2,1,0:T(8,128)S(1)}, f32[1,288,128]{2,1,0:T(8,128)S(1)}, u32[]{:S(2)}, u32[]{:S(2)}) collective-permute-start(f32[1,288,128]{2,1,0:T(8,128)S(1)} %shard_map.64.refs_0_), channel_id=1, source_target_pairs={{0,96},{8,40},{16,112},{24,56},{32,64},{40,8},{48,80},{56,24},{64,... | collective-permute-start | bytes 442376 | tf_op jit(solution)/shard_map/ppermute | solution.py:475
  70.6 4.0 %collective-permute-start.10 = (f32[1,288,128]{2,1,0:T(8,128)S(1)}, f32[1,288,128]{2,1,0:T(8,128)S(1)}, u32[]{:S(2)}, u32[]{:S(2)}) collective-permute-start(f32[1,288,128]{2,1,0:T(8,128)S(1)} %collective-permute-done.8.refs_1_), channel_id=1, source_target_pairs={{0,96},{8,40},{16,112},{24,56},{32,64},{40,8},{48,80},{56,24},{64,... | collective-permute-start | bytes 442376 | tf_op jit(solution)/shard_map/ppermute | solution.py:475
  70.6 4.3 %collective-permute-start.11 = (f32[1,288,128]{2,1,0:T(8,128)S(1)}, f32[1,288,128]{2,1,0:T(8,128)S(1)}, u32[]{:S(2)}, u32[]{:S(2)}) collective-permute-start(f32[1,288,128]{2,1,0:T(8,128)S(1)} %shard_map.64.refs_0_), channel_id=1, source_target_pairs={{0,32},{8,24},{16,48},{24,8},{32,0},{40,56},{48,16},{56,40},{64,96... | collective-permute-start | bytes 442376 | tf_op jit(solution)/shard_map/ppermute | solution.py:475
  70.9 7.1 %collective-permute-start.12 = (f32[1,288,128]{2,1,0:T(8,128)S(1)}, f32[1,288,128]{2,1,0:T(8,128)S(1)}, u32[]{:S(2)}, u32[]{:S(2)}) collective-permute-start(f32[1,288,128]{2,1,0:T(8,128)S(1)} %collective-permute-done.8.refs_1_), channel_id=1, source_target_pairs={{0,32},{8,24},{16,48},{24,8},{32,0},{40,56},{48,16},{56,40},{64,96... | collective-permute-start | bytes 442376 | tf_op jit(solution)/shard_map/ppermute | solution.py:475
  72.3 5.7 %collective-permute-start.13 = (f32[1,288,128]{2,1,0:T(8,128)S(1)}, f32[1,288,128]{2,1,0:T(8,128)S(1)}, u32[]{:S(2)}, u32[]{:S(2)}) collective-permute-start(f32[1,288,128]{2,1,0:T(8,128)S(1)} %collective-permute-done.9.refs_2_), channel_id=1, source_target_pairs={{0,32},{8,24},{16,48},{24,8},{32,0},{40,56},{48,16},{56,40},{64,96... | collective-permute-start | bytes 442376 | tf_op jit(solution)/shard_map/ppermute | solution.py:475
  74.6 5.0 %collective-permute-start.14 = (f32[1,288,128]{2,1,0:T(8,128)S(1)}, f32[1,288,128]{2,1,0:T(8,128)S(1)}, u32[]{:S(2)}, u32[]{:S(2)}) collective-permute-start(f32[1,288,128]{2,1,0:T(8,128)S(1)} %collective-permute-done.10.refs_3_), channel_id=1, source_target_pairs={{0,32},{8,24},{16,48},{24,8},{32,0},{40,56},{48,16},{56,40},{64,96... | collective-permute-start | bytes 442376 | tf_op jit(solution)/shard_map/ppermute | solution.py:475
  79.7 8.6 %collective-permute-start.15 = (f32[2304,128]{1,0:T(8,128)S(1)}, f32[2304,128]{1,0:T(8,128)S(1)}, u32[]{:S(2)}, u32[]{:S(2)}) collective-permute-start(f32[2304,128]{1,0:T(8,128)S(1)} %bitcast.7), channel_id=1, source_target_pairs={{0,8},{8,0},{1,9},{9,1},{2,10},{10,2},{3,11},{11,3},{4,12},{12,4},... | collective-permute-start | bytes 3538952 | tf_op jit(solution)/shard_map/ppermute | solution.py:455
  119.4 3.8 %collective-permute-start.16 = (f32[2,288,128]{2,1,0:T(8,128)S(1)}, f32[2,288,128]{2,1,0:T(8,128)S(1)}, u32[]{:S(2)}, u32[]{:S(2)}) collective-permute-start(f32[2,288,128]{2,1,0:T(8,128)S(1)} %get-tuple-element.66), channel_id=1, source_target_pairs={{0,8},{8,0},{1,9},{9,1},{2,10},{10,2},{3,11},{11,3},{4,12},{12,4},... | collective-permute-start | bytes 884744 | tf_op jit(solution)/shard_map/ppermute | solution.py:455
  124.1 1.7 collective-permute-start.17
  124.5 5.9 %collective-permute-start.19 = (f32[2,288,128]{2,1,0:T(8,128)S(1)}, f32[2,288,128]{2,1,0:T(8,128)S(1)}, u32[]{:S(2)}, u32[]{:S(2)}) collective-permute-start(f32[2,288,128]{2,1,0:T(8,128)S(1)} %shard_map.71), channel_id=1, source_target_pairs={{0,32},{8,24},{16,48},{24,8},{32,0},{40,56},{48,16},{56,40},{64,96... | collective-permute-start | bytes 884744 | tf_op jit(solution)/shard_map/ppermute | solution.py:475
  126.6 3.8 %collective-permute-start.18 = (f32[2,288,128]{2,1,0:T(8,128)S(1)}, f32[2,288,128]{2,1,0:T(8,128)S(1)}, u32[]{:S(2)}, u32[]{:S(2)}) collective-permute-start(f32[2,288,128]{2,1,0:T(8,128)S(1)} %shard_map.76), channel_id=1, source_target_pairs={{0,8},{8,0},{1,9},{9,1},{2,10},{10,2},{3,11},{11,3},{4,12},{12,4},... | collective-permute-start | bytes 884744 | tf_op jit(solution)/shard_map/ppermute | solution.py:455
  131.3 5.6 %collective-permute-start.21 = (f32[2,288,128]{2,1,0:T(8,128)S(1)}, f32[2,288,128]{2,1,0:T(8,128)S(1)}, u32[]{:S(2)}, u32[]{:S(2)}) collective-permute-start(f32[2,288,128]{2,1,0:T(8,128)S(1)} %shard_map.79), channel_id=1, source_target_pairs={{0,8},{8,0},{1,9},{9,1},{2,10},{10,2},{3,11},{11,3},{4,12},{12,4},... | collective-permute-start | bytes 884744 | tf_op jit(solution)/shard_map/ppermute | solution.py:455
  132.3 6.9 %collective-permute-start.20 = (f32[2,288,128]{2,1,0:T(8,128)S(1)}, f32[2,288,128]{2,1,0:T(8,128)S(1)}, u32[]{:S(2)}, u32[]{:S(2)}) collective-permute-start(f32[2,288,128]{2,1,0:T(8,128)S(1)} %shard_map.77), channel_id=1, source_target_pairs={{0,96},{8,40},{16,112},{24,56},{32,64},{40,8},{48,80},{56,24},{64,... | collective-permute-start | bytes 884744 | tf_op jit(solution)/shard_map/ppermute | solution.py:475
  132.5 6.7 %collective-permute-start.22 = (f32[2,288,128]{2,1,0:T(8,128)S(1)}, f32[2,288,128]{2,1,0:T(8,128)S(1)}, u32[]{:S(2)}, u32[]{:S(2)}) collective-permute-start(f32[2,288,128]{2,1,0:T(8,128)S(1)} %shard_map.74), channel_id=1, source_target_pairs={{0,32},{8,24},{16,48},{24,8},{32,0},{40,56},{48,16},{56,40},{64,96... | collective-permute-start | bytes 884744 | tf_op jit(solution)/shard_map/ppermute | solution.py:475
  139.3 5.3 %collective-permute-start.23 = (f32[1,288,128]{2,1,0:T(8,128)S(1)}, f32[1,288,128]{2,1,0:T(8,128)S(1)}, u32[]{:S(2)}, u32[]{:S(2)}) collective-permute-start(f32[1,288,128]{2,1,0:T(8,128)S(1)} %shard_map.81), channel_id=1, source_target_pairs={{0,16},{8,104},{16,0},{24,120},{32,48},{40,72},{48,32},{56,88},{64... | collective-permute-start | bytes 442376 | tf_op jit(solution)/shard_map/ppermute | solution.py:475
  144.8 5.3 %collective-permute-start.24 = (f32[1,288,128]{2,1,0:T(8,128)S(1)}, f32[1,288,128]{2,1,0:T(8,128)S(1)}, u32[]{:S(2)}, u32[]{:S(2)}) collective-permute-start(f32[1,288,128]{2,1,0:T(8,128)S(1)} %shard_map.83.refs_0_), channel_id=1, source_target_pairs={{0,16},{8,104},{16,0},{24,120},{32,48},{40,72},{48,32},{56,88},{64... | collective-permute-start | bytes 442376 | tf_op jit(solution)/shard_map/ppermute | solution.py:475
  146.2 5.4 %collective-permute-start.25 = (f32[1,288,128]{2,1,0:T(8,128)S(1)}, f32[1,288,128]{2,1,0:T(8,128)S(1)}, u32[]{:S(2)}, u32[]{:S(2)}) collective-permute-start(f32[1,288,128]{2,1,0:T(8,128)S(1)} %shard_map.83.refs_0_), channel_id=1, source_target_pairs={{0,96},{8,40},{16,112},{24,56},{32,64},{40,8},{48,80},{56,24},{64,... | collective-permute-start | bytes 442376 | tf_op jit(solution)/shard_map/ppermute | solution.py:475
  150.1 4.0 %collective-permute-start.26 = (f32[1,288,128]{2,1,0:T(8,128)S(1)}, f32[1,288,128]{2,1,0:T(8,128)S(1)}, u32[]{:S(2)}, u32[]{:S(2)}) collective-permute-start(f32[1,288,128]{2,1,0:T(8,128)S(1)} %collective-permute-done.24.refs_1_), channel_id=1, source_target_pairs={{0,96},{8,40},{16,112},{24,56},{32,64},{40,8},{48,80},{56,24},{64,... | collective-permute-start | bytes 442376 | tf_op jit(solution)/shard_map/ppermute | solution.py:475
  150.1 4.6 %collective-permute-start.27 = (f32[1,288,128]{2,1,0:T(8,128)S(1)}, f32[1,288,128]{2,1,0:T(8,128)S(1)}, u32[]{:S(2)}, u32[]{:S(2)}) collective-permute-start(f32[1,288,128]{2,1,0:T(8,128)S(1)} %shard_map.83.refs_0_), channel_id=1, source_target_pairs={{0,32},{8,24},{16,48},{24,8},{32,0},{40,56},{48,16},{56,40},{64,96... | collective-permute-start | bytes 442376 | tf_op jit(solution)/shard_map/ppermute | solution.py:475
  150.5 7.1 %collective-permute-start.28 = (f32[1,288,128]{2,1,0:T(8,128)S(1)}, f32[1,288,128]{2,1,0:T(8,128)S(1)}, u32[]{:S(2)}, u32[]{:S(2)}) collective-permute-start(f32[1,288,128]{2,1,0:T(8,128)S(1)} %collective-permute-done.24.refs_1_), channel_id=1, source_target_pairs={{0,32},{8,24},{16,48},{24,8},{32,0},{40,56},{48,16},{56,40},{64,96... | collective-permute-start | bytes 442376 | tf_op jit(solution)/shard_map/ppermute | solution.py:475
  151.6 6.0 %collective-permute-start.29 = (f32[1,288,128]{2,1,0:T(8,128)S(1)}, f32[1,288,128]{2,1,0:T(8,128)S(1)}, u32[]{:S(2)}, u32[]{:S(2)}) collective-permute-start(f32[1,288,128]{2,1,0:T(8,128)S(1)} %collective-permute-done.25.refs_2_), channel_id=1, source_target_pairs={{0,32},{8,24},{16,48},{24,8},{32,0},{40,56},{48,16},{56,40},{64,96... | collective-permute-start | bytes 442376 | tf_op jit(solution)/shard_map/ppermute | solution.py:475
  154.1 5.0 %collective-permute-start.30 = (f32[1,288,128]{2,1,0:T(8,128)S(1)}, f32[1,288,128]{2,1,0:T(8,128)S(1)}, u32[]{:S(2)}, u32[]{:S(2)}) collective-permute-start(f32[1,288,128]{2,1,0:T(8,128)S(1)} %collective-permute-done.26.refs_3_), channel_id=1, source_target_pairs={{0,32},{8,24},{16,48},{24,8},{32,0},{40,56},{48,16},{56,40},{64,96... | collective-permute-start | bytes 442376 | tf_op jit(solution)/shard_map/ppermute | solution.py:475
  159.2 7.4 %collective-permute-start.31 = (f32[2304,128]{1,0:T(8,128)S(1)}, f32[2304,128]{1,0:T(8,128)S(1)}, u32[]{:S(2)}, u32[]{:S(2)}) collective-permute-start(f32[2304,128]{1,0:T(8,128)S(1)} %bitcast.4), channel_id=1, source_target_pairs={{0,8},{8,0},{1,9},{9,1},{2,10},{10,2},{3,11},{11,3},{4,12},{12,4},... | collective-permute-start | bytes 3538952 | tf_op jit(solution)/shard_map/ppermute | solution.py:455
  169.2 7.2 %collective-permute-start.32 = (f32[5,128,128]{2,1,0:T(8,128)S(1)}, f32[5,128,128]{2,1,0:T(8,128)S(1)}, u32[]{:S(2)}, u32[]{:S(2)}) collective-permute-start(f32[5,128,128]{2,1,0:T(8,128)S(1)} %get-tuple-element.83), channel_id=1, source_target_pairs={{0,1},{1,0},{2,3},{3,2},{4,5},{5,4},{6,7},{7,6},{8,11},{9,10},{10,... | collective-permute-start | bytes 983048 | tf_op jit(solution)/shard_map/ppermute | solution.py:475
  176.4 4.9 %collective-permute-start.33 = (f32[3,128,128]{2,1,0:T(8,128)S(1)}, f32[3,128,128]{2,1,0:T(8,128)S(1)}, u32[]{:S(2)}, u32[]{:S(2)}) collective-permute-start(f32[3,128,128]{2,1,0:T(8,128)S(1)} %shard_map.87), channel_id=1, source_target_pairs={{0,3},{1,2},{2,1},{3,0},{4,7},{5,6},{6,5},{7,4},{8,9},{9,8},{10,11... | collective-permute-start | bytes 589832 | tf_op jit(solution)/shard_map/ppermute | solution.py:475
  181.4 5.4 %collective-permute-start.34 = (f32[2,128,128]{2,1,0:T(8,128)S(1)}, f32[2,128,128]{2,1,0:T(8,128)S(1)}, u32[]{:S(2)}, u32[]{:S(2)}) collective-permute-start(f32[2,128,128]{2,1,0:T(8,128)S(1)} %shard_map.88), channel_id=1, source_target_pairs={{0,4},{1,5},{2,6},{3,7},{4,0},{5,1},{6,2},{7,3},{8,12},{9,13},{10,... | collective-permute-start | bytes 393224 | tf_op jit(solution)/shard_map/ppermute | solution.py:475
  187.0 4.6 %collective-permute-start.35 = (f32[2,128,128]{2,1,0:T(8,128)S(1)}, f32[2,128,128]{2,1,0:T(8,128)S(1)}, u32[]{:S(2)}, u32[]{:S(2)}) collective-permute-start(f32[2,128,128]{2,1,0:T(8,128)S(1)} %shard_map.89.own), channel_id=1, source_target_pairs={{0,8},{8,0},{1,9},{9,1},{2,10},{10,2},{3,11},{11,3},{4,12},{12,4},... | collective-permute-start | bytes 393224 | tf_op jit(solution)/shard_map/ppermute | solution.py:455
  191.6 5.3 %collective-permute-start.38 = (f32[128,128]{1,0:T(8,128)S(1)}, f32[128,128]{1,0:T(8,128)S(1)}, u32[]{:S(2)}, u32[]{:S(2)}) collective-permute-start(f32[128,128]{1,0:T(8,128)S(1)} %get-tuple-element.84), channel_id=1, source_target_pairs={{0,96},{32,64},{64,32},{96,0},{1,97},{33,65},{65,33},{97,1},{2,98}... | collective-permute-start | bytes 196616 | tf_op jit(solution)/shard_map/ppermute | solution.py:455
  193.1 4.6 %collective-permute-start.37 = (f32[128,128]{1,0:T(8,128)S(1)}, f32[128,128]{1,0:T(8,128)S(1)}, u32[]{:S(2)}, u32[]{:S(2)}) collective-permute-start(f32[128,128]{1,0:T(8,128)S(1)} %get-tuple-element.84), channel_id=1, source_target_pairs={{0,64},{32,96},{64,0},{96,32},{1,65},{33,97},{65,1},{97,33},{2,66}... | collective-permute-start | bytes 196616 | tf_op jit(solution)/shard_map/ppermute | solution.py:455
  193.7 4.0 %collective-permute-start.36 = (f32[128,128]{1,0:T(8,128)S(1)}, f32[128,128]{1,0:T(8,128)S(1)}, u32[]{:S(2)}, u32[]{:S(2)}) collective-permute-start(f32[128,128]{1,0:T(8,128)S(1)} %get-tuple-element.84), channel_id=1, source_target_pairs={{0,32},{32,0},{64,96},{96,64},{1,33},{33,1},{65,97},{97,65},{2,34}... | collective-permute-start | bytes 196616 | tf_op jit(solution)/shard_map/ppermute | solution.py:455
  197.7 5.3 %collective-permute-start.41 = (f32[128,128]{1,0:T(8,128)S(1)}, f32[128,128]{1,0:T(8,128)S(1)}, u32[]{:S(2)}, u32[]{:S(2)}) collective-permute-start(f32[128,128]{1,0:T(8,128)S(1)} %add_add_fusion.1), channel_id=1, source_target_pairs={{0,3},{1,2},{2,1},{3,0},{4,7},{5,6},{6,5},{7,4},{8,11},{9,10},{10,... | collective-permute-start | bytes 196616 | tf_op jit(solution)/shard_map/ppermute | solution.py:455
  198.7 4.6 %collective-permute-start.40 = (f32[128,128]{1,0:T(8,128)S(1)}, f32[128,128]{1,0:T(8,128)S(1)}, u32[]{:S(2)}, u32[]{:S(2)}) collective-permute-start(f32[128,128]{1,0:T(8,128)S(1)} %add_add_fusion.1), channel_id=1, source_target_pairs={{0,2},{1,3},{2,0},{3,1},{4,6},{5,7},{6,4},{7,5},{8,10},{9,11},{10,... | collective-permute-start | bytes 196616 | tf_op jit(solution)/shard_map/ppermute | solution.py:455
  198.7 4.7 %collective-permute-start.39 = (f32[128,128]{1,0:T(8,128)S(1)}, f32[128,128]{1,0:T(8,128)S(1)}, u32[]{:S(2)}, u32[]{:S(2)}) collective-permute-start(f32[128,128]{1,0:T(8,128)S(1)} %add_add_fusion.1), channel_id=1, source_target_pairs={{0,1},{1,0},{2,3},{3,2},{4,5},{5,4},{6,7},{7,6},{8,9},{9,8},{10,11... | collective-permute-start | bytes 196616 | tf_op jit(solution)/shard_map/ppermute | solution.py:455
  203.4 8.2 %collective-permute-start.44 = (f32[128,128]{1,0:T(8,128)S(1)}, f32[128,128]{1,0:T(8,128)S(1)}, u32[]{:S(2)}, u32[]{:S(2)}) collective-permute-start(f32[128,128]{1,0:T(8,128)S(1)} %add_add_fusion.a), channel_id=1, source_target_pairs={{0,20},{4,16},{16,4},{20,0},{1,21},{5,17},{17,5},{21,1},{2,22},{6,... | collective-permute-start | bytes 196616 | tf_op jit(solution)/shard_map/ppermute | solution.py:455
  203.6 8.0 %collective-permute-start.43 = (f32[128,128]{1,0:T(8,128)S(1)}, f32[128,128]{1,0:T(8,128)S(1)}, u32[]{:S(2)}, u32[]{:S(2)}) collective-permute-start(f32[128,128]{1,0:T(8,128)S(1)} %add_add_fusion.a), channel_id=1, source_target_pairs={{0,16},{4,20},{16,0},{20,4},{1,17},{5,21},{17,1},{21,5},{2,18},{6,... | collective-permute-start | bytes 196616 | tf_op jit(solution)/shard_map/ppermute | solution.py:455
  203.9 7.7 %collective-permute-start.42 = (f32[128,128]{1,0:T(8,128)S(1)}, f32[128,128]{1,0:T(8,128)S(1)}, u32[]{:S(2)}, u32[]{:S(2)}) collective-permute-start(f32[128,128]{1,0:T(8,128)S(1)} %add_add_fusion.a), channel_id=1, source_target_pairs={{0,4},{4,0},{16,20},{20,16},{1,5},{5,1},{17,21},{21,17},{2,6},{6,2... | collective-permute-start | bytes 196616 | tf_op jit(solution)/shard_map/ppermute | solution.py:455

commit v2 on v1

--- a/solution.py
+++ b/solution.py
@@ -107,7 +107,7 @@
             for c in copies(i):
                 c.start()
 
-        def chunk(slot, row0, first):
+        def chunk(slot, row0):
             vt = transposed_halves(vbuf[slot])
             for n in range(4):
                 hi, lo = split(bbuf[slot, :, 256 * n : 256 * n + 256])
@@ -115,21 +115,18 @@
                 blo[n, pl.ds(row0, CHUNK), :] = lo
                 part = fold(dot(vt, hi, 1, 0)) + dot(vt[0:K], lo, 1, 0)
                 for t in range(2):
-                    value = part[:, 128 * t : 128 * t + 128]
-                    out[2 * n + t] = value if first else out[2 * n + t] + value
-
-        for c in copies(0):
-            c.wait()
-        chunk(0, 0, True)
+                    out[2 * n + t] += part[:, 128 * t : 128 * t + 128]
+
+        out[...] = jnp.zeros(out.shape, F32)
 
         def middle(i, carry):
             rows = pl.ds(pl.multiple_of(i * CHUNK, CHUNK), CHUNK)
             pltpu.make_async_copy(b_hbm.at[rows], bbuf.at[i], sems.at[0, i]).wait()
             pltpu.make_async_copy(v_hbm.at[rows], vbuf.at[i], sems.at[1, i]).wait()
-            chunk(i, pl.multiple_of(i * CHUNK, CHUNK), False)
+            chunk(i, pl.multiple_of(i * CHUNK, CHUNK))
             return carry
 
-        lax.fori_loop(1, CHUNKS - 1, middle, 0)
+        lax.fori_loop(0, CHUNKS - 1, middle, 0)
         for c in copies(CHUNKS - 1):
             c.wait()
         whole = TAIL // 8 * 8
@@ -137,7 +134,7 @@
         vbuf[0, whole:, :] = jnp.zeros((CHUNK - whole, K), F32)
         bbuf[0, 0:TAIL, :] = btail[...]
         vbuf[0, 0:TAIL, :] = vtail[...]
-        chunk(0, CHUNK * (CHUNKS - 1), False)
+        chunk(0, CHUNK * (CHUNKS - 1))
 
     halves = ((4, ROWS, 256), BF16)
     coeffs = pltpu.with_memory_space_constraint(coeffs, pltpu.HBM)
@@ -188,11 +185,11 @@
             g = gacc[...] + gacc0[...]
             gram = (g[0:K, 0:K] + g[K:, K:]) + (g[0:K, K:] + g[K:, 0:K])
             if by_position:
-                for t, out in enumerate(outs):
-                    for p in range(4):
-                        at = piece_at(AUX_LINKS, core_of(dev), aux_of(dev), 4 - 4 * t + p)
-                        out[p] = acc[at]
-                    out[4] = gram
+                for out, places in zip(outs, ((6, 7), (4, 5), (0, 1, 2, 3))):
+                    for t, p in enumerate(places):
+                        out[t] = acc[piece_at(AUX_LINKS, core_of(dev), aux_of(dev), p)]
+                outs[0][2] = gram
+                outs[2][4] = gram
             else:
                 for j in range(CHIPS):
                     outs[0][j, 0:K, :] = acc[j]
@@ -204,7 +201,9 @@
         return kernel_call(body, [acc, gacc], [dev], [], [bhi, blo, v], us=3.0)
     return kernel_call(
         body,
-        [((5, K, K), F32)] * 2 if by_position else [((CHIPS, K + GRAM_J, PAIRS_J), F32)],
+        [((n, K, K), F32) for n in (3, 2, 5)]
+        if by_position
+        else [((CHIPS, K + GRAM_J, PAIRS_J), F32)],
         [dev],
         [],
         [bhi, blo, v, *so_far],
@@ -230,22 +229,29 @@
     return kernel_call(body, [(parts.shape, F32)], [dev], [], [parts, gaps])[0]
 
 
-def reduce_aux(dev, send, keep, gaps):
-    def last_step(k, r1, r2, out):
-        out[0] = (k[1] + r1[1]) + r2[1]
-        out[1] = (k[4] + r1[4]) + r2[2]
-
-    def finish_sum(dev, k, r1, r2, r3, gaps, out):
-        own = ((k[0] + r1[0]) + r2[0]) + r3[0]
+def reduce_aux(dev, early, late, keep, gaps):
+    def last_step(k, ra, rb, r2, out):
+        out[0] = (k[1] + rb[1]) + r2[1]
+        out[1] = (k[4] + ra[2]) + r2[2]
+
+    def finish_sum(dev, k, ra, rb, r2, r3, gaps, out):
+        own = ((k[0] + rb[0]) + r2[0]) + r3[0]
         out[0] = dot(own * weights_of(dev, gaps), own, 1, 1, HIGHEST)
-        out[1] = ((k[4] + r1[4]) + r2[2]) + r3[1]
-
-    two = ((2, K, K), F32)
-    r1 = cross(send, 0, AUX_LINKS)
-    r2 = cross(add_slots(2, 3, keep, r1), 1, AUX_LINKS)
-    (send,) = kernel_call(last_step, [two], [], [], [keep, r1, r2])
+        out[1] = ((k[4] + ra[2]) + r2[2]) + r3[1]
+
+    def second_step(k, ra, out):
+        out[...] = k[2:5] + ra[...]
+
+    def pieces(n):
+        return [((n, K, K), F32)]
+
+    ra = cross(early, 0, AUX_LINKS)
+    rb = cross(late, 0, AUX_LINKS)
+    (send,) = kernel_call(second_step, pieces(3), [], [], [keep, ra])
+    r2 = cross(send, 1, AUX_LINKS)
+    (send,) = kernel_call(last_step, pieces(2), [], [], [keep, ra, rb, r2])
     r3 = cross(send, 2, AUX_LINKS)
-    return kernel_call(finish_sum, [two], [dev], [], [keep, r1, r2, r3, gaps])[0]
+    return kernel_call(finish_sum, pieces(2), [dev], [], [keep, ra, rb, r2, r3, gaps])[0]
 
 
 def add_over_cores(dev, both):
@@ -297,6 +303,13 @@
 
     shape = (count, *parts[0].shape[1:])
     return kernel_call(body, [(shape, F32)], [], [], list(parts))[0]
+
+
+def add_last(own, got, r1, r2):
+    def body(own, got, r1, r2, out):
+        out[0] = ((own[1] + got[1]) + r1[1]) + r2[0]
+
+    return kernel_call(body, [((1, PIECE, K), F32)], [], [], [own, got, r1, r2])[0]
 
 
 def sum_rows(parts, inverse):
@@ -493,18 +506,23 @@
         own, got = apply_pair(first)
         if first == 0:
             break
-        value = add_slots(0, 2, own, got, *(steps[:1] if first == 2 else ()))
-        steps.append(cross(value, 1 if first == 2 else 0))
+        if first > 2:
+            value = add_slots(0, 2, own, got)
+            steps.append(cross(value, 0))
+        else:
+            for slot in (1, 0):
+                value = add_slots(slot, 1, own, got, steps[0])
+                steps.append(cross(value, 1))
         value, rhs = lax.optimization_barrier((value, rhs))
-    _, r1, r2 = steps
+    _, r1, r2, r2_own = steps
     inverse = None
     if eliminating:
         r2, own, got = lax.optimization_barrier((r2, own, got))
-        r2, state = in_between(r2, [scaled], (0, 64))
-    r3 = cross(add_slots(1, 1, own, got, r1, r2), 2)
+        r2, state = in_between(r2, [scaled], (0, 40))
+    r3 = cross(add_last(own, got, r1, r2), 2)
     if eliminating:
-        r3, (inverse,) = in_between(r3, state, (64, 128))
-    return sum_rows([own, got, r1, r2, r3], inverse)
+        r3, (inverse,) = in_between(r3, state, (40, 128))
+    return sum_rows([own, got, r1, r2_own, r3], inverse)
 
 
 def gather_rows(dev, own):
@@ -532,8 +550,8 @@
         mine = gather_rows(dev, reduce_rows(dev, bhi, blo, scaled, step == 1))
         theirs = exchange(mine, "c", 1)
         so_far = project_half(dev, bhi, blo, mine, None)
-        parts, *kept = project_half(dev, bhi, blo, theirs, so_far, step == 1)
-    total, gram = add_over_cores(dev, reduce_aux(dev, parts, *kept, gaps))
+        parts, *rest = project_half(dev, bhi, blo, theirs, so_far, step == 1)
+    total, gram = add_over_cores(dev, reduce_aux(dev, parts, *rest, gaps))
     state = [gram]
     for axis, cut in (("z", (0, 40)), ("y", (40, 84)), (("xl", "xh"), None)):
         got = []

time: 216 us -> 215 us (level)
  waiting for transfers between devices: 52.8 us -> 48.8 us
  starting transfers between devices: 54.5 us -> 57.4 us
    ppermute x25 -> x28, waiting for transfers between devices: 49.7 us -> 45.7 us  [cross(): return lax.ppermute(value, axes, pairs)]
    ppermute x25 -> x28, starting transfers between devices: 17.9 us -> 21 us  [cross(): return lax.ppermute(value, axes, pairs)]
    pallas_call x44 -> x46, Pallas kernels: 42.4 us -> 42.4 us  [kernel_call(): pl.pallas_call(body, out_shape=[pltpu.VMEM(s, d) for s, d in outs], in_sp...]
  transfers between devices with their start and end apart: 45 -> 48, of which waited for: 26 -> 26; matrix products, arithmetic and copies ran while one was open for 0% -> 0% of each run, Pallas kernels for 13% -> 13%
where the time goes in v2:
time: 215 us; the launch traced here: 212 us
  starting transfers between devices  57.4 us (27%)
  blocking collectives  57.1 us (27%)
  waiting for transfers between devices  48.8 us (23%)
  Pallas kernels  46.6 us (22%)
    all_to_all x4, blocking collectives, to_each(): return lax.all_to_all(value, axes, split_axis=0, concat_axis=0, tiled=True)  57.1 us
    ppermute x28, waiting for transfers between devices, cross(): return lax.ppermute(value, axes, pairs)  45.7 us
    pallas_call x46, Pallas kernels, kernel_call(): pl.pallas_call(body, out_shape=[pltpu.VMEM(s, d) for s, d in outs], in_sp...  42.4 us
    ppermute x20, starting transfers between devices, exchange(): return lax.ppermute(value, axis, [(i, i ^ mask) for i in range(n)])  36.4 us
    ppermute x28, starting transfers between devices, cross(): return lax.ppermute(value, axes, pairs)  21 us
  transfers between devices with their start and end apart: 48, of which 26 were waited for; matrix products, arithmetic and copies ran while one was open for 0% of the time, Pallas kernels for 13%

profile of v2, /device:TPU:1, one launch (start us, length us, event | category | flops | bytes accessed | tf_op | source)
XLA Modules:
  0.0 211.6 jit_solution(3448053276874983578)
XLA Ops:
  0.7 8.3 %shard_map.50 = (bf16[4,4608,256]{2,1,0:T(8,128)(2,1)S(1)}, bf16[4,4608,256]{2,1,0:T(8,128)(2,1)S(1)}, f32[8,128,128]{2,1,0:T(8,128)S(1)}) custom-call(f32[4500,1024]{1,0:T(8,128)} %b_hbm.1, f32[4500,128]{1,0:T(8,128)} %v_hbm), custom_call_target="tpu_custom_call" | custom-call | flops 1200000000 | tf_op jit(solution)/shard_map/pallas_call | solution.py:60
  8.9 17.3 %all_to_all.20.p = f32[8,128,128]{2,1,0:T(8,128)S(1)} all-to-all(f32[8,128,128]{2,1,0:T(8,128)S(1)} %get-tuple-element.57), channel_id=1, replica_groups=mesh['z'=4,'xl'=2,'c'=2,'xh'=2,'y'=4] {'xh','y'}, dimensions={0} | all-to-all | bytes 1048576 | tf_op jit(solution)/shard_map/all_to_all | solution.py:472
  26.3 12.1 %all_to_all.21.s = f32[8,128,128]{2,1,0:T(8,128)S(1)} all-to-all(f32[8,128,128]{2,1,0:T(8,128)S(1)} %shard_map.51), channel_id=1, replica_groups=mesh['z'=4,'xl'=2,'c'=2,'xh'=2,'y'=4] {'xh','y'}, dimensions={0} | all-to-all | bytes 1048576 | tf_op jit(solution)/shard_map/all_to_all | solution.py:472
  39.2 3.5 %collective-permute-start = (f32[2,288,128]{2,1,0:T(8,128)S(1)}, f32[2,288,128]{2,1,0:T(8,128)S(1)}, u32[]{:S(2)}, u32[]{:S(2)}) collective-permute-start(f32[2,288,128]{2,1,0:T(8,128)S(1)} %get-tuple-element.60), channel_id=1, source_target_pairs={{0,8},{8,0},{1,9},{9,1},{2,10},{10,2},{3,11},{11,3},{4,12},{12,4},... | collective-permute-start | bytes 884744 | tf_op jit(solution)/shard_map/ppermute | solution.py:468
  47.2 1.7 collective-permute-start.2
  53.0 1.7 collective-permute-start.7
  55.6 1.6 collective-permute-done.7.r2
  57.3 3.7 %collective-permute-start.8 = (f32[1,288,128]{2,1,0:T(8,128)S(1)}, f32[1,288,128]{2,1,0:T(8,128)S(1)}, u32[]{:S(2)}, u32[]{:S(2)}) collective-permute-start(f32[1,288,128]{2,1,0:T(8,128)S(1)} %shard_map.64), channel_id=1, source_target_pairs={{0,16},{8,104},{16,0},{24,120},{32,48},{40,72},{48,32},{56,88},{64... | collective-permute-start | bytes 442376 | tf_op jit(solution)/shard_map/ppermute | solution.py:488
  60.9 3.4 %collective-permute-done.8.refs_4_ = f32[1,288,128]{2,1,0:T(8,128)S(1)} collective-permute-done((f32[1,288,128]{2,1,0:T(8,128)S(1)}, f32[1,288,128]{2,1,0:T(8,128)S(1)}, u32[]{:S(2)}, u32[]{:S(2)}) %collective-permute-start.8) | collective-permute-done | bytes 147488 | tf_op jit(solution)/shard_map/ppermute | solution.py:488
  64.4 1.9 collective-permute-start.9
  66.3 3.4 %collective-permute-done.9.refs_1_ = f32[1,288,128]{2,1,0:T(8,128)S(1)} collective-permute-done((f32[1,288,128]{2,1,0:T(8,128)S(1)}, f32[1,288,128]{2,1,0:T(8,128)S(1)}, u32[]{:S(2)}, u32[]{:S(2)}) %collective-permute-start.9) | collective-permute-done | bytes 147488 | tf_op jit(solution)/shard_map/ppermute | solution.py:488
  70.0 1.1 collective-permute-start.13
  71.5 2.2 %collective-permute-done.11.refs_3_ = f32[1,288,128]{2,1,0:T(8,128)S(1)} collective-permute-done((f32[1,288,128]{2,1,0:T(8,128)S(1)}, f32[1,288,128]{2,1,0:T(8,128)S(1)}, u32[]{:S(2)}, u32[]{:S(2)}) %collective-permute-start.11) | collective-permute-done | bytes 147488 | tf_op jit(solution)/shard_map/ppermute | solution.py:488
  74.0 2.8 %collective-permute-done.14.refs_6_ = f32[1,288,128]{2,1,0:T(8,128)S(1)} collective-permute-done((f32[1,288,128]{2,1,0:T(8,128)S(1)}, f32[1,288,128]{2,1,0:T(8,128)S(1)}, u32[]{:S(2)}, u32[]{:S(2)}) %collective-permute-start.14) | collective-permute-done | bytes 147488 | tf_op jit(solution)/shard_map/ppermute | solution.py:488
  76.8 1.9 collective-permute-done.15.refs_7_
  78.8 5.4 %collective-permute-start.16 = (f32[2304,128]{1,0:T(8,128)S(1)}, f32[2304,128]{1,0:T(8,128)S(1)}, u32[]{:S(2)}, u32[]{:S(2)}) collective-permute-start(f32[2304,128]{1,0:T(8,128)S(1)} %bitcast.7), channel_id=1, source_target_pairs={{0,8},{8,0},{1,9},{9,1},{2,10},{10,2},{3,11},{11,3},{4,12},{12,4},... | collective-permute-start | bytes 3538952 | tf_op jit(solution)/shard_map/ppermute | solution.py:468
  84.2 2.5 %shard_map.67 = (f32[8,128,128]{2,1,0:T(8,128)S(1)}, f32[256,256]{1,0:T(8,128)S(1)}) custom-call(s32[1]{0:T(128)} %bitcast.dev, bf16[4,4608,256]{2,1,0:T(8,128)(2,1)S(1)} %get-tuple-element.55.bhi, bf16[4,4608,256]{2,1,0:T(8,128)(2,1)S(1)} %get-tuple-element.56.blo, f32[2304,128]{1,0:T(8,128)S(1)} %bitcast.8), custom_call_target="tpu_custom_call" | custom-call | flops 450000000 | tf_op jit(solution)/shard_map/pallas_call | solution.py:60
  86.7 2.5 %shard_map.68 = f32[8,144,128]{2,1,0:T(8,128)S(1)} custom-call(s32[1]{0:T(128)} %bitcast.dev, bf16[4,4608,256]{2,1,0:T(8,128)(2,1)S(1)} %get-tuple-element.55.bhi, bf16[4,4608,256]{2,1,0:T(8,128)(2,1)S(1)} %get-tuple-element.56.blo, f32[2304,128]{1,0:T(8,128)S(1)} %collective-permute-done.16.v, f32[8,128,128]{2,1,0:T(8,128)S(1)} %get-tuple-element.64.rest_0_, ...), custom_call_target="tpu_custom_call" | custom-call | flops 450000000 | tf_op jit(solution)/shard_map/pallas_call | solution.py:60
  89.2 14.1 %all_to_all.22.p = f32[8,144,128]{2,1,0:T(8,128)S(1)} all-to-all(f32[8,144,128]{2,1,0:T(8,128)S(1)} %shard_map.68), channel_id=1, replica_groups=mesh['z'=4,'xl'=2,'c'=2,'xh'=2,'y'=4] {'xh','y'}, dimensions={0} | all-to-all | bytes 1179648 | tf_op jit(solution)/shard_map/all_to_all | solution.py:472
  103.4 13.6 %all_to_all.23.s.refs_0_ = f32[8,144,128]{2,1,0:T(8,128)S(1)} all-to-all(f32[8,144,128]{2,1,0:T(8,128)S(1)} %shard_map.69), channel_id=1, replica_groups=mesh['z'=4,'xl'=2,'c'=2,'xh'=2,'y'=4] {'xh','y'}, dimensions={0} | all-to-all | bytes 1179648 | tf_op jit(solution)/shard_map/all_to_all | solution.py:472
  117.8 2.6 %collective-permute-start.17 = (f32[2,288,128]{2,1,0:T(8,128)S(1)}, f32[2,288,128]{2,1,0:T(8,128)S(1)}, u32[]{:S(2)}, u32[]{:S(2)}) collective-permute-start(f32[2,288,128]{2,1,0:T(8,128)S(1)} %get-tuple-element.67), channel_id=1, source_target_pairs={{0,8},{8,0},{1,9},{9,1},{2,10},{10,2},{3,11},{11,3},{4,12},{12,4},... | collective-permute-start | bytes 884744 | tf_op jit(solution)/shard_map/ppermute | solution.py:468
  126.3 2.5 %collective-permute-done.20.refs_2_ = f32[2,288,128]{2,1,0:T(8,128)S(1)} collective-permute-done((f32[2,288,128]{2,1,0:T(8,128)S(1)}, f32[2,288,128]{2,1,0:T(8,128)S(1)}, u32[]{:S(2)}, u32[]{:S(2)}) %collective-permute-start.20) | collective-permute-done | bytes 294944 | tf_op jit(solution)/shard_map/ppermute | solution.py:488
  131.4 2.0 shard_map.82
  134.2 2.8 %collective-permute-done.21.r2 = f32[1,288,128]{2,1,0:T(8,128)S(1)} collective-permute-done((f32[1,288,128]{2,1,0:T(8,128)S(1)}, f32[1,288,128]{2,1,0:T(8,128)S(1)}, u32[]{:S(2)}, u32[]{:S(2)}) %collective-permute-start.21) | collective-permute-done | bytes 147488 | tf_op jit(solution)/shard_map/ppermute | solution.py:488
  137.0 1.4 collective-permute-start.25
  138.4 3.7 %shard_map.84.refs_5_ = f32[128,128]{1,0:T(8,128)S(1)} custom-call(f32[128,128]{1,0:T(8,128)S(1)} %get-tuple-element.77.refs_0_, f32[128,128]{1,0:T(8,128)S(1)} %get-tuple-element.78.refs_1_), custom_call_target="tpu_custom_call" | custom-call | flops 660000000 | tf_op jit(solution)/shard_map/pallas_call | solution.py:60
  143.0 1.4 collective-permute-start.26
  144.7 3.6 %collective-permute-done.26.refs_1_ = f32[1,288,128]{2,1,0:T(8,128)S(1)} collective-permute-done((f32[1,288,128]{2,1,0:T(8,128)S(1)}, f32[1,288,128]{2,1,0:T(8,128)S(1)}, u32[]{:S(2)}, u32[]{:S(2)}) %collective-permute-start.26) | collective-permute-done | bytes 147488 | tf_op jit(solution)/shard_map/ppermute | solution.py:488
  148.3 1.3 collective-permute-start.29
  149.7 1.3 collective-permute-start.31
  151.0 1.6 collective-permute-done.28.refs_3_
  152.6 1.3 collective-permute-start.32
  153.8 2.0 collective-permute-done.31.refs_6_
  155.8 1.9 collective-permute-done.32.refs_7_
  157.7 6.0 %collective-permute-start.33 = (f32[2304,128]{1,0:T(8,128)S(1)}, f32[2304,128]{1,0:T(8,128)S(1)}, u32[]{:S(2)}, u32[]{:S(2)}) collective-permute-start(f32[2304,128]{1,0:T(8,128)S(1)} %bitcast.4), channel_id=1, source_target_pairs={{0,8},{8,0},{1,9},{9,1},{2,10},{10,2},{3,11},{11,3},{4,12},{12,4},... | collective-permute-start | bytes 3538952 | tf_op jit(solution)/shard_map/ppermute | solution.py:468
  163.8 2.5 %shard_map.87 = (f32[8,128,128]{2,1,0:T(8,128)S(1)}, f32[256,256]{1,0:T(8,128)S(1)}) custom-call(s32[1]{0:T(128)} %bitcast.dev, bf16[4,4608,256]{2,1,0:T(8,128)(2,1)S(1)} %get-tuple-element.55.bhi, bf16[4,4608,256]{2,1,0:T(8,128)(2,1)S(1)} %get-tuple-element.56.blo, f32[2304,128]{1,0:T(8,128)S(1)} %bitcast.5), custom_call_target="tpu_custom_call" | custom-call | flops 450000000 | tf_op jit(solution)/shard_map/pallas_call | solution.py:60
  166.3 2.5 %shard_map.88 = (f32[3,128,128]{2,1,0:T(8,128)S(1)}, f32[2,128,128]{2,1,0:T(8,128)S(1)}, f32[5,128,128]{2,1,0:T(8,128)S(1)}) custom-call(s32[1]{0:T(128)} %bitcast.dev, bf16[4,4608,256]{2,1,0:T(8,128)(2,1)S(1)} %get-tuple-element.55.bhi, bf16[4,4608,256]{2,1,0:T(8,128)(2,1)S(1)} %get-tuple-element.56.blo, f32[2304,128]{1,0:T(8,128)S(1)} %collective-permute-done.33.v.theirs, ...), custom_call_target="tpu_custom_call" | custom-call | flops 450000000 | tf_op jit(solution)/shard_map/pallas_call | solution.py:60
  169.7 4.8 %collective-permute-done.34.ra = f32[3,128,128]{2,1,0:T(8,128)S(1)} collective-permute-done((f32[3,128,128]{2,1,0:T(8,128)S(1)}, f32[3,128,128]{2,1,0:T(8,128)S(1)}, u32[]{:S(2)}, u32[]{:S(2)}) %collective-permute-start.34) | collective-permute-done | bytes 196640 | tf_op jit(solution)/shard_map/ppermute | solution.py:488
  175.7 5.2 %collective-permute-done.35.rb = f32[2,128,128]{2,1,0:T(8,128)S(1)} collective-permute-done((f32[2,128,128]{2,1,0:T(8,128)S(1)}, f32[2,128,128]{2,1,0:T(8,128)S(1)}, u32[]{:S(2)}, u32[]{:S(2)}) %collective-permute-start.35) | collective-permute-done | bytes 131104 | tf_op jit(solution)/shard_map/ppermute | solution.py:488
  181.7 4.5 %collective-permute-done.37.r3 = f32[2,128,128]{2,1,0:T(8,128)S(1)} collective-permute-done((f32[2,128,128]{2,1,0:T(8,128)S(1)}, f32[2,128,128]{2,1,0:T(8,128)S(1)}, u32[]{:S(2)}, u32[]{:S(2)}) %collective-permute-start.37) | collective-permute-done | bytes 131104 | tf_op jit(solution)/shard_map/ppermute | solution.py:488
  186.5 3.0 %collective-permute-start.38 = (f32[2,128,128]{2,1,0:T(8,128)S(1)}, f32[2,128,128]{2,1,0:T(8,128)S(1)}, u32[]{:S(2)}, u32[]{:S(2)}) collective-permute-start(f32[2,128,128]{2,1,0:T(8,128)S(1)} %shard_map.91.own), channel_id=1, source_target_pairs={{0,8},{8,0},{1,9},{9,1},{2,10},{10,2},{3,11},{11,3},{4,12},{12,4},... | collective-permute-start | bytes 393224 | tf_op jit(solution)/shard_map/ppermute | solution.py:468
  190.5 1.4 collective-permute-start.41
  192.6 1.3 collective-permute-start.39
  193.9 2.0 shard_map.93
  198.5 1.5 collective-permute-start.42
  199.9 1.9 shard_map.94
  203.2 3.0 %collective-permute-start.45 = (f32[128,128]{1,0:T(8,128)S(1)}, f32[128,128]{1,0:T(8,128)S(1)}, u32[]{:S(2)}, u32[]{:S(2)}) collective-permute-start(f32[128,128]{1,0:T(8,128)S(1)} %add_add_fusion.a), channel_id=1, source_target_pairs={{0,4},{4,0},{16,20},{20,16},{1,5},{5,1},{17,21},{21,17},{2,6},{6,2... | collective-permute-start | bytes 196616 | tf_op jit(solution)/shard_map/ppermute | solution.py:468
  206.2 4.2 %finish.1 = (f32[4500,128]{1,0:T(8,128)}, f32[128,128]{1,0:T(8,128)S(1)}) custom-call(s32[1]{0:T(128)} %bitcast.dev, f32[2304,128]{1,0:T(8,128)S(1)} %bitcast.6, f32[2304,128]{1,0:T(8,128)S(1)} %collective-permute-done.33.v.theirs, f32[128,128]{1,0:T(8,128)S(1)} %get-tuple-element.97.g, f32[128,128]{1,0:T(8,128)S(1)} %get-tuple-element.98.w), custom_call_target="tpu_custom_call" | custom-call | flops 630000000 | tf_op jit(solution)/shard_map/finish/pallas_call | solution.py:439
  (104 shorter events, 32.9 us)
Async XLA Ops:
  39.2 4.7 %collective-permute-start = (f32[2,288,128]{2,1,0:T(8,128)S(1)}, f32[2,288,128]{2,1,0:T(8,128)S(1)}, u32[]{:S(2)}, u32[]{:S(2)}) collective-permute-start(f32[2,288,128]{2,1,0:T(8,128)S(1)} %get-tuple-element.60), channel_id=1, source_target_pairs={{0,8},{8,0},{1,9},{9,1},{2,10},{10,2},{3,11},{11,3},{4,12},{12,4},... | collective-permute-start | bytes 884744 | tf_op jit(solution)/shard_map/ppermute | solution.py:468
  44.7 1.7 collective-permute-start.1
  45.2 5.9 %collective-permute-start.3 = (f32[2,288,128]{2,1,0:T(8,128)S(1)}, f32[2,288,128]{2,1,0:T(8,128)S(1)}, u32[]{:S(2)}, u32[]{:S(2)}) collective-permute-start(f32[2,288,128]{2,1,0:T(8,128)S(1)} %shard_map.54), channel_id=1, source_target_pairs={{0,32},{8,24},{16,48},{24,8},{32,0},{40,56},{48,16},{56,40},{64,96... | collective-permute-start | bytes 884744 | tf_op jit(solution)/shard_map/ppermute | solution.py:488
  47.2 3.8 %collective-permute-start.2 = (f32[2,288,128]{2,1,0:T(8,128)S(1)}, f32[2,288,128]{2,1,0:T(8,128)S(1)}, u32[]{:S(2)}, u32[]{:S(2)}) collective-permute-start(f32[2,288,128]{2,1,0:T(8,128)S(1)} %shard_map.59), channel_id=1, source_target_pairs={{0,8},{8,0},{1,9},{9,1},{2,10},{10,2},{3,11},{11,3},{4,12},{12,4},... | collective-permute-start | bytes 884744 | tf_op jit(solution)/shard_map/ppermute | solution.py:468
  49.0 6.6 %collective-permute-start.5 = (f32[2,288,128]{2,1,0:T(8,128)S(1)}, f32[2,288,128]{2,1,0:T(8,128)S(1)}, u32[]{:S(2)}, u32[]{:S(2)}) collective-permute-start(f32[2,288,128]{2,1,0:T(8,128)S(1)} %shard_map.57), channel_id=1, source_target_pairs={{0,32},{8,24},{16,48},{24,8},{32,0},{40,56},{48,16},{56,40},{64,96... | collective-permute-start | bytes 884744 | tf_op jit(solution)/shard_map/ppermute | solution.py:488
  51.9 5.4 %collective-permute-start.4 = (f32[2,288,128]{2,1,0:T(8,128)S(1)}, f32[2,288,128]{2,1,0:T(8,128)S(1)}, u32[]{:S(2)}, u32[]{:S(2)}) collective-permute-start(f32[2,288,128]{2,1,0:T(8,128)S(1)} %shard_map.62), channel_id=1, source_target_pairs={{0,8},{8,0},{1,9},{9,1},{2,10},{10,2},{3,11},{11,3},{4,12},{12,4},... | collective-permute-start | bytes 884744 | tf_op jit(solution)/shard_map/ppermute | solution.py:468
  53.0 4.3 %collective-permute-start.7 = (f32[1,288,128]{2,1,0:T(8,128)S(1)}, f32[1,288,128]{2,1,0:T(8,128)S(1)}, u32[]{:S(2)}, u32[]{:S(2)}) collective-permute-start(f32[1,288,128]{2,1,0:T(8,128)S(1)} %shard_map.63), channel_id=1, source_target_pairs={{0,96},{8,40},{16,112},{24,56},{32,64},{40,8},{48,80},{56,24},{64,... | collective-permute-start | bytes 442376 | tf_op jit(solution)/shard_map/ppermute | solution.py:488
  54.7 6.2 %collective-permute-start.6 = (f32[1,288,128]{2,1,0:T(8,128)S(1)}, f32[1,288,128]{2,1,0:T(8,128)S(1)}, u32[]{:S(2)}, u32[]{:S(2)}) collective-permute-start(f32[1,288,128]{2,1,0:T(8,128)S(1)} %shard_map.60), channel_id=1, source_target_pairs={{0,96},{8,40},{16,112},{24,56},{32,64},{40,8},{48,80},{56,24},{64,... | collective-permute-start | bytes 442376 | tf_op jit(solution)/shard_map/ppermute | solution.py:488
  57.3 7.1 %collective-permute-start.8 = (f32[1,288,128]{2,1,0:T(8,128)S(1)}, f32[1,288,128]{2,1,0:T(8,128)S(1)}, u32[]{:S(2)}, u32[]{:S(2)}) collective-permute-start(f32[1,288,128]{2,1,0:T(8,128)S(1)} %shard_map.64), channel_id=1, source_target_pairs={{0,16},{8,104},{16,0},{24,120},{32,48},{40,72},{48,32},{56,88},{64... | collective-permute-start | bytes 442376 | tf_op jit(solution)/shard_map/ppermute | solution.py:488
  64.4 5.3 %collective-permute-start.9 = (f32[1,288,128]{2,1,0:T(8,128)S(1)}, f32[1,288,128]{2,1,0:T(8,128)S(1)}, u32[]{:S(2)}, u32[]{:S(2)}) collective-permute-start(f32[1,288,128]{2,1,0:T(8,128)S(1)} %shard_map.65.refs_0_), channel_id=1, source_target_pairs={{0,16},{8,104},{16,0},{24,120},{32,48},{40,72},{48,32},{56,88},{64... | collective-permute-start | bytes 442376 | tf_op jit(solution)/shard_map/ppermute | solution.py:488
  66.3 4.9 %collective-permute-start.10 = (f32[1,288,128]{2,1,0:T(8,128)S(1)}, f32[1,288,128]{2,1,0:T(8,128)S(1)}, u32[]{:S(2)}, u32[]{:S(2)}) collective-permute-start(f32[1,288,128]{2,1,0:T(8,128)S(1)} %shard_map.65.refs_0_), channel_id=1, source_target_pairs={{0,96},{8,40},{16,112},{24,56},{32,64},{40,8},{48,80},{56,24},{64,... | collective-permute-start | bytes 442376 | tf_op jit(solution)/shard_map/ppermute | solution.py:488
  69.7 4.0 %collective-permute-start.11 = (f32[1,288,128]{2,1,0:T(8,128)S(1)}, f32[1,288,128]{2,1,0:T(8,128)S(1)}, u32[]{:S(2)}, u32[]{:S(2)}) collective-permute-start(f32[1,288,128]{2,1,0:T(8,128)S(1)} %collective-permute-done.9.refs_1_), channel_id=1, source_target_pairs={{0,96},{8,40},{16,112},{24,56},{32,64},{40,8},{48,80},{56,24},{64,... | collective-permute-start | bytes 442376 | tf_op jit(solution)/shard_map/ppermute | solution.py:488
  69.7 4.3 %collective-permute-start.12 = (f32[1,288,128]{2,1,0:T(8,128)S(1)}, f32[1,288,128]{2,1,0:T(8,128)S(1)}, u32[]{:S(2)}, u32[]{:S(2)}) collective-permute-start(f32[1,288,128]{2,1,0:T(8,128)S(1)} %shard_map.65.refs_0_), channel_id=1, source_target_pairs={{0,32},{8,24},{16,48},{24,8},{32,0},{40,56},{48,16},{56,40},{64,96... | collective-permute-start | bytes 442376 | tf_op jit(solution)/shard_map/ppermute | solution.py:488
  70.0 6.8 %collective-permute-start.13 = (f32[1,288,128]{2,1,0:T(8,128)S(1)}, f32[1,288,128]{2,1,0:T(8,128)S(1)}, u32[]{:S(2)}, u32[]{:S(2)}) collective-permute-start(f32[1,288,128]{2,1,0:T(8,128)S(1)} %collective-permute-done.9.refs_1_), channel_id=1, source_target_pairs={{0,32},{8,24},{16,48},{24,8},{32,0},{40,56},{48,16},{56,40},{64,96... | collective-permute-start | bytes 442376 | tf_op jit(solution)/shard_map/ppermute | solution.py:488
  71.2 5.7 %collective-permute-start.14 = (f32[1,288,128]{2,1,0:T(8,128)S(1)}, f32[1,288,128]{2,1,0:T(8,128)S(1)}, u32[]{:S(2)}, u32[]{:S(2)}) collective-permute-start(f32[1,288,128]{2,1,0:T(8,128)S(1)} %collective-permute-done.10.refs_2_), channel_id=1, source_target_pairs={{0,32},{8,24},{16,48},{24,8},{32,0},{40,56},{48,16},{56,40},{64,96... | collective-permute-start | bytes 442376 | tf_op jit(solution)/shard_map/ppermute | solution.py:488
  73.7 5.0 %collective-permute-start.15 = (f32[1,288,128]{2,1,0:T(8,128)S(1)}, f32[1,288,128]{2,1,0:T(8,128)S(1)}, u32[]{:S(2)}, u32[]{:S(2)}) collective-permute-start(f32[1,288,128]{2,1,0:T(8,128)S(1)} %collective-permute-done.11.refs_3_), channel_id=1, source_target_pairs={{0,32},{8,24},{16,48},{24,8},{32,0},{40,56},{48,16},{56,40},{64,96... | collective-permute-start | bytes 442376 | tf_op jit(solution)/shard_map/ppermute | solution.py:488
  78.8 7.9 %collective-permute-start.16 = (f32[2304,128]{1,0:T(8,128)S(1)}, f32[2304,128]{1,0:T(8,128)S(1)}, u32[]{:S(2)}, u32[]{:S(2)}) collective-permute-start(f32[2304,128]{1,0:T(8,128)S(1)} %bitcast.7), channel_id=1, source_target_pairs={{0,8},{8,0},{1,9},{9,1},{2,10},{10,2},{3,11},{11,3},{4,12},{12,4},... | collective-permute-start | bytes 3538952 | tf_op jit(solution)/shard_map/ppermute | solution.py:468
  117.8 3.8 %collective-permute-start.17 = (f32[2,288,128]{2,1,0:T(8,128)S(1)}, f32[2,288,128]{2,1,0:T(8,128)S(1)}, u32[]{:S(2)}, u32[]{:S(2)}) collective-permute-start(f32[2,288,128]{2,1,0:T(8,128)S(1)} %get-tuple-element.67), channel_id=1, source_target_pairs={{0,8},{8,0},{1,9},{9,1},{2,10},{10,2},{3,11},{11,3},{4,12},{12,4},... | collective-permute-start | bytes 884744 | tf_op jit(solution)/shard_map/ppermute | solution.py:468
  122.5 1.7 collective-permute-start.18
  123.0 5.9 %collective-permute-start.20 = (f32[2,288,128]{2,1,0:T(8,128)S(1)}, f32[2,288,128]{2,1,0:T(8,128)S(1)}, u32[]{:S(2)}, u32[]{:S(2)}) collective-permute-start(f32[2,288,128]{2,1,0:T(8,128)S(1)} %shard_map.72), channel_id=1, source_target_pairs={{0,32},{8,24},{16,48},{24,8},{32,0},{40,56},{48,16},{56,40},{64,96... | collective-permute-start | bytes 884744 | tf_op jit(solution)/shard_map/ppermute | solution.py:488
  125.0 3.8 %collective-permute-start.19 = (f32[2,288,128]{2,1,0:T(8,128)S(1)}, f32[2,288,128]{2,1,0:T(8,128)S(1)}, u32[]{:S(2)}, u32[]{:S(2)}) collective-permute-start(f32[2,288,128]{2,1,0:T(8,128)S(1)} %shard_map.77), channel_id=1, source_target_pairs={{0,8},{8,0},{1,9},{9,1},{2,10},{10,2},{3,11},{11,3},{4,12},{12,4},... | collective-permute-start | bytes 884744 | tf_op jit(solution)/shard_map/ppermute | solution.py:468
  129.7 7.3 %collective-permute-start.22 = (f32[2,288,128]{2,1,0:T(8,128)S(1)}, f32[2,288,128]{2,1,0:T(8,128)S(1)}, u32[]{:S(2)}, u32[]{:S(2)}) collective-permute-start(f32[2,288,128]{2,1,0:T(8,128)S(1)} %shard_map.81), channel_id=1, source_target_pairs={{0,8},{8,0},{1,9},{9,1},{2,10},{10,2},{3,11},{11,3},{4,12},{12,4},... | collective-permute-start | bytes 884744 | tf_op jit(solution)/shard_map/ppermute | solution.py:468
  130.7 6.2 %collective-permute-start.23 = (f32[2,288,128]{2,1,0:T(8,128)S(1)}, f32[2,288,128]{2,1,0:T(8,128)S(1)}, u32[]{:S(2)}, u32[]{:S(2)}) collective-permute-start(f32[2,288,128]{2,1,0:T(8,128)S(1)} %shard_map.75), channel_id=1, source_target_pairs={{0,32},{8,24},{16,48},{24,8},{32,0},{40,56},{48,16},{56,40},{64,96... | collective-permute-start | bytes 884744 | tf_op jit(solution)/shard_map/ppermute | solution.py:488
  131.1 5.8 %collective-permute-start.21 = (f32[1,288,128]{2,1,0:T(8,128)S(1)}, f32[1,288,128]{2,1,0:T(8,128)S(1)}, u32[]{:S(2)}, u32[]{:S(2)}) collective-permute-start(f32[1,288,128]{2,1,0:T(8,128)S(1)} %shard_map.78), channel_id=1, source_target_pairs={{0,96},{8,40},{16,112},{24,56},{32,64},{40,8},{48,80},{56,24},{64,... | collective-permute-start | bytes 442376 | tf_op jit(solution)/shard_map/ppermute | solution.py:488
  137.0 5.3 %collective-permute-start.25 = (f32[1,288,128]{2,1,0:T(8,128)S(1)}, f32[1,288,128]{2,1,0:T(8,128)S(1)}, u32[]{:S(2)}, u32[]{:S(2)}) collective-permute-start(f32[1,288,128]{2,1,0:T(8,128)S(1)} %shard_map.83), channel_id=1, source_target_pairs={{0,16},{8,104},{16,0},{24,120},{32,48},{40,72},{48,32},{56,88},{64... | collective-permute-start | bytes 442376 | tf_op jit(solution)/shard_map/ppermute | solution.py:488
  138.4 4.3 %collective-permute-start.24 = (f32[1,288,128]{2,1,0:T(8,128)S(1)}, f32[1,288,128]{2,1,0:T(8,128)S(1)}, u32[]{:S(2)}, u32[]{:S(2)}) collective-permute-start(f32[1,288,128]{2,1,0:T(8,128)S(1)} %shard_map.79), channel_id=1, source_target_pairs={{0,96},{8,40},{16,112},{24,56},{32,64},{40,8},{48,80},{56,24},{64,... | collective-permute-start | bytes 442376 | tf_op jit(solution)/shard_map/ppermute | solution.py:488
  143.0 5.3 %collective-permute-start.26 = (f32[1,288,128]{2,1,0:T(8,128)S(1)}, f32[1,288,128]{2,1,0:T(8,128)S(1)}, u32[]{:S(2)}, u32[]{:S(2)}) collective-permute-start(f32[1,288,128]{2,1,0:T(8,128)S(1)} %shard_map.85.refs_0_), channel_id=1, source_target_pairs={{0,16},{8,104},{16,0},{24,120},{32,48},{40,72},{48,32},{56,88},{64... | collective-permute-start | bytes 442376 | tf_op jit(solution)/shard_map/ppermute | solution.py:488
  144.4 5.3 %collective-permute-start.27 = (f32[1,288,128]{2,1,0:T(8,128)S(1)}, f32[1,288,128]{2,1,0:T(8,128)S(1)}, u32[]{:S(2)}, u32[]{:S(2)}) collective-permute-start(f32[1,288,128]{2,1,0:T(8,128)S(1)} %shard_map.85.refs_0_), channel_id=1, source_target_pairs={{0,96},{8,40},{16,112},{24,56},{32,64},{40,8},{48,80},{56,24},{64,... | collective-permute-start | bytes 442376 | tf_op jit(solution)/shard_map/ppermute | solution.py:488
  148.3 4.3 %collective-permute-start.28 = (f32[1,288,128]{2,1,0:T(8,128)S(1)}, f32[1,288,128]{2,1,0:T(8,128)S(1)}, u32[]{:S(2)}, u32[]{:S(2)}) collective-permute-start(f32[1,288,128]{2,1,0:T(8,128)S(1)} %collective-permute-done.26.refs_1_), channel_id=1, source_target_pairs={{0,96},{8,40},{16,112},{24,56},{32,64},{40,8},{48,80},{56,24},{64,... | collective-permute-start | bytes 442376 | tf_op jit(solution)/shard_map/ppermute | solution.py:488
  148.3 5.6 %collective-permute-start.29 = (f32[1,288,128]{2,1,0:T(8,128)S(1)}, f32[1,288,128]{2,1,0:T(8,128)S(1)}, u32[]{:S(2)}, u32[]{:S(2)}) collective-permute-start(f32[1,288,128]{2,1,0:T(8,128)S(1)} %shard_map.85.refs_0_), channel_id=1, source_target_pairs={{0,32},{8,24},{16,48},{24,8},{32,0},{40,56},{48,16},{56,40},{64,96... | collective-permute-start | bytes 442376 | tf_op jit(solution)/shard_map/ppermute | solution.py:488
  149.5 6.3 %collective-permute-start.30 = (f32[1,288,128]{2,1,0:T(8,128)S(1)}, f32[1,288,128]{2,1,0:T(8,128)S(1)}, u32[]{:S(2)}, u32[]{:S(2)}) collective-permute-start(f32[1,288,128]{2,1,0:T(8,128)S(1)} %collective-permute-done.26.refs_1_), channel_id=1, source_target_pairs={{0,32},{8,24},{16,48},{24,8},{32,0},{40,56},{48,16},{56,40},{64,96... | collective-permute-start | bytes 442376 | tf_op jit(solution)/shard_map/ppermute | solution.py:488
  149.7 6.0 %collective-permute-start.31 = (f32[1,288,128]{2,1,0:T(8,128)S(1)}, f32[1,288,128]{2,1,0:T(8,128)S(1)}, u32[]{:S(2)}, u32[]{:S(2)}) collective-permute-start(f32[1,288,128]{2,1,0:T(8,128)S(1)} %collective-permute-done.27.refs_2_), channel_id=1, source_target_pairs={{0,32},{8,24},{16,48},{24,8},{32,0},{40,56},{48,16},{56,40},{64,96... | collective-permute-start | bytes 442376 | tf_op jit(solution)/shard_map/ppermute | solution.py:488
  152.6 5.1 %collective-permute-start.32 = (f32[1,288,128]{2,1,0:T(8,128)S(1)}, f32[1,288,128]{2,1,0:T(8,128)S(1)}, u32[]{:S(2)}, u32[]{:S(2)}) collective-permute-start(f32[1,288,128]{2,1,0:T(8,128)S(1)} %collective-permute-done.28.refs_3_), channel_id=1, source_target_pairs={{0,32},{8,24},{16,48},{24,8},{32,0},{40,56},{48,16},{56,40},{64,96... | collective-permute-start | bytes 442376 | tf_op jit(solution)/shard_map/ppermute | solution.py:488
  157.7 8.5 %collective-permute-start.33 = (f32[2304,128]{1,0:T(8,128)S(1)}, f32[2304,128]{1,0:T(8,128)S(1)}, u32[]{:S(2)}, u32[]{:S(2)}) collective-permute-start(f32[2304,128]{1,0:T(8,128)S(1)} %bitcast.4), channel_id=1, source_target_pairs={{0,8},{8,0},{1,9},{9,1},{2,10},{10,2},{3,11},{11,3},{4,12},{12,4},... | collective-permute-start | bytes 3538952 | tf_op jit(solution)/shard_map/ppermute | solution.py:468
  168.8 5.8 %collective-permute-start.34 = (f32[3,128,128]{2,1,0:T(8,128)S(1)}, f32[3,128,128]{2,1,0:T(8,128)S(1)}, u32[]{:S(2)}, u32[]{:S(2)}) collective-permute-start(f32[3,128,128]{2,1,0:T(8,128)S(1)} %get-tuple-element.84), channel_id=1, source_target_pairs={{0,1},{1,0},{2,3},{3,2},{4,5},{5,4},{6,7},{7,6},{8,11},{9,10},{10,... | collective-permute-start | bytes 589832 | tf_op jit(solution)/shard_map/ppermute | solution.py:488
  174.6 6.2 %collective-permute-start.36 = (f32[3,128,128]{2,1,0:T(8,128)S(1)}, f32[3,128,128]{2,1,0:T(8,128)S(1)}, u32[]{:S(2)}, u32[]{:S(2)}) collective-permute-start(f32[3,128,128]{2,1,0:T(8,128)S(1)} %shard_map.89), channel_id=1, source_target_pairs={{0,3},{1,2},{2,1},{3,0},{4,7},{5,6},{6,5},{7,4},{8,9},{9,8},{10,11... | collective-permute-start | bytes 589832 | tf_op jit(solution)/shard_map/ppermute | solution.py:488
  174.7 6.1 %collective-permute-start.35 = (f32[2,128,128]{2,1,0:T(8,128)S(1)}, f32[2,128,128]{2,1,0:T(8,128)S(1)}, u32[]{:S(2)}, u32[]{:S(2)}) collective-permute-start(f32[2,128,128]{2,1,0:T(8,128)S(1)} %get-tuple-element.85), channel_id=1, source_target_pairs={{0,1},{1,0},{2,3},{3,2},{4,5},{5,4},{6,7},{7,6},{8,11},{9,10},{10,... | collective-permute-start | bytes 393224 | tf_op jit(solution)/shard_map/ppermute | solution.py:488
  180.8 5.4 %collective-permute-start.37 = (f32[2,128,128]{2,1,0:T(8,128)S(1)}, f32[2,128,128]{2,1,0:T(8,128)S(1)}, u32[]{:S(2)}, u32[]{:S(2)}) collective-permute-start(f32[2,128,128]{2,1,0:T(8,128)S(1)} %shard_map.90), channel_id=1, source_target_pairs={{0,4},{1,5},{2,6},{3,7},{4,0},{5,1},{6,2},{7,3},{8,12},{9,13},{10,... | collective-permute-start | bytes 393224 | tf_op jit(solution)/shard_map/ppermute | solution.py:488
  186.5 4.0 %collective-permute-start.38 = (f32[2,128,128]{2,1,0:T(8,128)S(1)}, f32[2,128,128]{2,1,0:T(8,128)S(1)}, u32[]{:S(2)}, u32[]{:S(2)}) collective-permute-start(f32[2,128,128]{2,1,0:T(8,128)S(1)} %shard_map.91.own), channel_id=1, source_target_pairs={{0,8},{8,0},{1,9},{9,1},{2,10},{10,2},{3,11},{11,3},{4,12},{12,4},... | collective-permute-start | bytes 393224 | tf_op jit(solution)/shard_map/ppermute | solution.py:468
  190.5 5.3 %collective-permute-start.41 = (f32[128,128]{1,0:T(8,128)S(1)}, f32[128,128]{1,0:T(8,128)S(1)}, u32[]{:S(2)}, u32[]{:S(2)}) collective-permute-start(f32[128,128]{1,0:T(8,128)S(1)} %get-tuple-element.86), channel_id=1, source_target_pairs={{0,96},{32,64},{64,32},{96,0},{1,97},{33,65},{65,33},{97,1},{2,98}... | collective-permute-start | bytes 196616 | tf_op jit(solution)/shard_map/ppermute | solution.py:468
  191.9 4.6 %collective-permute-start.40 = (f32[128,128]{1,0:T(8,128)S(1)}, f32[128,128]{1,0:T(8,128)S(1)}, u32[]{:S(2)}, u32[]{:S(2)}) collective-permute-start(f32[128,128]{1,0:T(8,128)S(1)} %get-tuple-element.86), channel_id=1, source_target_pairs={{0,64},{32,96},{64,0},{96,32},{1,65},{33,97},{65,1},{97,33},{2,66}... | collective-permute-start | bytes 196616 | tf_op jit(solution)/shard_map/ppermute | solution.py:468
  192.6 4.0 %collective-permute-start.39 = (f32[128,128]{1,0:T(8,128)S(1)}, f32[128,128]{1,0:T(8,128)S(1)}, u32[]{:S(2)}, u32[]{:S(2)}) collective-permute-start(f32[128,128]{1,0:T(8,128)S(1)} %get-tuple-element.86), channel_id=1, source_target_pairs={{0,32},{32,0},{64,96},{96,64},{1,33},{33,1},{65,97},{97,65},{2,34}... | collective-permute-start | bytes 196616 | tf_op jit(solution)/shard_map/ppermute | solution.py:468
  196.6 5.3 %collective-permute-start.44 = (f32[128,128]{1,0:T(8,128)S(1)}, f32[128,128]{1,0:T(8,128)S(1)}, u32[]{:S(2)}, u32[]{:S(2)}) collective-permute-start(f32[128,128]{1,0:T(8,128)S(1)} %add_add_fusion.1), channel_id=1, source_target_pairs={{0,3},{1,2},{2,1},{3,0},{4,7},{5,6},{6,5},{7,4},{8,11},{9,10},{10,... | collective-permute-start | bytes 196616 | tf_op jit(solution)/shard_map/ppermute | solution.py:468
  197.6 4.6 %collective-permute-start.43 = (f32[128,128]{1,0:T(8,128)S(1)}, f32[128,128]{1,0:T(8,128)S(1)}, u32[]{:S(2)}, u32[]{:S(2)}) collective-permute-start(f32[128,128]{1,0:T(8,128)S(1)} %add_add_fusion.1), channel_id=1, source_target_pairs={{0,2},{1,3},{2,0},{3,1},{4,6},{5,7},{6,4},{7,5},{8,10},{9,11},{10,... | collective-permute-start | bytes 196616 | tf_op jit(solution)/shard_map/ppermute | solution.py:468
  198.5 3.8 %collective-permute-start.42 = (f32[128,128]{1,0:T(8,128)S(1)}, f32[128,128]{1,0:T(8,128)S(1)}, u32[]{:S(2)}, u32[]{:S(2)}) collective-permute-start(f32[128,128]{1,0:T(8,128)S(1)} %add_add_fusion.1), channel_id=1, source_target_pairs={{0,1},{1,0},{2,3},{3,2},{4,5},{5,4},{6,7},{7,6},{8,9},{9,8},{10,11... | collective-permute-start | bytes 196616 | tf_op jit(solution)/shard_map/ppermute | solution.py:468
  202.3 8.2 %collective-permute-start.47 = (f32[128,128]{1,0:T(8,128)S(1)}, f32[128,128]{1,0:T(8,128)S(1)}, u32[]{:S(2)}, u32[]{:S(2)}) collective-permute-start(f32[128,128]{1,0:T(8,128)S(1)} %add_add_fusion.a), channel_id=1, source_target_pairs={{0,20},{4,16},{16,4},{20,0},{1,21},{5,17},{17,5},{21,1},{2,22},{6,... | collective-permute-start | bytes 196616 | tf_op jit(solution)/shard_map/ppermute | solution.py:468
  202.6 7.9 %collective-permute-start.46 = (f32[128,128]{1,0:T(8,128)S(1)}, f32[128,128]{1,0:T(8,128)S(1)}, u32[]{:S(2)}, u32[]{:S(2)}) collective-permute-start(f32[128,128]{1,0:T(8,128)S(1)} %add_add_fusion.a), channel_id=1, source_target_pairs={{0,16},{4,20},{16,0},{20,4},{1,17},{5,21},{17,1},{21,5},{2,18},{6,... | collective-permute-start | bytes 196616 | tf_op jit(solution)/shard_map/ppermute | solution.py:468
  203.2 7.2 %collective-permute-start.45 = (f32[128,128]{1,0:T(8,128)S(1)}, f32[128,128]{1,0:T(8,128)S(1)}, u32[]{:S(2)}, u32[]{:S(2)}) collective-permute-start(f32[128,128]{1,0:T(8,128)S(1)} %add_add_fusion.a), channel_id=1, source_target_pairs={{0,4},{4,0},{16,20},{20,16},{1,5},{5,1},{17,21},{21,17},{2,6},{6,2... | collective-permute-start | bytes 196616 | tf_op jit(solution)/shard_map/ppermute | solution.py:468
  (1 other events, 25.6 us)

commit v3 on v2

--- a/solution.py
+++ b/solution.py
@@ -230,28 +230,32 @@
 
 
 def reduce_aux(dev, early, late, keep, gaps):
+    def second_step(k, ra, first, other):
+        first[0] = k[3] + ra[1]
+        first[1] = k[4] + ra[2]
+        other[0] = k[2] + ra[0]
+
     def last_step(k, ra, rb, r2, out):
-        out[0] = (k[1] + rb[1]) + r2[1]
-        out[1] = (k[4] + ra[2]) + r2[2]
-
-    def finish_sum(dev, k, ra, rb, r2, r3, gaps, out):
-        own = ((k[0] + rb[0]) + r2[0]) + r3[0]
+        out[0] = (k[1] + rb[1]) + r2[0]
+        out[1] = (k[4] + ra[2]) + r2[1]
+
+    def finish_sum(dev, k, ra, rb, r2, r2_own, r3, gaps, out):
+        own = ((k[0] + rb[0]) + r2_own[0]) + r3[0]
         out[0] = dot(own * weights_of(dev, gaps), own, 1, 1, HIGHEST)
-        out[1] = ((k[4] + ra[2]) + r2[2]) + r3[1]
-
-    def second_step(k, ra, out):
-        out[...] = k[2:5] + ra[...]
+        out[1] = ((k[4] + ra[2]) + r2[1]) + r3[1]
 
     def pieces(n):
         return [((n, K, K), F32)]
 
     ra = cross(early, 0, AUX_LINKS)
     rb = cross(late, 0, AUX_LINKS)
-    (send,) = kernel_call(second_step, pieces(3), [], [], [keep, ra])
-    r2 = cross(send, 1, AUX_LINKS)
+    first, other = kernel_call(second_step, pieces(2) + pieces(1), [], [], [keep, ra])
+    r2 = cross(first, 1, AUX_LINKS)
+    r2_own = cross(other, 1, AUX_LINKS)
     (send,) = kernel_call(last_step, pieces(2), [], [], [keep, ra, rb, r2])
     r3 = cross(send, 2, AUX_LINKS)
-    return kernel_call(finish_sum, pieces(2), [dev], [], [keep, ra, rb, r2, r3, gaps])[0]
+    ins = [keep, ra, rb, r2, r2_own, r3, gaps]
+    return kernel_call(finish_sum, pieces(2), [dev], [], ins)[0]
 
 
 def add_over_cores(dev, both):

time: 215 us -> 214 us (level)
  waiting for transfers between devices: 48.8 us -> 45.5 us
    ppermute x28 -> x29, waiting for transfers between devices: 45.7 us -> 42.3 us  [cross(): return lax.ppermute(value, axes, pairs)]
    ppermute x28 -> x29, starting transfers between devices: 21 us -> 22.1 us  [cross(): return lax.ppermute(value, axes, pairs)]
  transfers between devices with their start and end apart: 48 -> 49, of which waited for: 26 -> 27; matrix products, arithmetic and copies ran while one was open for 0% -> 0% of each run, Pallas kernels for 13% -> 13%
where the time goes in v3:
time: 214 us; the launch traced here: 210 us
  starting transfers between devices  59.5 us (28%)
  blocking collectives  57.1 us (27%)
  Pallas kernels  46.6 us (22%)
  waiting for transfers between devices  45.5 us (21%)
    all_to_all x4, blocking collectives, to_each(): return lax.all_to_all(value, axes, split_axis=0, concat_axis=0, tiled=True)  57.1 us
    pallas_call x46, Pallas kernels, kernel_call(): pl.pallas_call(body, out_shape=[pltpu.VMEM(s, d) for s, d in outs], in_sp...  42.4 us
    ppermute x29, waiting for transfers between devices, cross(): return lax.ppermute(value, axes, pairs)  42.3 us
    ppermute x20, starting transfers between devices, exchange(): return lax.ppermute(value, axis, [(i, i ^ mask) for i in range(n)])  37.3 us
    ppermute x29, starting transfers between devices, cross(): return lax.ppermute(value, axes, pairs)  22.1 us
  transfers between devices with their start and end apart: 49, of which 27 were waited for; matrix products, arithmetic and copies ran while one was open for 0% of the time, Pallas kernels for 13%

profile of v3, /device:TPU:1, one launch (start us, length us, event | category | flops | bytes accessed | tf_op | source)
XLA Modules:
  0.0 210.4 jit_solution(8456171688157185523)
XLA Ops:
  0.7 8.3 %shard_map.50 = (bf16[4,4608,256]{2,1,0:T(8,128)(2,1)S(1)}, bf16[4,4608,256]{2,1,0:T(8,128)(2,1)S(1)}, f32[8,128,128]{2,1,0:T(8,128)S(1)}) custom-call(f32[4500,1024]{1,0:T(8,128)} %b_hbm.1, f32[4500,128]{1,0:T(8,128)} %v_hbm), custom_call_target="tpu_custom_call" | custom-call | flops 1200000000 | tf_op jit(solution)/shard_map/pallas_call | solution.py:60
  8.9 17.3 %all_to_all.20.p = f32[8,128,128]{2,1,0:T(8,128)S(1)} all-to-all(f32[8,128,128]{2,1,0:T(8,128)S(1)} %get-tuple-element.59), channel_id=1, replica_groups=mesh['z'=4,'xl'=2,'c'=2,'xh'=2,'y'=4] {'xh','y'}, dimensions={0} | all-to-all | bytes 1048576 | tf_op jit(solution)/shard_map/all_to_all | solution.py:476
  26.3 12.1 %all_to_all.21.s = f32[8,128,128]{2,1,0:T(8,128)S(1)} all-to-all(f32[8,128,128]{2,1,0:T(8,128)S(1)} %shard_map.51), channel_id=1, replica_groups=mesh['z'=4,'xl'=2,'c'=2,'xh'=2,'y'=4] {'xh','y'}, dimensions={0} | all-to-all | bytes 1048576 | tf_op jit(solution)/shard_map/all_to_all | solution.py:476
  39.2 3.5 %collective-permute-start = (f32[2,288,128]{2,1,0:T(8,128)S(1)}, f32[2,288,128]{2,1,0:T(8,128)S(1)}, u32[]{:S(2)}, u32[]{:S(2)}) collective-permute-start(f32[2,288,128]{2,1,0:T(8,128)S(1)} %get-tuple-element.62), channel_id=1, source_target_pairs={{0,8},{8,0},{1,9},{9,1},{2,10},{10,2},{3,11},{11,3},{4,12},{12,4},... | collective-permute-start | bytes 884744 | tf_op jit(solution)/shard_map/ppermute | solution.py:472
  47.2 1.7 collective-permute-start.2
  53.0 1.7 collective-permute-start.7
  55.6 1.6 collective-permute-done.7.r2
  57.3 3.7 %collective-permute-start.8 = (f32[1,288,128]{2,1,0:T(8,128)S(1)}, f32[1,288,128]{2,1,0:T(8,128)S(1)}, u32[]{:S(2)}, u32[]{:S(2)}) collective-permute-start(f32[1,288,128]{2,1,0:T(8,128)S(1)} %shard_map.64), channel_id=1, source_target_pairs={{0,16},{8,104},{16,0},{24,120},{32,48},{40,72},{48,32},{56,88},{64... | collective-permute-start | bytes 442376 | tf_op jit(solution)/shard_map/ppermute | solution.py:492
  60.9 3.4 %collective-permute-done.8.refs_4_ = f32[1,288,128]{2,1,0:T(8,128)S(1)} collective-permute-done((f32[1,288,128]{2,1,0:T(8,128)S(1)}, f32[1,288,128]{2,1,0:T(8,128)S(1)}, u32[]{:S(2)}, u32[]{:S(2)}) %collective-permute-start.8) | collective-permute-done | bytes 147488 | tf_op jit(solution)/shard_map/ppermute | solution.py:492
  64.4 1.9 collective-permute-start.9
  66.3 3.4 %collective-permute-done.9.refs_1_ = f32[1,288,128]{2,1,0:T(8,128)S(1)} collective-permute-done((f32[1,288,128]{2,1,0:T(8,128)S(1)}, f32[1,288,128]{2,1,0:T(8,128)S(1)}, u32[]{:S(2)}, u32[]{:S(2)}) %collective-permute-start.9) | collective-permute-done | bytes 147488 | tf_op jit(solution)/shard_map/ppermute | solution.py:492
  71.5 2.2 %collective-permute-done.11.refs_3_ = f32[1,288,128]{2,1,0:T(8,128)S(1)} collective-permute-done((f32[1,288,128]{2,1,0:T(8,128)S(1)}, f32[1,288,128]{2,1,0:T(8,128)S(1)}, u32[]{:S(2)}, u32[]{:S(2)}) %collective-permute-start.11) | collective-permute-done | bytes 147488 | tf_op jit(solution)/shard_map/ppermute | solution.py:492
  74.0 2.8 %collective-permute-done.14.refs_6_ = f32[1,288,128]{2,1,0:T(8,128)S(1)} collective-permute-done((f32[1,288,128]{2,1,0:T(8,128)S(1)}, f32[1,288,128]{2,1,0:T(8,128)S(1)}, u32[]{:S(2)}, u32[]{:S(2)}) %collective-permute-start.14) | collective-permute-done | bytes 147488 | tf_op jit(solution)/shard_map/ppermute | solution.py:492
  76.8 1.9 collective-permute-done.15.refs_7_
  78.8 5.4 %collective-permute-start.16 = (f32[2304,128]{1,0:T(8,128)S(1)}, f32[2304,128]{1,0:T(8,128)S(1)}, u32[]{:S(2)}, u32[]{:S(2)}) collective-permute-start(f32[2304,128]{1,0:T(8,128)S(1)} %bitcast.7), channel_id=1, source_target_pairs={{0,8},{8,0},{1,9},{9,1},{2,10},{10,2},{3,11},{11,3},{4,12},{12,4},... | collective-permute-start | bytes 3538952 | tf_op jit(solution)/shard_map/ppermute | solution.py:472
  84.2 2.5 %shard_map.67 = (f32[8,128,128]{2,1,0:T(8,128)S(1)}, f32[256,256]{1,0:T(8,128)S(1)}) custom-call(s32[1]{0:T(128)} %bitcast.dev, bf16[4,4608,256]{2,1,0:T(8,128)(2,1)S(1)} %get-tuple-element.57.bhi, bf16[4,4608,256]{2,1,0:T(8,128)(2,1)S(1)} %get-tuple-element.58.blo, f32[2304,128]{1,0:T(8,128)S(1)} %bitcast.8), custom_call_target="tpu_custom_call" | custom-call | flops 450000000 | tf_op jit(solution)/shard_map/pallas_call | solution.py:60
  86.7 2.5 %shard_map.68 = f32[8,144,128]{2,1,0:T(8,128)S(1)} custom-call(s32[1]{0:T(128)} %bitcast.dev, bf16[4,4608,256]{2,1,0:T(8,128)(2,1)S(1)} %get-tuple-element.57.bhi, bf16[4,4608,256]{2,1,0:T(8,128)(2,1)S(1)} %get-tuple-element.58.blo, f32[2304,128]{1,0:T(8,128)S(1)} %collective-permute-done.16.v, f32[8,128,128]{2,1,0:T(8,128)S(1)} %get-tuple-element.66.rest_0_, ...), custom_call_target="tpu_custom_call" | custom-call | flops 450000000 | tf_op jit(solution)/shard_map/pallas_call | solution.py:60
  89.2 14.1 %all_to_all.22.p = f32[8,144,128]{2,1,0:T(8,128)S(1)} all-to-all(f32[8,144,128]{2,1,0:T(8,128)S(1)} %shard_map.68), channel_id=1, replica_groups=mesh['z'=4,'xl'=2,'c'=2,'xh'=2,'y'=4] {'xh','y'}, dimensions={0} | all-to-all | bytes 1179648 | tf_op jit(solution)/shard_map/all_to_all | solution.py:476
  103.4 13.6 %all_to_all.23.s.refs_0_ = f32[8,144,128]{2,1,0:T(8,128)S(1)} all-to-all(f32[8,144,128]{2,1,0:T(8,128)S(1)} %shard_map.69), channel_id=1, replica_groups=mesh['z'=4,'xl'=2,'c'=2,'xh'=2,'y'=4] {'xh','y'}, dimensions={0} | all-to-all | bytes 1179648 | tf_op jit(solution)/shard_map/all_to_all | solution.py:476
  117.8 2.6 %collective-permute-start.17 = (f32[2,288,128]{2,1,0:T(8,128)S(1)}, f32[2,288,128]{2,1,0:T(8,128)S(1)}, u32[]{:S(2)}, u32[]{:S(2)}) collective-permute-start(f32[2,288,128]{2,1,0:T(8,128)S(1)} %get-tuple-element.69), channel_id=1, source_target_pairs={{0,8},{8,0},{1,9},{9,1},{2,10},{10,2},{3,11},{11,3},{4,12},{12,4},... | collective-permute-start | bytes 884744 | tf_op jit(solution)/shard_map/ppermute | solution.py:472
  126.3 2.5 %collective-permute-done.20.refs_2_ = f32[2,288,128]{2,1,0:T(8,128)S(1)} collective-permute-done((f32[2,288,128]{2,1,0:T(8,128)S(1)}, f32[2,288,128]{2,1,0:T(8,128)S(1)}, u32[]{:S(2)}, u32[]{:S(2)}) %collective-permute-start.20) | collective-permute-done | bytes 294944 | tf_op jit(solution)/shard_map/ppermute | solution.py:492
  131.4 2.0 shard_map.82
  134.2 2.8 %collective-permute-done.21.r2 = f32[1,288,128]{2,1,0:T(8,128)S(1)} collective-permute-done((f32[1,288,128]{2,1,0:T(8,128)S(1)}, f32[1,288,128]{2,1,0:T(8,128)S(1)}, u32[]{:S(2)}, u32[]{:S(2)}) %collective-permute-start.21) | collective-permute-done | bytes 147488 | tf_op jit(solution)/shard_map/ppermute | solution.py:492
  137.0 1.4 collective-permute-start.25
  138.4 3.7 %shard_map.84.refs_5_ = f32[128,128]{1,0:T(8,128)S(1)} custom-call(f32[128,128]{1,0:T(8,128)S(1)} %get-tuple-element.79.refs_0_, f32[128,128]{1,0:T(8,128)S(1)} %get-tuple-element.80.refs_1_), custom_call_target="tpu_custom_call" | custom-call | flops 660000000 | tf_op jit(solution)/shard_map/pallas_call | solution.py:60
  143.0 1.4 collective-permute-start.26
  144.7 3.6 %collective-permute-done.26.refs_1_ = f32[1,288,128]{2,1,0:T(8,128)S(1)} collective-permute-done((f32[1,288,128]{2,1,0:T(8,128)S(1)}, f32[1,288,128]{2,1,0:T(8,128)S(1)}, u32[]{:S(2)}, u32[]{:S(2)}) %collective-permute-start.26) | collective-permute-done | bytes 147488 | tf_op jit(solution)/shard_map/ppermute | solution.py:492
  151.0 1.6 collective-permute-done.28.refs_3_
  153.8 2.0 collective-permute-done.31.refs_6_
  155.8 1.9 collective-permute-done.32.refs_7_
  157.7 6.0 %collective-permute-start.33 = (f32[2304,128]{1,0:T(8,128)S(1)}, f32[2304,128]{1,0:T(8,128)S(1)}, u32[]{:S(2)}, u32[]{:S(2)}) collective-permute-start(f32[2304,128]{1,0:T(8,128)S(1)} %bitcast.4), channel_id=1, source_target_pairs={{0,8},{8,0},{1,9},{9,1},{2,10},{10,2},{3,11},{11,3},{4,12},{12,4},... | collective-permute-start | bytes 3538952 | tf_op jit(solution)/shard_map/ppermute | solution.py:472
  163.8 2.5 %shard_map.87 = (f32[8,128,128]{2,1,0:T(8,128)S(1)}, f32[256,256]{1,0:T(8,128)S(1)}) custom-call(s32[1]{0:T(128)} %bitcast.dev, bf16[4,4608,256]{2,1,0:T(8,128)(2,1)S(1)} %get-tuple-element.57.bhi, bf16[4,4608,256]{2,1,0:T(8,128)(2,1)S(1)} %get-tuple-element.58.blo, f32[2304,128]{1,0:T(8,128)S(1)} %bitcast.5), custom_call_target="tpu_custom_call" | custom-call | flops 450000000 | tf_op jit(solution)/shard_map/pallas_call | solution.py:60
  166.3 2.5 %shard_map.88 = (f32[3,128,128]{2,1,0:T(8,128)S(1)}, f32[2,128,128]{2,1,0:T(8,128)S(1)}, f32[5,128,128]{2,1,0:T(8,128)S(1)}) custom-call(s32[1]{0:T(128)} %bitcast.dev, bf16[4,4608,256]{2,1,0:T(8,128)(2,1)S(1)} %get-tuple-element.57.bhi, bf16[4,4608,256]{2,1,0:T(8,128)(2,1)S(1)} %get-tuple-element.58.blo, f32[2304,128]{1,0:T(8,128)S(1)} %collective-permute-done.33.v.theirs, ...), custom_call_target="tpu_custom_call" | custom-call | flops 450000000 | tf_op jit(solution)/shard_map/pallas_call | solution.py:60
  169.7 1.8 collective-permute-start.35
  171.5 3.1 %collective-permute-done.34.ra = f32[3,128,128]{2,1,0:T(8,128)S(1)} collective-permute-done((f32[3,128,128]{2,1,0:T(8,128)S(1)}, f32[3,128,128]{2,1,0:T(8,128)S(1)}, u32[]{:S(2)}, u32[]{:S(2)}) %collective-permute-start.34) | collective-permute-done | bytes 196640 | tf_op jit(solution)/shard_map/ppermute | solution.py:492
  174.7 1.3 collective-permute-done.35.rb
  176.0 2.5 %collective-permute-done.36.r2 = f32[2,128,128]{2,1,0:T(8,128)S(1)} collective-permute-done((f32[2,128,128]{2,1,0:T(8,128)S(1)}, f32[2,128,128]{2,1,0:T(8,128)S(1)}, u32[]{:S(2)}, u32[]{:S(2)}) %collective-permute-start.36) | collective-permute-done | bytes 131104 | tf_op jit(solution)/shard_map/ppermute | solution.py:492
  179.7 2.8 %collective-permute-done.37.r2_own = f32[1,128,128]{2,1,0:T(8,128)S(1)} collective-permute-done((f32[1,128,128]{2,1,0:T(8,128)S(1)}, f32[1,128,128]{2,1,0:T(8,128)S(1)}, u32[]{:S(2)}, u32[]{:S(2)}) %collective-permute-start.37) | collective-permute-done | bytes 65568 | tf_op jit(solution)/shard_map/ppermute | solution.py:492
  182.5 1.4 collective-permute-done.38.r3
  184.2 4.0 %collective-permute-start.39 = (f32[2,128,128]{2,1,0:T(8,128)S(1)}, f32[2,128,128]{2,1,0:T(8,128)S(1)}, u32[]{:S(2)}, u32[]{:S(2)}) collective-permute-start(f32[2,128,128]{2,1,0:T(8,128)S(1)} %shard_map.91.own), channel_id=1, source_target_pairs={{0,8},{8,0},{1,9},{9,1},{2,10},{10,2},{3,11},{11,3},{4,12},{12,4},... | collective-permute-start | bytes 393224 | tf_op jit(solution)/shard_map/ppermute | solution.py:472
  189.2 1.4 collective-permute-start.42
  191.2 1.3 collective-permute-start.40
  192.5 2.0 shard_map.93
  196.4 2.2 %collective-permute-start.43 = (f32[128,128]{1,0:T(8,128)S(1)}, f32[128,128]{1,0:T(8,128)S(1)}, u32[]{:S(2)}, u32[]{:S(2)}) collective-permute-start(f32[128,128]{1,0:T(8,128)S(1)} %add_add_fusion.1), channel_id=1, source_target_pairs={{0,1},{1,0},{2,3},{3,2},{4,5},{5,4},{6,7},{7,6},{8,9},{9,8},{10,11... | collective-permute-start | bytes 196616 | tf_op jit(solution)/shard_map/ppermute | solution.py:472
  198.6 1.9 shard_map.94
  201.0 2.4 %collective-permute-start.48 = (f32[128,128]{1,0:T(8,128)S(1)}, f32[128,128]{1,0:T(8,128)S(1)}, u32[]{:S(2)}, u32[]{:S(2)}) collective-permute-start(f32[128,128]{1,0:T(8,128)S(1)} %add_add_fusion.a), channel_id=1, source_target_pairs={{0,20},{4,16},{16,4},{20,0},{1,21},{5,17},{17,5},{21,1},{2,22},{6,... | collective-permute-start | bytes 196616 | tf_op jit(solution)/shard_map/ppermute | solution.py:472
  203.4 1.5 collective-permute-start.46
  205.0 4.2 %finish.1 = (f32[4500,128]{1,0:T(8,128)}, f32[128,128]{1,0:T(8,128)S(1)}) custom-call(s32[1]{0:T(128)} %bitcast.dev, f32[2304,128]{1,0:T(8,128)S(1)} %bitcast.6, f32[2304,128]{1,0:T(8,128)S(1)} %collective-permute-done.33.v.theirs, f32[128,128]{1,0:T(8,128)S(1)} %get-tuple-element.101.g, f32[128,128]{1,0:T(8,128)S(1)} %get-tuple-element.102.w), custom_call_target="tpu_custom_call" | custom-call | flops 630000000 | tf_op jit(solution)/shard_map/finish/pallas_call | solution.py:443
  (106 shorter events, 35.6 us)
Async XLA Ops:
  39.2 4.7 %collective-permute-start = (f32[2,288,128]{2,1,0:T(8,128)S(1)}, f32[2,288,128]{2,1,0:T(8,128)S(1)}, u32[]{:S(2)}, u32[]{:S(2)}) collective-permute-start(f32[2,288,128]{2,1,0:T(8,128)S(1)} %get-tuple-element.62), channel_id=1, source_target_pairs={{0,8},{8,0},{1,9},{9,1},{2,10},{10,2},{3,11},{11,3},{4,12},{12,4},... | collective-permute-start | bytes 884744 | tf_op jit(solution)/shard_map/ppermute | solution.py:472
  45.2 5.9 %collective-permute-start.3 = (f32[2,288,128]{2,1,0:T(8,128)S(1)}, f32[2,288,128]{2,1,0:T(8,128)S(1)}, u32[]{:S(2)}, u32[]{:S(2)}) collective-permute-start(f32[2,288,128]{2,1,0:T(8,128)S(1)} %shard_map.54), channel_id=1, source_target_pairs={{0,32},{8,24},{16,48},{24,8},{32,0},{40,56},{48,16},{56,40},{64,96... | collective-permute-start | bytes 884744 | tf_op jit(solution)/shard_map/ppermute | solution.py:492
  47.2 3.8 %collective-permute-start.2 = (f32[2,288,128]{2,1,0:T(8,128)S(1)}, f32[2,288,128]{2,1,0:T(8,128)S(1)}, u32[]{:S(2)}, u32[]{:S(2)}) collective-permute-start(f32[2,288,128]{2,1,0:T(8,128)S(1)} %shard_map.59), channel_id=1, source_target_pairs={{0,8},{8,0},{1,9},{9,1},{2,10},{10,2},{3,11},{11,3},{4,12},{12,4},... | collective-permute-start | bytes 884744 | tf_op jit(solution)/shard_map/ppermute | solution.py:472
  49.0 6.6 %collective-permute-start.5 = (f32[2,288,128]{2,1,0:T(8,128)S(1)}, f32[2,288,128]{2,1,0:T(8,128)S(1)}, u32[]{:S(2)}, u32[]{:S(2)}) collective-permute-start(f32[2,288,128]{2,1,0:T(8,128)S(1)} %shard_map.57), channel_id=1, source_target_pairs={{0,32},{8,24},{16,48},{24,8},{32,0},{40,56},{48,16},{56,40},{64,96... | collective-permute-start | bytes 884744 | tf_op jit(solution)/shard_map/ppermute | solution.py:492
  51.9 5.4 %collective-permute-start.4 = (f32[2,288,128]{2,1,0:T(8,128)S(1)}, f32[2,288,128]{2,1,0:T(8,128)S(1)}, u32[]{:S(2)}, u32[]{:S(2)}) collective-permute-start(f32[2,288,128]{2,1,0:T(8,128)S(1)} %shard_map.62), channel_id=1, source_target_pairs={{0,8},{8,0},{1,9},{9,1},{2,10},{10,2},{3,11},{11,3},{4,12},{12,4},... | collective-permute-start | bytes 884744 | tf_op jit(solution)/shard_map/ppermute | solution.py:472
  53.0 4.3 %collective-permute-start.7 = (f32[1,288,128]{2,1,0:T(8,128)S(1)}, f32[1,288,128]{2,1,0:T(8,128)S(1)}, u32[]{:S(2)}, u32[]{:S(2)}) collective-permute-start(f32[1,288,128]{2,1,0:T(8,128)S(1)} %shard_map.63), channel_id=1, source_target_pairs={{0,96},{8,40},{16,112},{24,56},{32,64},{40,8},{48,80},{56,24},{64,... | collective-permute-start | bytes 442376 | tf_op jit(solution)/shard_map/ppermute | solution.py:492
  54.7 6.2 %collective-permute-start.6 = (f32[1,288,128]{2,1,0:T(8,128)S(1)}, f32[1,288,128]{2,1,0:T(8,128)S(1)}, u32[]{:S(2)}, u32[]{:S(2)}) collective-permute-start(f32[1,288,128]{2,1,0:T(8,128)S(1)} %shard_map.60), channel_id=1, source_target_pairs={{0,96},{8,40},{16,112},{24,56},{32,64},{40,8},{48,80},{56,24},{64,... | collective-permute-start | bytes 442376 | tf_op jit(solution)/shard_map/ppermute | solution.py:492
  57.3 7.1 %collective-permute-start.8 = (f32[1,288,128]{2,1,0:T(8,128)S(1)}, f32[1,288,128]{2,1,0:T(8,128)S(1)}, u32[]{:S(2)}, u32[]{:S(2)}) collective-permute-start(f32[1,288,128]{2,1,0:T(8,128)S(1)} %shard_map.64), channel_id=1, source_target_pairs={{0,16},{8,104},{16,0},{24,120},{32,48},{40,72},{48,32},{56,88},{64... | collective-permute-start | bytes 442376 | tf_op jit(solution)/shard_map/ppermute | solution.py:492
  64.4 5.3 %collective-permute-start.9 = (f32[1,288,128]{2,1,0:T(8,128)S(1)}, f32[1,288,128]{2,1,0:T(8,128)S(1)}, u32[]{:S(2)}, u32[]{:S(2)}) collective-permute-start(f32[1,288,128]{2,1,0:T(8,128)S(1)} %shard_map.65.refs_0_), channel_id=1, source_target_pairs={{0,16},{8,104},{16,0},{24,120},{32,48},{40,72},{48,32},{56,88},{64... | collective-permute-start | bytes 442376 | tf_op jit(solution)/shard_map/ppermute | solution.py:492
  66.3 4.9 %collective-permute-start.10 = (f32[1,288,128]{2,1,0:T(8,128)S(1)}, f32[1,288,128]{2,1,0:T(8,128)S(1)}, u32[]{:S(2)}, u32[]{:S(2)}) collective-permute-start(f32[1,288,128]{2,1,0:T(8,128)S(1)} %shard_map.65.refs_0_), channel_id=1, source_target_pairs={{0,96},{8,40},{16,112},{24,56},{32,64},{40,8},{48,80},{56,24},{64,... | collective-permute-start | bytes 442376 | tf_op jit(solution)/shard_map/ppermute | solution.py:492
  69.7 4.0 %collective-permute-start.11 = (f32[1,288,128]{2,1,0:T(8,128)S(1)}, f32[1,288,128]{2,1,0:T(8,128)S(1)}, u32[]{:S(2)}, u32[]{:S(2)}) collective-permute-start(f32[1,288,128]{2,1,0:T(8,128)S(1)} %collective-permute-done.9.refs_1_), channel_id=1, source_target_pairs={{0,96},{8,40},{16,112},{24,56},{32,64},{40,8},{48,80},{56,24},{64,... | collective-permute-start | bytes 442376 | tf_op jit(solution)/shard_map/ppermute | solution.py:492
  69.7 4.3 %collective-permute-start.12 = (f32[1,288,128]{2,1,0:T(8,128)S(1)}, f32[1,288,128]{2,1,0:T(8,128)S(1)}, u32[]{:S(2)}, u32[]{:S(2)}) collective-permute-start(f32[1,288,128]{2,1,0:T(8,128)S(1)} %shard_map.65.refs_0_), channel_id=1, source_target_pairs={{0,32},{8,24},{16,48},{24,8},{32,0},{40,56},{48,16},{56,40},{64,96... | collective-permute-start | bytes 442376 | tf_op jit(solution)/shard_map/ppermute | solution.py:492
  70.0 6.8 %collective-permute-start.13 = (f32[1,288,128]{2,1,0:T(8,128)S(1)}, f32[1,288,128]{2,1,0:T(8,128)S(1)}, u32[]{:S(2)}, u32[]{:S(2)}) collective-permute-start(f32[1,288,128]{2,1,0:T(8,128)S(1)} %collective-permute-done.9.refs_1_), channel_id=1, source_target_pairs={{0,32},{8,24},{16,48},{24,8},{32,0},{40,56},{48,16},{56,40},{64,96... | collective-permute-start | bytes 442376 | tf_op jit(solution)/shard_map/ppermute | solution.py:492
  71.2 5.7 %collective-permute-start.14 = (f32[1,288,128]{2,1,0:T(8,128)S(1)}, f32[1,288,128]{2,1,0:T(8,128)S(1)}, u32[]{:S(2)}, u32[]{:S(2)}) collective-permute-start(f32[1,288,128]{2,1,0:T(8,128)S(1)} %collective-permute-done.10.refs_2_), channel_id=1, source_target_pairs={{0,32},{8,24},{16,48},{24,8},{32,0},{40,56},{48,16},{56,40},{64,96... | collective-permute-start | bytes 442376 | tf_op jit(solution)/shard_map/ppermute | solution.py:492
  73.7 5.0 %collective-permute-start.15 = (f32[1,288,128]{2,1,0:T(8,128)S(1)}, f32[1,288,128]{2,1,0:T(8,128)S(1)}, u32[]{:S(2)}, u32[]{:S(2)}) collective-permute-start(f32[1,288,128]{2,1,0:T(8,128)S(1)} %collective-permute-done.11.refs_3_), channel_id=1, source_target_pairs={{0,32},{8,24},{16,48},{24,8},{32,0},{40,56},{48,16},{56,40},{64,96... | collective-permute-start | bytes 442376 | tf_op jit(solution)/shard_map/ppermute | solution.py:492
  78.8 7.9 %collective-permute-start.16 = (f32[2304,128]{1,0:T(8,128)S(1)}, f32[2304,128]{1,0:T(8,128)S(1)}, u32[]{:S(2)}, u32[]{:S(2)}) collective-permute-start(f32[2304,128]{1,0:T(8,128)S(1)} %bitcast.7), channel_id=1, source_target_pairs={{0,8},{8,0},{1,9},{9,1},{2,10},{10,2},{3,11},{11,3},{4,12},{12,4},... | collective-permute-start | bytes 3538952 | tf_op jit(solution)/shard_map/ppermute | solution.py:472
  117.8 3.8 %collective-permute-start.17 = (f32[2,288,128]{2,1,0:T(8,128)S(1)}, f32[2,288,128]{2,1,0:T(8,128)S(1)}, u32[]{:S(2)}, u32[]{:S(2)}) collective-permute-start(f32[2,288,128]{2,1,0:T(8,128)S(1)} %get-tuple-element.69), channel_id=1, source_target_pairs={{0,8},{8,0},{1,9},{9,1},{2,10},{10,2},{3,11},{11,3},{4,12},{12,4},... | collective-permute-start | bytes 884744 | tf_op jit(solution)/shard_map/ppermute | solution.py:472
  122.5 1.7 collective-permute-start.18
  123.0 5.9 %collective-permute-start.20 = (f32[2,288,128]{2,1,0:T(8,128)S(1)}, f32[2,288,128]{2,1,0:T(8,128)S(1)}, u32[]{:S(2)}, u32[]{:S(2)}) collective-permute-start(f32[2,288,128]{2,1,0:T(8,128)S(1)} %shard_map.72), channel_id=1, source_target_pairs={{0,32},{8,24},{16,48},{24,8},{32,0},{40,56},{48,16},{56,40},{64,96... | collective-permute-start | bytes 884744 | tf_op jit(solution)/shard_map/ppermute | solution.py:492
  125.0 3.8 %collective-permute-start.19 = (f32[2,288,128]{2,1,0:T(8,128)S(1)}, f32[2,288,128]{2,1,0:T(8,128)S(1)}, u32[]{:S(2)}, u32[]{:S(2)}) collective-permute-start(f32[2,288,128]{2,1,0:T(8,128)S(1)} %shard_map.77), channel_id=1, source_target_pairs={{0,8},{8,0},{1,9},{9,1},{2,10},{10,2},{3,11},{11,3},{4,12},{12,4},... | collective-permute-start | bytes 884744 | tf_op jit(solution)/shard_map/ppermute | solution.py:472
  129.7 7.3 %collective-permute-start.22 = (f32[2,288,128]{2,1,0:T(8,128)S(1)}, f32[2,288,128]{2,1,0:T(8,128)S(1)}, u32[]{:S(2)}, u32[]{:S(2)}) collective-permute-start(f32[2,288,128]{2,1,0:T(8,128)S(1)} %shard_map.81), channel_id=1, source_target_pairs={{0,8},{8,0},{1,9},{9,1},{2,10},{10,2},{3,11},{11,3},{4,12},{12,4},... | collective-permute-start | bytes 884744 | tf_op jit(solution)/shard_map/ppermute | solution.py:472
  130.7 6.2 %collective-permute-start.23 = (f32[2,288,128]{2,1,0:T(8,128)S(1)}, f32[2,288,128]{2,1,0:T(8,128)S(1)}, u32[]{:S(2)}, u32[]{:S(2)}) collective-permute-start(f32[2,288,128]{2,1,0:T(8,128)S(1)} %shard_map.75), channel_id=1, source_target_pairs={{0,32},{8,24},{16,48},{24,8},{32,0},{40,56},{48,16},{56,40},{64,96... | collective-permute-start | bytes 884744 | tf_op jit(solution)/shard_map/ppermute | solution.py:492
  131.1 5.8 %collective-permute-start.21 = (f32[1,288,128]{2,1,0:T(8,128)S(1)}, f32[1,288,128]{2,1,0:T(8,128)S(1)}, u32[]{:S(2)}, u32[]{:S(2)}) collective-permute-start(f32[1,288,128]{2,1,0:T(8,128)S(1)} %shard_map.78), channel_id=1, source_target_pairs={{0,96},{8,40},{16,112},{24,56},{32,64},{40,8},{48,80},{56,24},{64,... | collective-permute-start | bytes 442376 | tf_op jit(solution)/shard_map/ppermute | solution.py:492
  137.0 5.3 %collective-permute-start.25 = (f32[1,288,128]{2,1,0:T(8,128)S(1)}, f32[1,288,128]{2,1,0:T(8,128)S(1)}, u32[]{:S(2)}, u32[]{:S(2)}) collective-permute-start(f32[1,288,128]{2,1,0:T(8,128)S(1)} %shard_map.83), channel_id=1, source_target_pairs={{0,16},{8,104},{16,0},{24,120},{32,48},{40,72},{48,32},{56,88},{64... | collective-permute-start | bytes 442376 | tf_op jit(solution)/shard_map/ppermute | solution.py:492
  138.4 4.3 %collective-permute-start.24 = (f32[1,288,128]{2,1,0:T(8,128)S(1)}, f32[1,288,128]{2,1,0:T(8,128)S(1)}, u32[]{:S(2)}, u32[]{:S(2)}) collective-permute-start(f32[1,288,128]{2,1,0:T(8,128)S(1)} %shard_map.79), channel_id=1, source_target_pairs={{0,96},{8,40},{16,112},{24,56},{32,64},{40,8},{48,80},{56,24},{64,... | collective-permute-start | bytes 442376 | tf_op jit(solution)/shard_map/ppermute | solution.py:492
  143.0 5.3 %collective-permute-start.26 = (f32[1,288,128]{2,1,0:T(8,128)S(1)}, f32[1,288,128]{2,1,0:T(8,128)S(1)}, u32[]{:S(2)}, u32[]{:S(2)}) collective-permute-start(f32[1,288,128]{2,1,0:T(8,128)S(1)} %shard_map.85.refs_0_), channel_id=1, source_target_pairs={{0,16},{8,104},{16,0},{24,120},{32,48},{40,72},{48,32},{56,88},{64... | collective-permute-start | bytes 442376 | tf_op jit(solution)/shard_map/ppermute | solution.py:492
  144.4 5.3 %collective-permute-start.27 = (f32[1,288,128]{2,1,0:T(8,128)S(1)}, f32[1,288,128]{2,1,0:T(8,128)S(1)}, u32[]{:S(2)}, u32[]{:S(2)}) collective-permute-start(f32[1,288,128]{2,1,0:T(8,128)S(1)} %shard_map.85.refs_0_), channel_id=1, source_target_pairs={{0,96},{8,40},{16,112},{24,56},{32,64},{40,8},{48,80},{56,24},{64,... | collective-permute-start | bytes 442376 | tf_op jit(solution)/shard_map/ppermute | solution.py:492
  148.3 4.3 %collective-permute-start.28 = (f32[1,288,128]{2,1,0:T(8,128)S(1)}, f32[1,288,128]{2,1,0:T(8,128)S(1)}, u32[]{:S(2)}, u32[]{:S(2)}) collective-permute-start(f32[1,288,128]{2,1,0:T(8,128)S(1)} %collective-permute-done.26.refs_1_), channel_id=1, source_target_pairs={{0,96},{8,40},{16,112},{24,56},{32,64},{40,8},{48,80},{56,24},{64,... | collective-permute-start | bytes 442376 | tf_op jit(solution)/shard_map/ppermute | solution.py:492
  148.3 5.6 %collective-permute-start.29 = (f32[1,288,128]{2,1,0:T(8,128)S(1)}, f32[1,288,128]{2,1,0:T(8,128)S(1)}, u32[]{:S(2)}, u32[]{:S(2)}) collective-permute-start(f32[1,288,128]{2,1,0:T(8,128)S(1)} %shard_map.85.refs_0_), channel_id=1, source_target_pairs={{0,32},{8,24},{16,48},{24,8},{32,0},{40,56},{48,16},{56,40},{64,96... | collective-permute-start | bytes 442376 | tf_op jit(solution)/shard_map/ppermute | solution.py:492
  149.5 6.3 %collective-permute-start.30 = (f32[1,288,128]{2,1,0:T(8,128)S(1)}, f32[1,288,128]{2,1,0:T(8,128)S(1)}, u32[]{:S(2)}, u32[]{:S(2)}) collective-permute-start(f32[1,288,128]{2,1,0:T(8,128)S(1)} %collective-permute-done.26.refs_1_), channel_id=1, source_target_pairs={{0,32},{8,24},{16,48},{24,8},{32,0},{40,56},{48,16},{56,40},{64,96... | collective-permute-start | bytes 442376 | tf_op jit(solution)/shard_map/ppermute | solution.py:492
  149.7 6.0 %collective-permute-start.31 = (f32[1,288,128]{2,1,0:T(8,128)S(1)}, f32[1,288,128]{2,1,0:T(8,128)S(1)}, u32[]{:S(2)}, u32[]{:S(2)}) collective-permute-start(f32[1,288,128]{2,1,0:T(8,128)S(1)} %collective-permute-done.27.refs_2_), channel_id=1, source_target_pairs={{0,32},{8,24},{16,48},{24,8},{32,0},{40,56},{48,16},{56,40},{64,96... | collective-permute-start | bytes 442376 | tf_op jit(solution)/shard_map/ppermute | solution.py:492
  152.6 5.1 %collective-permute-start.32 = (f32[1,288,128]{2,1,0:T(8,128)S(1)}, f32[1,288,128]{2,1,0:T(8,128)S(1)}, u32[]{:S(2)}, u32[]{:S(2)}) collective-permute-start(f32[1,288,128]{2,1,0:T(8,128)S(1)} %collective-permute-done.28.refs_3_), channel_id=1, source_target_pairs={{0,32},{8,24},{16,48},{24,8},{32,0},{40,56},{48,16},{56,40},{64,96... | collective-permute-start | bytes 442376 | tf_op jit(solution)/shard_map/ppermute | solution.py:492
  157.7 8.5 %collective-permute-start.33 = (f32[2304,128]{1,0:T(8,128)S(1)}, f32[2304,128]{1,0:T(8,128)S(1)}, u32[]{:S(2)}, u32[]{:S(2)}) collective-permute-start(f32[2304,128]{1,0:T(8,128)S(1)} %bitcast.4), channel_id=1, source_target_pairs={{0,8},{8,0},{1,9},{9,1},{2,10},{10,2},{3,11},{11,3},{4,12},{12,4},... | collective-permute-start | bytes 3538952 | tf_op jit(solution)/shard_map/ppermute | solution.py:472
  168.8 5.8 %collective-permute-start.34 = (f32[3,128,128]{2,1,0:T(8,128)S(1)}, f32[3,128,128]{2,1,0:T(8,128)S(1)}, u32[]{:S(2)}, u32[]{:S(2)}) collective-permute-start(f32[3,128,128]{2,1,0:T(8,128)S(1)} %get-tuple-element.86), channel_id=1, source_target_pairs={{0,1},{1,0},{2,3},{3,2},{4,5},{5,4},{6,7},{7,6},{8,11},{9,10},{10,... | collective-permute-start | bytes 589832 | tf_op jit(solution)/shard_map/ppermute | solution.py:492
  169.7 6.2 %collective-permute-start.35 = (f32[2,128,128]{2,1,0:T(8,128)S(1)}, f32[2,128,128]{2,1,0:T(8,128)S(1)}, u32[]{:S(2)}, u32[]{:S(2)}) collective-permute-start(f32[2,128,128]{2,1,0:T(8,128)S(1)} %get-tuple-element.87), channel_id=1, source_target_pairs={{0,1},{1,0},{2,3},{3,2},{4,5},{5,4},{6,7},{7,6},{8,11},{9,10},{10,... | collective-permute-start | bytes 393224 | tf_op jit(solution)/shard_map/ppermute | solution.py:492
  174.6 3.9 %collective-permute-start.36 = (f32[2,128,128]{2,1,0:T(8,128)S(1)}, f32[2,128,128]{2,1,0:T(8,128)S(1)}, u32[]{:S(2)}, u32[]{:S(2)}) collective-permute-start(f32[2,128,128]{2,1,0:T(8,128)S(1)} %get-tuple-element.88), channel_id=1, source_target_pairs={{0,3},{1,2},{2,1},{3,0},{4,7},{5,6},{6,5},{7,4},{8,9},{9,8},{10,11... | collective-permute-start | bytes 393224 | tf_op jit(solution)/shard_map/ppermute | solution.py:492
  178.5 5.4 %collective-permute-start.38 = (f32[2,128,128]{2,1,0:T(8,128)S(1)}, f32[2,128,128]{2,1,0:T(8,128)S(1)}, u32[]{:S(2)}, u32[]{:S(2)}) collective-permute-start(f32[2,128,128]{2,1,0:T(8,128)S(1)} %shard_map.90), channel_id=1, source_target_pairs={{0,4},{1,5},{2,6},{3,7},{4,0},{5,1},{6,2},{7,3},{8,12},{9,13},{10,... | collective-permute-start | bytes 393224 | tf_op jit(solution)/shard_map/ppermute | solution.py:492
  179.4 3.1 %collective-permute-start.37 = (f32[1,128,128]{2,1,0:T(8,128)S(1)}, f32[1,128,128]{2,1,0:T(8,128)S(1)}, u32[]{:S(2)}, u32[]{:S(2)}) collective-permute-start(f32[1,128,128]{2,1,0:T(8,128)S(1)} %get-tuple-element.89), channel_id=1, source_target_pairs={{0,3},{1,2},{2,1},{3,0},{4,7},{5,6},{6,5},{7,4},{8,9},{9,8},{10,11... | collective-permute-start | bytes 196616 | tf_op jit(solution)/shard_map/ppermute | solution.py:492
  184.2 4.9 %collective-permute-start.39 = (f32[2,128,128]{2,1,0:T(8,128)S(1)}, f32[2,128,128]{2,1,0:T(8,128)S(1)}, u32[]{:S(2)}, u32[]{:S(2)}) collective-permute-start(f32[2,128,128]{2,1,0:T(8,128)S(1)} %shard_map.91.own), channel_id=1, source_target_pairs={{0,8},{8,0},{1,9},{9,1},{2,10},{10,2},{3,11},{11,3},{4,12},{12,4},... | collective-permute-start | bytes 393224 | tf_op jit(solution)/shard_map/ppermute | solution.py:472
  189.2 5.3 %collective-permute-start.42 = (f32[128,128]{1,0:T(8,128)S(1)}, f32[128,128]{1,0:T(8,128)S(1)}, u32[]{:S(2)}, u32[]{:S(2)}) collective-permute-start(f32[128,128]{1,0:T(8,128)S(1)} %get-tuple-element.90), channel_id=1, source_target_pairs={{0,96},{32,64},{64,32},{96,0},{1,97},{33,65},{65,33},{97,1},{2,98}... | collective-permute-start | bytes 196616 | tf_op jit(solution)/shard_map/ppermute | solution.py:472
  190.6 4.6 %collective-permute-start.41 = (f32[128,128]{1,0:T(8,128)S(1)}, f32[128,128]{1,0:T(8,128)S(1)}, u32[]{:S(2)}, u32[]{:S(2)}) collective-permute-start(f32[128,128]{1,0:T(8,128)S(1)} %get-tuple-element.90), channel_id=1, source_target_pairs={{0,64},{32,96},{64,0},{96,32},{1,65},{33,97},{65,1},{97,33},{2,66}... | collective-permute-start | bytes 196616 | tf_op jit(solution)/shard_map/ppermute | solution.py:472
  191.2 4.0 %collective-permute-start.40 = (f32[128,128]{1,0:T(8,128)S(1)}, f32[128,128]{1,0:T(8,128)S(1)}, u32[]{:S(2)}, u32[]{:S(2)}) collective-permute-start(f32[128,128]{1,0:T(8,128)S(1)} %get-tuple-element.90), channel_id=1, source_target_pairs={{0,32},{32,0},{64,96},{96,64},{1,33},{33,1},{65,97},{97,65},{2,34}... | collective-permute-start | bytes 196616 | tf_op jit(solution)/shard_map/ppermute | solution.py:472
  195.2 5.3 %collective-permute-start.45 = (f32[128,128]{1,0:T(8,128)S(1)}, f32[128,128]{1,0:T(8,128)S(1)}, u32[]{:S(2)}, u32[]{:S(2)}) collective-permute-start(f32[128,128]{1,0:T(8,128)S(1)} %add_add_fusion.1), channel_id=1, source_target_pairs={{0,3},{1,2},{2,1},{3,0},{4,7},{5,6},{6,5},{7,4},{8,11},{9,10},{10,... | collective-permute-start | bytes 196616 | tf_op jit(solution)/shard_map/ppermute | solution.py:472
  196.4 4.6 %collective-permute-start.44 = (f32[128,128]{1,0:T(8,128)S(1)}, f32[128,128]{1,0:T(8,128)S(1)}, u32[]{:S(2)}, u32[]{:S(2)}) collective-permute-start(f32[128,128]{1,0:T(8,128)S(1)} %add_add_fusion.1), channel_id=1, source_target_pairs={{0,2},{1,3},{2,0},{3,1},{4,6},{5,7},{6,4},{7,5},{8,10},{9,11},{10,... | collective-permute-start | bytes 196616 | tf_op jit(solution)/shard_map/ppermute | solution.py:472
  196.4 4.6 %collective-permute-start.43 = (f32[128,128]{1,0:T(8,128)S(1)}, f32[128,128]{1,0:T(8,128)S(1)}, u32[]{:S(2)}, u32[]{:S(2)}) collective-permute-start(f32[128,128]{1,0:T(8,128)S(1)} %add_add_fusion.1), channel_id=1, source_target_pairs={{0,1},{1,0},{2,3},{3,2},{4,5},{5,4},{6,7},{7,6},{8,9},{9,8},{10,11... | collective-permute-start | bytes 196616 | tf_op jit(solution)/shard_map/ppermute | solution.py:472
  201.0 8.2 %collective-permute-start.48 = (f32[128,128]{1,0:T(8,128)S(1)}, f32[128,128]{1,0:T(8,128)S(1)}, u32[]{:S(2)}, u32[]{:S(2)}) collective-permute-start(f32[128,128]{1,0:T(8,128)S(1)} %add_add_fusion.a), channel_id=1, source_target_pairs={{0,20},{4,16},{16,4},{20,0},{1,21},{5,17},{17,5},{21,1},{2,22},{6,... | collective-permute-start | bytes 196616 | tf_op jit(solution)/shard_map/ppermute | solution.py:472
  203.4 5.8 %collective-permute-start.47 = (f32[128,128]{1,0:T(8,128)S(1)}, f32[128,128]{1,0:T(8,128)S(1)}, u32[]{:S(2)}, u32[]{:S(2)}) collective-permute-start(f32[128,128]{1,0:T(8,128)S(1)} %add_add_fusion.a), channel_id=1, source_target_pairs={{0,16},{4,20},{16,0},{20,4},{1,17},{5,21},{17,1},{21,5},{2,18},{6,... | collective-permute-start | bytes 196616 | tf_op jit(solution)/shard_map/ppermute | solution.py:472
  203.4 5.8 %collective-permute-start.46 = (f32[128,128]{1,0:T(8,128)S(1)}, f32[128,128]{1,0:T(8,128)S(1)}, u32[]{:S(2)}, u32[]{:S(2)}) collective-permute-start(f32[128,128]{1,0:T(8,128)S(1)} %add_add_fusion.a), channel_id=1, source_target_pairs={{0,4},{4,0},{16,20},{20,16},{1,5},{5,1},{17,21},{21,17},{2,6},{6,2... | collective-permute-start | bytes 196616 | tf_op jit(solution)/shard_map/ppermute | solution.py:472
  (2 other events, 27.3 us)
